TPU v7x, 32 devices: a whole 2x2x4 slice. The times are simulated.
32 devices in a mesh: ta: 16 (over z, y, core), ka: 2 (over x).
Axes of the slice: x: 2, y: 2, z: 4, core: 2. Of those that a mesh axis runs over, the one named last changes fastest.
Arguments:
- green_row: float32 [2, 4, 4, 32, 1024], P(None, None, None, 'ta', 'ka'), may hold values from -6 to 6
- screen_lesser: float32 [2, 4, 4, 32, 1024], P(None, None, None, 'ta', 'ka'), may hold values from -6 to 6
- screen_retarded: float32 [2, 4, 4, 32, 1024], P(None, None, None, 'ta', 'ka'), may hold values from -6 to 6
- onsite: float32 [2, 4, 4], replicated, may hold values from -3 to 3
- lesser_slab: bfloat16 [2, 4, 4, 32, 32, 1024], P(None, None, None, 'ta', None, 'ka'), may hold values from -0.5 to 0.5
- advanced_slab: bfloat16 [2, 4, 4, 32, 32, 1024], P(None, None, None, 'ta', None, 'ka'), may hold values from -0.5 to 0.5
- slab_start: int32 [1], replicated, may hold values from 0 to 4095
- block_table: int32 [16], replicated, may hold values from 0 to 15, each once
Outputs:
- next_row: float32 [2, 4, 4, 32, 1024], P(None, None, None, 'ta', 'ka')
- derivative: float32 [2, 4, 4, 32, 1024], P(None, None, None, 'ta', 'ka')
Inputs may be any that keep to these rules, and one draw needn't show every extreme that they name: block_table is a permutation: each time block 0 to 15 appears once.
All inputs are finite; a program needn't handle non-finite values.
Results may differ from a plain program's by a relative error of at most 0.0019.
Values sent between devices are 32-bit elements; how exact they have to be, the bound alone decides.
No kernel may reach another device: no remote copies, remote signals or barrier semaphores. Data moves between devices by JAX's collectives and lax.ppermute only.
A program may use at most 128 MiB of HBM per device.

v0:
```python
import functools
import math

import jax
import jax.numpy as jnp
import numpy as np
from jax import lax
from jax.experimental import pallas as pl
from jax.experimental.pallas import tpu as pltpu
from jax.sharding import PartitionSpec as P

KS = 32
LANES = 128
SUBLANES = 8


time_step = 0.1
drive_amp = 1.0
drive_freq = 0.37
highest = lax.Precision.HIGHEST


def phase_table(row_ids, col_ids, sign_value):
    products = row_ids[:, None] * col_ids[None, :] % KS
    angle = products.astype(jnp.float32) * (2.0 * math.pi / KS)
    factor = 1.0 / math.sqrt(KS)
    return (jnp.cos(angle) * factor, sign_value * jnp.sin(angle) * factor)


def along_last(values_in, cosine, sine_part):
    real_part = jnp.einsum("...m,mn->...n", values_in[0], cosine, precision=highest) - jnp.einsum(
        "...m,mn->...n", values_in[1], sine_part, precision=highest
    )
    imag_part = jnp.einsum(
        "...m,mn->...n", values_in[0], sine_part, precision=highest
    ) + jnp.einsum("...m,mn->...n", values_in[1], cosine, precision=highest)
    return jnp.stack([real_part, imag_part])


def along_second(values_in, cosine, sine_part):
    real_part = jnp.einsum("...mj,mn->...nj", values_in[0], cosine, precision=highest) - jnp.einsum(
        "...mj,mn->...nj", values_in[1], sine_part, precision=highest
    )
    imag_part = jnp.einsum(
        "...mj,mn->...nj", values_in[0], sine_part, precision=highest
    ) + jnp.einsum("...mj,mn->...nj", values_in[1], cosine, precision=highest)
    return jnp.stack([real_part, imag_part])


def transform(values_in, sign_value, ka_index):
    leading = values_in.shape[:-1]
    x_local = values_in.shape[-1] // KS
    numbers = jnp.arange(KS, dtype=jnp.int32)
    owned = ka_index * x_local + jnp.arange(x_local, dtype=jnp.int32)
    cosine, sine_part = phase_table(numbers, numbers, sign_value)
    partly = along_last(values_in.reshape(leading + (x_local, KS)), cosine, sine_part)
    gathered = lax.all_gather(partly.reshape(values_in.shape), "ka", axis=5, tiled=True)
    grid = gathered.reshape(leading + (KS, KS))
    col_cos, col_sin = phase_table(numbers, owned, sign_value)
    return along_second(grid, col_cos, col_sin).reshape(values_in.shape)


def self_energy(row_space, screens):
    green_real = row_space[0][None]
    green_imag = row_space[1][None]
    real_part = -(green_real * screens[1] + green_imag * screens[0])
    imag_part = green_real * screens[0] - green_imag * screens[1]
    return jnp.stack([real_part, imag_part])


def coupling(sigma_pair):
    return jnp.stack(
        [jnp.stack([sigma_pair[0], -sigma_pair[1]]), jnp.stack([sigma_pair[1], sigma_pair[0]])]
    )


def dispersion(slab_start, all_times, kx_ids, ky_ids):
    current = (slab_start[0] + all_times).astype(jnp.float32)
    shift = drive_amp * jnp.sin(drive_freq * current)
    factor = 2.0 * math.pi / KS
    return -2.0 * (
        jnp.cos(kx_ids.astype(jnp.float32) * factor + shift)
        + jnp.cos(ky_ids.astype(jnp.float32) * factor)
    )


def apply_h(row, onsite, energy):
    real_part = (
        jnp.einsum("ab,bctk->actk", onsite[0], row[0], precision=highest)
        - jnp.einsum("ab,bctk->actk", onsite[1], row[1], precision=highest)
        + energy * row[0]
    )
    imag_part = (
        jnp.einsum("ab,bctk->actk", onsite[0], row[1], precision=highest)
        + jnp.einsum("ab,bctk->actk", onsite[1], row[0], precision=highest)
        + energy * row[1]
    )
    return jnp.stack([real_part, imag_part])


def masked_product(less_coupling, row_times, piece_times, piece_adv):
    visible = row_times[:, None] <= piece_times[None, :]
    masked = jnp.where(visible[:, :, None], piece_adv, jnp.zeros_like(piece_adv))
    return jnp.einsum(
        "pqabsk,qbcstk->tpack", less_coupling, masked, preferred_element_type=jnp.float32
    )


def plain(
    green_row,
    screen_lesser,
    screen_retarded,
    onsite,
    lesser_slab,
    advanced_slab,
    slab_start,
    block_table,
):
    local_rows = green_row.shape[3]
    k_local = green_row.shape[4]
    ta_count = lax.axis_size("ta")
    all_times = local_rows * ta_count
    my_index = lax.axis_index("ta")
    ka_index = lax.axis_index("ka")
    my_block = lax.dynamic_slice_in_dim(block_table, my_index, 1)[0]
    row_times = my_block * local_rows + jnp.arange(local_rows, dtype=jnp.int32)
    col_times = jnp.repeat(block_table, local_rows) * local_rows + jnp.tile(
        jnp.arange(local_rows, dtype=jnp.int32), ta_count
    )
    momenta = ka_index * k_local + jnp.arange(k_local, dtype=jnp.int32)
    energy = dispersion(slab_start, all_times, momenta // KS, momenta % KS)
    first_space = transform(
        jnp.stack([screen_lesser, screen_retarded, green_row], axis=1), 1.0, ka_index
    )
    screens = first_space[:, 0:2]

    def rate_of(row, row_space):
        sigma_all = transform(self_energy(row_space, screens), -1.0, ka_index).astype(jnp.bfloat16)
        less_coupling = coupling(sigma_all[:, 0])
        ret_coupling = coupling(sigma_all[:, 1])
        totals = jnp.einsum(
            "pqabsk,qbcstk->tpack", ret_coupling, lesser_slab, preferred_element_type=jnp.float32
        )
        own_rows = lax.psum_scatter(
            totals + masked_product(less_coupling, row_times, col_times, advanced_slab),
            "ta",
            scatter_dimension=0,
            tiled=True,
        )
        collision = jnp.transpose(own_rows, (1, 2, 3, 0, 4))
        totals = apply_h(row, onsite, energy) + collision
        return jnp.stack([totals[1], -totals[0]])

    first_rate = rate_of(green_row, first_space[:, 2])
    estimate = green_row + time_step * first_rate
    latest = first_rate
    for _ in range(2):
        row_space = transform(estimate[:, None], 1.0, ka_index)[:, 0]
        latest = rate_of(estimate, row_space)
        estimate = green_row + 0.5 * time_step * (first_rate + latest)
    return (estimate, latest)


def halving(size):
    return size > 0 and size & (size - 1) == 0


def suits(green_row, ta_count, ka_count):
    orbitals, local_rows, k_local = green_row.shape[1], green_row.shape[3], green_row.shape[4]
    return (
        ka_count == 2
        and orbitals * local_rows == SUBLANES
        and orbitals >= 4
        and halving(orbitals)
        and halving(ta_count)
        and ta_count % (2 * orbitals) == 0
        and k_local % LANES == 0
        and halving(k_local // LANES)
        and LANES % KS == 0
        and k_local * ka_count == KS * KS
    )


def fourier_tables(tiles):
    lane = np.arange(LANES)
    outer, inner = lane // KS, lane % KS
    group = LANES // KS
    angle = 2.0 * np.pi * (
        (outer[:, None] * outer[None, :] % group) / group + (inner[:, None] * inner[None, :] % KS) / KS
    )
    cosine, sine = np.cos(angle) / KS, np.sin(angle) / KS
    full = np.block([[cosine, sine], [-sine, cosine]]).astype(np.float32)
    high = full.astype(jnp.bfloat16)
    low = (full - high.astype(np.float32)).astype(jnp.bfloat16)
    turn = 2.0 * np.pi * (outer[None, :] * np.arange(tiles)[:, None]) / KS
    twiddle = np.stack([np.cos(turn), np.sin(turn)], axis=1).astype(np.float32)
    return jnp.asarray(np.stack([high, low])), jnp.asarray(twiddle)


def radix(values):
    count = len(values)
    if count == 1:
        return values
    half = count // 2
    sums, differences = [], []
    for place in range(half):
        (ar, ai), (br, bi) = values[place], values[place + half]
        sums.append((ar + br, ai + bi))
        dr, di = ar - br, ai - bi
        if place == 0:
            differences.append((dr, di))
        elif 4 * place == count:
            differences.append((-di, dr))
        else:
            cosine = math.cos(2.0 * math.pi * place / count)
            sine = math.sin(2.0 * math.pi * place / count)
            differences.append((dr * cosine - di * sine, dr * sine + di * cosine))
    even, odd = radix(sums), radix(differences)
    return [pair for both in zip(even, odd) for pair in both]


def turned(pair, twiddle_ref, tile):
    if tile == 0:
        return pair
    cosine, sine = twiddle_ref[tile, 0:1, :], twiddle_ref[tile, 1:2, :]
    return (pair[0] * cosine - pair[1] * sine, pair[0] * sine + pair[1] * cosine)


def lane_transform(rows, table_ref):
    high = rows.astype(jnp.bfloat16)
    low = (rows - high.astype(jnp.float32)).astype(jnp.bfloat16)
    first, second = table_ref[0], table_ref[1]
    dot = functools.partial(jnp.dot, preferred_element_type=jnp.float32)
    return dot(high, first) + (dot(low, first) + dot(high, second))


def to_sites(fields, table_ref, twiddle_ref):
    pieces = []
    for tiles in fields:
        for tile, pair in enumerate(radix(tiles)):
            pieces.append(jnp.concatenate(turned(pair, twiddle_ref, tile), axis=1))
    return lane_transform(jnp.concatenate(pieces, axis=0), table_ref)


def tiles_of(load, count):
    return [
        (load(0, pl.ds(tile * LANES, LANES)), load(1, pl.ds(tile * LANES, LANES)))
        for tile in range(count)
    ]


def emit_sigma(ka, space, screens_ref, table_ref, twiddle_ref, own_ref, send_ref):
    halves, k_local = own_ref.shape[2], own_ref.shape[4]
    local_tiles = k_local // LANES
    tiles = 2 * local_tiles
    green_real, green_imag = space[:, :LANES], space[:, LANES:]
    products = []
    for field in range(2):
        screen_real, screen_imag = screens_ref[field, :, :LANES], screens_ref[field, :, LANES:]
        real_part = -(green_real * screen_imag + green_imag * screen_real)
        conjugate = green_imag * screen_imag - green_real * screen_real
        products.append(jnp.concatenate([real_part, conjugate], axis=1))
    back = lane_transform(jnp.concatenate(products, axis=0), table_ref)
    for field in range(2):
        for half in range(halves):
            parts = []
            for tile in range(tiles):
                row = ((field * halves + half) * tiles + tile) * SUBLANES
                pair = (back[row : row + SUBLANES, :LANES], back[row : row + SUBLANES, LANES:])
                parts.append(turned(pair, twiddle_ref, tile))
            parts = radix(parts)
            for tile in range(local_tiles):
                for plane, sign in ((0, 1.0), (1, -1.0)):
                    near = (sign * parts[tile][plane]).astype(jnp.bfloat16).astype(jnp.float32)
                    far = (
                        (sign * parts[tile + local_tiles][plane])
                        .astype(jnp.bfloat16)
                        .astype(jnp.float32)
                    )
                    where_to = pl.ds(tile * LANES, LANES)
                    own_ref[field, plane, half, :, where_to] = jnp.where(ka == 0, near, far)
                    send_ref[field, plane, half, :, where_to] = jnp.where(ka == 0, far, near)


def pack_kernel(own_side, place_ref, lesser_ref, retarded_ref, green_ref, packed_ref):
    halves, inner, local_rows = packed_ref.shape[2], lesser_ref.shape[2], lesser_ref.shape[3]
    side = place_ref[1] if own_side else 1 - place_ref[1]
    for field, ref in enumerate((lesser_ref, retarded_ref, green_ref)):
        for plane in range(2):
            for half in range(halves):
                for column in range(inner):
                    begin = column * local_rows
                    packed_ref[field, plane, half, begin : begin + local_rows, :] = ref[
                        plane, side * halves + half, column
                    ]


def opening_kernel(
    place_ref, own_ref, other_ref, table_ref, twiddle_ref, screens_ref, sigma_ref, send_ref
):
    halves, k_local = own_ref.shape[2], own_ref.shape[4]
    local_tiles = k_local // LANES
    spaces = []
    for field in range(3):
        rows = []
        for half in range(halves):
            near = tiles_of(lambda p, ds: own_ref[field, p, half, :, ds], local_tiles)
            far = tiles_of(lambda p, ds: other_ref[field, p, half, :, ds], local_tiles)
            rows.append(near + far)
        spaces.append(to_sites(rows, table_ref, twiddle_ref))
    screens_ref[0] = spaces[0]
    screens_ref[1] = spaces[1]
    emit_sigma(
        place_ref[1], spaces[2], screens_ref, table_ref, twiddle_ref, sigma_ref, send_ref
    )


def rate_pieces(own_side, ka, half, tile, onsite_ref, energy_ref, near_ref, far_ref, sums_refs):
    halves = near_ref.shape[1]
    lanes = pl.ds(tile * LANES, LANES)
    mine = ka if own_side else 1 - ka
    row = mine * halves + half
    here = near_ref if own_side else far_ref
    real_part = functools.reduce(jnp.add, [ref[0, half, :, lanes] for ref in sums_refs])
    imag_part = functools.reduce(jnp.add, [ref[1, half, :, lanes] for ref in sums_refs])
    energy = energy_ref[0:1, lanes]
    real_part = real_part + energy * here[0, half, :, lanes]
    imag_part = imag_part + energy * here[1, half, :, lanes]
    for side, ref in ((ka, near_ref), (1 - ka, far_ref)):
        for column in range(halves):
            coupling_real = onsite_ref[0, row, side * halves + column]
            coupling_imag = onsite_ref[1, row, side * halves + column]
            value_real, value_imag = ref[0, column, :, lanes], ref[1, column, :, lanes]
            real_part = real_part + coupling_real * value_real - coupling_imag * value_imag
            imag_part = imag_part + coupling_real * value_imag + coupling_imag * value_real
    return imag_part, -real_part


def advance_far_kernel(
    is_first, sums_count, place_ref, onsite_ref, energy_ref, near_ref, far_ref, green_ref, *refs
):
    ka = place_ref[1]
    sums_refs, (first_ref, estimate_ref) = refs[:sums_count], refs[sums_count:]
    halves, k_local = far_ref.shape[1], far_ref.shape[3]
    for half in range(halves):
        for tile in range(k_local // LANES):
            lanes = pl.ds(tile * LANES, LANES)
            rates = rate_pieces(
                False, ka, half, tile, onsite_ref, energy_ref, near_ref, far_ref, sums_refs
            )
            for plane in range(2):
                start = green_ref[plane, half, :, lanes]
                if is_first:
                    first_ref[plane, half, :, lanes] = rates[plane]
                    estimate_ref[plane, half, :, lanes] = start + time_step * rates[plane]
                else:
                    estimate_ref[plane, half, :, lanes] = start + 0.5 * time_step * (
                        first_ref[plane, half, :, lanes] + rates[plane]
                    )


def advance_near_kernel(
    is_first, sums_count, place_ref, onsite_ref, energy_ref, near_ref, far_ref, green_ref,
    arrived_ref, screens_ref, table_ref, twiddle_ref, *refs
):
    ka = place_ref[1]
    sums_refs = refs[:sums_count]
    first_ref, estimate_ref, sigma_ref, send_ref = refs[sums_count:]
    halves, k_local = near_ref.shape[1], near_ref.shape[3]
    local_tiles = k_local // LANES
    fields = []
    for half in range(halves):
        parts = []
        for tile in range(local_tiles):
            lanes = pl.ds(tile * LANES, LANES)
            rates = rate_pieces(
                True, ka, half, tile, onsite_ref, energy_ref, near_ref, far_ref, sums_refs
            )
            pair = []
            for plane in range(2):
                start = green_ref[plane, half, :, lanes]
                if is_first:
                    first_ref[plane, half, :, lanes] = rates[plane]
                    value = start + time_step * rates[plane]
                else:
                    value = start + 0.5 * time_step * (
                        first_ref[plane, half, :, lanes] + rates[plane]
                    )
                estimate_ref[plane, half, :, lanes] = value
                pair.append(value)
            parts.append(tuple(pair))
        parts += tiles_of(lambda p, ds: arrived_ref[p, half, :, ds], local_tiles)
        fields.append(parts)
    space = to_sites(fields, table_ref, twiddle_ref)
    emit_sigma(ka, space, screens_ref, table_ref, twiddle_ref, sigma_ref, send_ref)


def closing_kernel(
    near_count, far_count, place_ref, onsite_ref, energy_ref, near_ref, far_ref, green_near_ref,
    green_far_ref, first_near_ref, first_far_ref, *refs
):
    ka = place_ref[1]
    near_sums, far_sums = refs[:near_count], refs[near_count : near_count + far_count]
    next_ref, latest_ref = refs[near_count + far_count :]
    halves, k_local = near_ref.shape[1], near_ref.shape[3]
    sides = (
        (True, ka, near_sums, green_near_ref, first_near_ref),
        (False, 1 - ka, far_sums, green_far_ref, first_far_ref),
    )
    for own_side, side, sums_refs, green_ref, first_ref in sides:
        for half in range(halves):
            for tile in range(k_local // LANES):
                lanes = pl.ds(tile * LANES, LANES)
                rates = rate_pieces(
                    own_side, ka, half, tile, onsite_ref, energy_ref, near_ref, far_ref, sums_refs
                )
                for plane in range(2):
                    value = green_ref[plane, half, :, lanes] + 0.5 * time_step * (
                        first_ref[plane, half, :, lanes] + rates[plane]
                    )
                    for column in range(next_ref.shape[2]):
                        begin = column * next_ref.shape[3]
                        span = slice(begin, begin + next_ref.shape[3])
                        latest_ref[plane, side * halves + half, column, :, lanes] = rates[plane][span]
                        next_ref[plane, side * halves + half, column, :, lanes] = value[span]


def swap_rows(values, local_rows):
    count = len(values)
    group = lax.broadcasted_iota(jnp.int32, (SUBLANES, LANES), 0) // local_rows
    values = list(values)
    step = 1
    while step < count:
        low = (group & step) == 0
        for place in range(count):
            if place & step == 0:
                first, second = values[place], values[place | step]
                shift = step * local_rows
                values[place] = jnp.where(low, first, pltpu.roll(second, shift, 0))
                values[place | step] = jnp.where(
                    low, pltpu.roll(first, SUBLANES - shift, 0), second
                )
        step *= 2
    return values


def collide_kernel(
    order, place_ref, sigma_ref, causal_ref, lesser_ref, advanced_ref, keep_ref, send_ref
):
    halves, k_local = sigma_ref.shape[2], sigma_ref.shape[4]
    orbitals, local_rows, times = lesser_ref.shape[1], lesser_ref.shape[3], lesser_ref.shape[4]
    rows = 2 * SUBLANES
    time_steps = times // rows
    me = place_ref[0]

    def gather(total, value):
        return value if total is None else total + value

    def step(counter, carried):
        time_step_index = counter % time_steps
        first_row = pl.multiple_of(time_step_index * rows, rows)
        lanes = pl.ds(pl.multiple_of(counter // time_steps * LANES, LANES), LANES)
        here = pl.ds(first_row, rows)
        sums_real = [[None] * orbitals for _ in range(halves)]
        sums_imag = [[None] * orbitals for _ in range(halves)]
        for field, slab_ref in ((1, lesser_ref), (0, advanced_ref)):
            for stored in range(local_rows):
                for inner in range(orbitals):
                    row = inner * local_rows + stored
                    sigma_real, sigma_imag = [], []
                    for half in range(halves):
                        for plane, found in ((0, sigma_real), (1, sigma_imag)):
                            value = sigma_ref[field, plane, half, row : row + 1, lanes]
                            value = jnp.broadcast_to(value, (rows, LANES))
                            if field == 0:
                                value = value * causal_ref[stored, here]
                            found.append(value)
                    for outer in range(orbitals):
                        slab_real = slab_ref[0, inner, outer, stored, here, lanes]
                        slab_imag = slab_ref[1, inner, outer, stored, here, lanes]
                        slab_real = slab_real.astype(jnp.float32)
                        slab_imag = slab_imag.astype(jnp.float32)
                        for half in range(halves):
                            sums_real[half][outer] = (
                                gather(sums_real[half][outer], sigma_real[half] * slab_real)
                                - sigma_imag[half] * slab_imag
                            )
                            sums_imag[half][outer] = (
                                gather(sums_imag[half][outer], sigma_real[half] * slab_imag)
                                + sigma_imag[half] * slab_real
                            )
        even = (me & 1) == 0
        for piece in range(rows // SUBLANES):
            tile = time_step_index * (rows // SUBLANES) + piece
            begin = piece * SUBLANES
            for half in range(halves):
                for plane, sums in ((0, sums_real), (1, sums_imag)):
                    owners = swap_rows(
                        [sums[half][outer][begin : begin + SUBLANES] for outer in range(orbitals)],
                        local_rows,
                    )
                    for pair in range(0, orbitals, 2):
                        relative = (tile * orbitals + pair) ^ me
                        where_to = 0
                        for bit in order[1:]:
                            where_to = where_to * 2 + ((relative >> bit) & 1)
                        first, second = owners[pair], owners[pair + 1]
                        keep_ref[where_to, plane, half, :, lanes] = jnp.where(even, first, second)
                        send_ref[where_to, plane, half, :, lanes] = jnp.where(even, second, first)
        return carried

    lax.fori_loop(0, time_steps * (k_local // LANES), step, 0)


def whole(memory_space=pltpu.VMEM):
    return pl.BlockSpec(memory_space=memory_space)


def float_like(*shape):
    return jax.ShapeDtypeStruct(shape, jnp.float32)


def flip(bit, count):
    return [(place, place ^ bit) for place in range(count)]


def halved_sum(keep, send, order, direct_bits, ta_count):
    got = lax.ppermute(send, "ta", flip(1 << order[0], ta_count))
    for bit in order[1 : len(order) - direct_bits]:
        half = keep.shape[0] // 2
        outgoing = keep[half:] + got[half:]
        arriving = lax.ppermute(outgoing, "ta", flip(1 << bit, ta_count))
        keep, got = keep[:half] + got[:half], arriving
    if direct_bits == 0:
        return keep[0], got[0]
    shift = order[-1]
    pieces = [keep[place] + got[place] for place in range(1 << direct_bits)]
    results = []
    for place in range(1, 1 << direct_bits):
        results.append(lax.ppermute(pieces[place], "ta", flip(place << shift, ta_count)))
    return (pieces[0], *results)


def fast(
    green_row, screen_lesser, screen_retarded, onsite, lesser_slab, advanced_slab, slab_start,
    block_table
):
    orbitals, local_rows, k_local = green_row.shape[1], green_row.shape[3], green_row.shape[4]
    ta_count, ka_count = lax.axis_size("ta"), lax.axis_size("ka")
    all_times = local_rows * ta_count
    halves = orbitals // 2
    tiles = k_local * ka_count // LANES
    ta_index, ka_index = lax.axis_index("ta"), lax.axis_index("ka")
    place = jnp.stack([ta_index, ka_index]).astype(jnp.int32)
    table, twiddle = fourier_tables(tiles)
    my_block = lax.dynamic_slice_in_dim(block_table, ta_index, 1)[0]
    row_times = my_block * local_rows + jnp.arange(local_rows, dtype=jnp.int32)
    col_times = jnp.repeat(block_table, local_rows) * local_rows + jnp.tile(
        jnp.arange(local_rows, dtype=jnp.int32), ta_count
    )
    causal = (row_times[:, None] <= col_times[None, :]).astype(jnp.float32)
    causal = jnp.broadcast_to(causal[:, :, None], (local_rows, all_times, LANES))
    momenta = ka_index * k_local + jnp.arange(k_local, dtype=jnp.int32)
    energy = dispersion(slab_start, all_times, momenta // KS, momenta % KS)[None]

    chunk = (2, halves, SUBLANES, k_local)
    scalar = whole(pltpu.SMEM)
    space_rows = halves * tiles * SUBLANES
    sigma_shape = float_like(2, *chunk)
    small = pltpu.CompilerParams(vmem_limit_bytes=8 * 1024 * 1024)

    def packed(own_side):
        return pl.pallas_call(
            functools.partial(pack_kernel, own_side),
            out_shape=float_like(3, *chunk),
            in_specs=[scalar] + [whole()] * 3,
            out_specs=whole(),
            compiler_params=small,
            name="pack",
        )(place, screen_lesser, screen_retarded, green_row)

    far_fields = packed(False)
    arrived_fields = lax.ppermute(far_fields, "ka", flip(1, ka_count))
    near_fields = packed(True)
    green_near, green_far = near_fields[2], far_fields[2]

    screens, sigma_near, sigma_send = pl.pallas_call(
        opening_kernel,
        out_shape=(float_like(2, space_rows, 2 * LANES), sigma_shape, sigma_shape),
        in_specs=[scalar] + [whole()] * 4,
        out_specs=(whole(),) * 3,
        compiler_params=small,
        name="opening",
    )(place, near_fields, arrived_fields, table, twiddle)

    bits = ta_count.bit_length() - 1
    owner_bits = orbitals.bit_length() - 1
    order = list(range(owner_bits)) + list(range(owner_bits, bits))[::-1]
    direct_bits = bits - owner_bits

    def collide(sigma):
        return pl.pallas_call(
            functools.partial(collide_kernel, order),
            out_shape=(float_like(ta_count // 2, *chunk),) * 2,
            in_specs=[scalar] + [whole()] * 4,
            out_specs=(whole(),) * 2,
            compiler_params=small,
            cost_estimate=pl.CostEstimate(
                flops=16 * halves * orbitals * orbitals * local_rows * all_times * k_local,
                bytes_accessed=4 * lesser_slab.size,
                transcendentals=0,
            ),
            name="collide",
        )(place, sigma, causal, lesser_slab, advanced_slab)

    def collisions(sigma_near, sigma_send):
        sigma_far = lax.ppermute(sigma_send, "ka", flip(1, ka_count))
        near = collide(sigma_near)
        far = collide(sigma_far)
        near_sums = halved_sum(*near, order, 0, ta_count)
        far_sums = halved_sum(*far, order, direct_bits, ta_count)
        return near_sums, far_sums

    estimate_near, estimate_far = green_near, green_far
    first_near = first_far = None
    chunk_shape = float_like(*chunk)
    for corrector in range(2):
        near_sums, far_sums = collisions(sigma_near, sigma_send)
        is_first = corrector == 0
        common = (place, onsite, energy, estimate_near, estimate_far)
        tables = (screens, table, twiddle)
        if is_first:
            far_out, near_out = (chunk_shape,) * 2, (chunk_shape,) * 2
            extra_far, extra_near = (), ()
        else:
            far_out, near_out = (chunk_shape,), (chunk_shape,)
            extra_far, extra_near = (first_far,), (first_near,)
        near_out = near_out + (sigma_shape,) * 2
        far_inputs = common + (green_far,) + far_sums + extra_far
        far_result = pl.pallas_call(
            functools.partial(advance_far_kernel, is_first, len(far_sums)),
            out_shape=far_out,
            in_specs=[scalar, scalar] + [whole()] * (len(far_inputs) - 2),
            out_specs=(whole(),) * len(far_out),
            compiler_params=small,
            name="advance_far",
        )(*far_inputs)
        arrived = lax.ppermute(far_result[-1], "ka", flip(1, ka_count))
        near_inputs = common + (green_near, arrived) + tables + near_sums + extra_near
        near_result = pl.pallas_call(
            functools.partial(advance_near_kernel, is_first, len(near_sums)),
            out_shape=near_out,
            in_specs=[scalar, scalar] + [whole()] * (len(near_inputs) - 2),
            out_specs=(whole(),) * len(near_out),
            compiler_params=small,
            name="advance_near",
        )(*near_inputs)
        if is_first:
            first_far, first_near = far_result[0], near_result[0]
        estimate_far = far_result[-1]
        estimate_near, sigma_near, sigma_send = near_result[-3:]
    near_sums, far_sums = collisions(sigma_near, sigma_send)
    full = float_like(*green_row.shape)
    return pl.pallas_call(
        functools.partial(closing_kernel, len(near_sums), len(far_sums)),
        out_shape=(full, full),
        in_specs=[scalar, scalar] + [whole()] * (7 + len(near_sums) + len(far_sums)),
        out_specs=(whole(), whole()),
        compiler_params=small,
        name="closing",
    )(
        place, onsite, energy, estimate_near, estimate_far, green_near, green_far, first_near,
        first_far, *near_sums, *far_sums,
    )


def local(*args):
    if suits(args[0], lax.axis_size("ta"), lax.axis_size("ka")):
        return fast(*args)
    return plain(*args)


def solution(mesh):
    return jax.shard_map(
        local,
        mesh=mesh,
        in_specs=(
            P(None, None, None, "ta", "ka"),
            P(None, None, None, "ta", "ka"),
            P(None, None, None, "ta", "ka"),
            P(),
            P(None, None, None, "ta", None, "ka"),
            P(None, None, None, "ta", None, "ka"),
            P(),
            P(),
        ),
        out_specs=(P(None, None, None, "ta", "ka"), P(None, None, None, "ta", "ka")),
        check_vma=False,
    )
```

profile of v0, /device:TPU:0, one launch (start us, length us, event | category | flops | bytes accessed | tf_op | source)
XLA Modules:
  0.0 145.7 jit_solution(9279358610830315453)
XLA Ops:
  4.0 3.0 %collective-permute-start = (f32[3,2,2,8,512]{4,3,2,1,0:T(8,128)S(1)}, f32[3,2,2,8,512]{4,3,2,1,0:T(8,128)S(1)}, u32[]{:S(2)}, u32[]{:S(2)}) collective-permute-start(f32[3,2,2,8,512]{4,3,2,1,0:T(8,128)S(1)} %pack.3), channel_id=1, source_target_pairs={{0,1},{1,0},{2,3},{3,2},{4,5},{5,4},{6,7},{7,6},{8,9},{9,8},{10,11... | collective-permute-start | bytes 589832 | tf_op jit(solution)/shard_map/ppermute | solution.py:583
  8.3 1.2 dynamic_slice.3
  10.5 1.5 %collective-permute-done.other_ref = f32[3,2,2,8,512]{4,3,2,1,0:T(8,128)S(1)} collective-permute-done((f32[3,2,2,8,512]{4,3,2,1,0:T(8,128)S(1)}, f32[3,2,2,8,512]{4,3,2,1,0:T(8,128)S(1)}, u32[]{:S(2)}, u32[]{:S(2)}) %collective-permute-start) | collective-permute-done | bytes 196640 | tf_op jit(solution)/shard_map/ppermute | solution.py:583
  14.9 1.6 %copy-done = bf16[2,4,4,2,32,512]{5,4,3,2,1,0:T(8,128)(2,1)S(1)} copy-done((bf16[2,4,4,2,32,512]{5,4,3,2,1,0:T(8,128)(2,1)S(1)}, bf16[2,4,4,2,32,512]{5,4,3,2,1,0:T(8,128)(2,1)}, u32[]{:S(2)}) %copy-start) | copy-done | bytes 2097176
  16.5 1.6 %copy-done.2 = bf16[2,4,4,2,32,512]{5,4,3,2,1,0:T(8,128)(2,1)S(1)} copy-done((bf16[2,4,4,2,32,512]{5,4,3,2,1,0:T(8,128)(2,1)S(1)}, bf16[2,4,4,2,32,512]{5,4,3,2,1,0:T(8,128)(2,1)}, u32[]{:S(2)}) %copy-start.2) | copy-done | bytes 2097176
  18.1 3.7 %collide.7 = (f32[8,2,2,8,512]{4,3,2,1,0:T(8,128)S(1)}, f32[8,2,2,8,512]{4,3,2,1,0:T(8,128)S(1)}) custom-call(s32[2]{0:T(128)S(1)} %pad_add_fusion.place_ref, f32[2,2,2,8,512]{4,3,2,1,0:T(8,128)S(1)} %get-tuple-element.31.sigma_ref, f32[2,32,128]{2,1,0:T(8,128)S(1)} %broadcast_in_dim.5.causal_ref, bf16[2,4,4,2,32,512]{5,4,3,2,1,0:T(8,128)(2,1)S(1)} %copy-done, ...), custom_call_target="tpu_custom_call" | custom-call | flops 16777216 | bytes 4194304 | tf_op jit(solution)/shard_map/collide/pallas_call | solution.py:602
  21.8 1.8 %collective-permute-start.1 = (f32[2,2,2,8,512]{4,3,2,1,0:T(8,128)S(1)}, f32[2,2,2,8,512]{4,3,2,1,0:T(8,128)S(1)}, u32[]{:S(2)}, u32[]{:S(2)}) collective-permute-start(f32[2,2,2,8,512]{4,3,2,1,0:T(8,128)S(1)} %get-tuple-element.26), channel_id=1, source_target_pairs={{0,1},{1,0},{2,3},{3,2},{4,5},{5,4},{6,7},{7,6},{8,9},{9,8},{10,11... | collective-permute-start | bytes 393224 | tf_op jit(solution)/shard_map/ppermute | solution.py:617
  23.6 4.1 %collective-permute-done.1.sigma_ref = f32[2,2,2,8,512]{4,3,2,1,0:T(8,128)S(1)} collective-permute-done((f32[2,2,2,8,512]{4,3,2,1,0:T(8,128)S(1)}, f32[2,2,2,8,512]{4,3,2,1,0:T(8,128)S(1)}, u32[]{:S(2)}, u32[]{:S(2)}) %collective-permute-start.1) | collective-permute-done | bytes 131104 | tf_op jit(solution)/shard_map/ppermute | solution.py:617
  27.7 3.7 %collide.6 = (f32[8,2,2,8,512]{4,3,2,1,0:T(8,128)S(1)}, f32[8,2,2,8,512]{4,3,2,1,0:T(8,128)S(1)}) custom-call(s32[2]{0:T(128)S(1)} %pad_add_fusion.place_ref, f32[2,2,2,8,512]{4,3,2,1,0:T(8,128)S(1)} %collective-permute-done.1.sigma_ref, f32[2,32,128]{2,1,0:T(8,128)S(1)} %broadcast_in_dim.5.causal_ref, bf16[2,4,4,2,32,512]{5,4,3,2,1,0:T(8,128)(2,1)S(1)} %copy-done, ...), custom_call_target="tpu_custom_call" | custom-call | flops 16777216 | bytes 4194304 | tf_op jit(solution)/shard_map/collide/pallas_call | solution.py:602
  32.4 1.8 %collective-permute-start.9 = (f32[4,2,2,8,512]{4,3,2,1,0:T(8,128)S(1)}, f32[4,2,2,8,512]{4,3,2,1,0:T(8,128)S(1)}, u32[]{:S(2)}, u32[]{:S(2)}) collective-permute-start(f32[4,2,2,8,512]{4,3,2,1,0:T(8,128)S(1)} %get-tuple-element.59), channel_id=1, source_target_pairs={{0,4},{2,6},{4,0},{6,2},{8,12},{10,14},{12,8},{14,10},{16,20},{18,... | collective-permute-start | bytes 786440 | tf_op jit(solution)/shard_map/ppermute | solution.py:532
  34.2 1.3 slice_add_fusion.11
  36.8 4.9 %collective-permute-done.9 = f32[4,2,2,8,512]{4,3,2,1,0:T(8,128)S(1)} collective-permute-done((f32[4,2,2,8,512]{4,3,2,1,0:T(8,128)S(1)}, f32[4,2,2,8,512]{4,3,2,1,0:T(8,128)S(1)}, u32[]{:S(2)}, u32[]{:S(2)}) %collective-permute-start.9) | collective-permute-done | bytes 262176 | tf_op jit(solution)/shard_map/ppermute | solution.py:532
  41.7 2.9 %collective-permute-start.10 = (f32[2,2,2,8,512]{4,3,2,1,0:T(8,128)S(1)}, f32[2,2,2,8,512]{4,3,2,1,0:T(8,128)S(1)}, u32[]{:S(2)}, u32[]{:S(2)}) collective-permute-start(f32[2,2,2,8,512]{4,3,2,1,0:T(8,128)S(1)} %get-tuple-element.75), channel_id=1, source_target_pairs={{0,16},{2,18},{4,20},{6,22},{8,24},{10,26},{12,28},{14,30},{16,0},... | collective-permute-start | bytes 393224 | tf_op jit(solution)/shard_map/ppermute | solution.py:532
  44.6 2.2 %collective-permute-done.3 = f32[4,2,2,8,512]{4,3,2,1,0:T(8,128)S(1)} collective-permute-done((f32[4,2,2,8,512]{4,3,2,1,0:T(8,128)S(1)}, f32[4,2,2,8,512]{4,3,2,1,0:T(8,128)S(1)}, u32[]{:S(2)}, u32[]{:S(2)}) %collective-permute-start.3) | collective-permute-done | bytes 262176 | tf_op jit(solution)/shard_map/ppermute | solution.py:532
  46.8 3.9 %collective-permute-start.6 = (f32[2,2,8,512]{3,2,1,0:T(8,128)S(1)}, f32[2,2,8,512]{3,2,1,0:T(8,128)S(1)}, u32[]{:S(2)}, u32[]{:S(2)}) collective-permute-start(f32[2,2,8,512]{3,2,1,0:T(8,128)S(1)} %get-tuple-element.76), channel_id=1, source_target_pairs={{0,24},{2,26},{4,28},{6,30},{8,16},{10,18},{12,20},{14,22},{16,8},... | collective-permute-start | bytes 196616 | tf_op jit(solution)/shard_map/ppermute | solution.py:540
  51.4 1.5 collective-permute-start.11
  53.4 2.9 %collective-permute-done.5.refs_2_ = f32[2,2,8,512]{3,2,1,0:T(8,128)S(1)} collective-permute-done((f32[2,2,8,512]{3,2,1,0:T(8,128)S(1)}, f32[2,2,8,512]{3,2,1,0:T(8,128)S(1)}, u32[]{:S(2)}, u32[]{:S(2)}) %collective-permute-start.5) | collective-permute-done | bytes 65568 | tf_op jit(solution)/shard_map/ppermute | solution.py:540
  57.2 1.8 %collective-permute-start.7 = (f32[2,2,8,512]{3,2,1,0:T(8,128)S(1)}, f32[2,2,8,512]{3,2,1,0:T(8,128)S(1)}, u32[]{:S(2)}, u32[]{:S(2)}) collective-permute-start(f32[2,2,8,512]{3,2,1,0:T(8,128)S(1)} %get-tuple-element.29.far_ref), channel_id=1, source_target_pairs={{0,1},{1,0},{2,3},{3,2},{4,5},{5,4},{6,7},{7,6},{8,9},{9,8},{10,11... | collective-permute-start | bytes 196616 | tf_op jit(solution)/shard_map/ppermute | solution.py:648
  59.0 2.5 %collective-permute-done.7.arrived_ref = f32[2,2,8,512]{3,2,1,0:T(8,128)S(1)} collective-permute-done((f32[2,2,8,512]{3,2,1,0:T(8,128)S(1)}, f32[2,2,8,512]{3,2,1,0:T(8,128)S(1)}, u32[]{:S(2)}, u32[]{:S(2)}) %collective-permute-start.7) | collective-permute-done | bytes 65568 | tf_op jit(solution)/shard_map/ppermute | solution.py:648
  61.6 1.2 advance_near.2
  62.8 3.7 %collide.9 = (f32[8,2,2,8,512]{4,3,2,1,0:T(8,128)S(1)}, f32[8,2,2,8,512]{4,3,2,1,0:T(8,128)S(1)}) custom-call(s32[2]{0:T(128)S(1)} %pad_add_fusion.place_ref, f32[2,2,2,8,512]{4,3,2,1,0:T(8,128)S(1)} %get-tuple-element.39.sigma_ref, f32[2,32,128]{2,1,0:T(8,128)S(1)} %broadcast_in_dim.5.causal_ref, bf16[2,4,4,2,32,512]{5,4,3,2,1,0:T(8,128)(2,1)S(1)} %copy-done.1, ...), custom_call_target="tpu_custom_call" | custom-call | flops 16777216 | bytes 4194304 | tf_op jit(solution)/shard_map/collide/pallas_call | solution.py:602
  66.6 1.8 %collective-permute-start.12 = (f32[2,2,2,8,512]{4,3,2,1,0:T(8,128)S(1)}, f32[2,2,2,8,512]{4,3,2,1,0:T(8,128)S(1)}, u32[]{:S(2)}, u32[]{:S(2)}) collective-permute-start(f32[2,2,2,8,512]{4,3,2,1,0:T(8,128)S(1)} %get-tuple-element.35), channel_id=1, source_target_pairs={{0,1},{1,0},{2,3},{3,2},{4,5},{5,4},{6,7},{7,6},{8,9},{9,8},{10,11... | collective-permute-start | bytes 393224 | tf_op jit(solution)/shard_map/ppermute | solution.py:617
  68.4 4.1 %collective-permute-done.12.sigma_ref = f32[2,2,2,8,512]{4,3,2,1,0:T(8,128)S(1)} collective-permute-done((f32[2,2,2,8,512]{4,3,2,1,0:T(8,128)S(1)}, f32[2,2,2,8,512]{4,3,2,1,0:T(8,128)S(1)}, u32[]{:S(2)}, u32[]{:S(2)}) %collective-permute-start.12) | collective-permute-done | bytes 131104 | tf_op jit(solution)/shard_map/ppermute | solution.py:617
  72.5 3.7 %collide.8 = (f32[8,2,2,8,512]{4,3,2,1,0:T(8,128)S(1)}, f32[8,2,2,8,512]{4,3,2,1,0:T(8,128)S(1)}) custom-call(s32[2]{0:T(128)S(1)} %pad_add_fusion.place_ref, f32[2,2,2,8,512]{4,3,2,1,0:T(8,128)S(1)} %collective-permute-done.12.sigma_ref, f32[2,32,128]{2,1,0:T(8,128)S(1)} %broadcast_in_dim.5.causal_ref, bf16[2,4,4,2,32,512]{5,4,3,2,1,0:T(8,128)(2,1)S(1)} %copy-done.1, ...), custom_call_target="tpu_custom_call" | custom-call | flops 16777216 | bytes 4194304 | tf_op jit(solution)/shard_map/collide/pallas_call | solution.py:602
  76.3 1.8 %collective-permute-start.20 = (f32[4,2,2,8,512]{4,3,2,1,0:T(8,128)S(1)}, f32[4,2,2,8,512]{4,3,2,1,0:T(8,128)S(1)}, u32[]{:S(2)}, u32[]{:S(2)}) collective-permute-start(f32[4,2,2,8,512]{4,3,2,1,0:T(8,128)S(1)} %get-tuple-element.55), channel_id=1, source_target_pairs={{0,4},{2,6},{4,0},{6,2},{8,12},{10,14},{12,8},{14,10},{16,20},{18,... | collective-permute-start | bytes 786440 | tf_op jit(solution)/shard_map/ppermute | solution.py:532
  78.3 1.8 %collective-permute-start.14 = (f32[4,2,2,8,512]{4,3,2,1,0:T(8,128)S(1)}, f32[4,2,2,8,512]{4,3,2,1,0:T(8,128)S(1)}, u32[]{:S(2)}, u32[]{:S(2)}) collective-permute-start(f32[4,2,2,8,512]{4,3,2,1,0:T(8,128)S(1)} %get-tuple-element.57), channel_id=1, source_target_pairs={{0,4},{2,6},{4,0},{6,2},{8,12},{10,14},{12,8},{14,10},{16,20},{18,... | collective-permute-start | bytes 786440 | tf_op jit(solution)/shard_map/ppermute | solution.py:532
  80.1 5.5 %collective-permute-done.20 = f32[4,2,2,8,512]{4,3,2,1,0:T(8,128)S(1)} collective-permute-done((f32[4,2,2,8,512]{4,3,2,1,0:T(8,128)S(1)}, f32[4,2,2,8,512]{4,3,2,1,0:T(8,128)S(1)}, u32[]{:S(2)}, u32[]{:S(2)}) %collective-permute-start.20) | collective-permute-done | bytes 262176 | tf_op jit(solution)/shard_map/ppermute | solution.py:532
  85.6 1.5 %collective-permute-start.21 = (f32[2,2,2,8,512]{4,3,2,1,0:T(8,128)S(1)}, f32[2,2,2,8,512]{4,3,2,1,0:T(8,128)S(1)}, u32[]{:S(2)}, u32[]{:S(2)}) collective-permute-start(f32[2,2,2,8,512]{4,3,2,1,0:T(8,128)S(1)} %get-tuple-element.69), channel_id=1, source_target_pairs={{0,16},{2,18},{4,20},{6,22},{8,24},{10,26},{12,28},{14,30},{16,0},... | collective-permute-start | bytes 393224 | tf_op jit(solution)/shard_map/ppermute | solution.py:532
  87.1 3.6 %collective-permute-done.14 = f32[4,2,2,8,512]{4,3,2,1,0:T(8,128)S(1)} collective-permute-done((f32[4,2,2,8,512]{4,3,2,1,0:T(8,128)S(1)}, f32[4,2,2,8,512]{4,3,2,1,0:T(8,128)S(1)}, u32[]{:S(2)}, u32[]{:S(2)}) %collective-permute-start.14) | collective-permute-done | bytes 262176 | tf_op jit(solution)/shard_map/ppermute | solution.py:532
  90.8 3.2 %collective-permute-start.17 = (f32[2,2,8,512]{3,2,1,0:T(8,128)S(1)}, f32[2,2,8,512]{3,2,1,0:T(8,128)S(1)}, u32[]{:S(2)}, u32[]{:S(2)}) collective-permute-start(f32[2,2,8,512]{3,2,1,0:T(8,128)S(1)} %get-tuple-element.70), channel_id=1, source_target_pairs={{0,24},{2,26},{4,28},{6,30},{8,16},{10,18},{12,20},{14,22},{16,8},... | collective-permute-start | bytes 196616 | tf_op jit(solution)/shard_map/ppermute | solution.py:540
  94.0 1.2 collective-permute-start.15
  97.2 2.7 %collective-permute-done.16.refs_2_ = f32[2,2,8,512]{3,2,1,0:T(8,128)S(1)} collective-permute-done((f32[2,2,8,512]{3,2,1,0:T(8,128)S(1)}, f32[2,2,8,512]{3,2,1,0:T(8,128)S(1)}, u32[]{:S(2)}, u32[]{:S(2)}) %collective-permute-start.16) | collective-permute-done | bytes 65568 | tf_op jit(solution)/shard_map/ppermute | solution.py:540
  100.9 1.6 %collective-permute-start.18 = (f32[2,2,8,512]{3,2,1,0:T(8,128)S(1)}, f32[2,2,8,512]{3,2,1,0:T(8,128)S(1)}, u32[]{:S(2)}, u32[]{:S(2)}) collective-permute-start(f32[2,2,8,512]{3,2,1,0:T(8,128)S(1)} %advance_far.3.far_ref), channel_id=1, source_target_pairs={{0,1},{1,0},{2,3},{3,2},{4,5},{5,4},{6,7},{7,6},{8,9},{9,8},{10,11... | collective-permute-start | bytes 196616 | tf_op jit(solution)/shard_map/ppermute | solution.py:648
  102.4 2.8 %collective-permute-done.18.arrived_ref = f32[2,2,8,512]{3,2,1,0:T(8,128)S(1)} collective-permute-done((f32[2,2,8,512]{3,2,1,0:T(8,128)S(1)}, f32[2,2,8,512]{3,2,1,0:T(8,128)S(1)}, u32[]{:S(2)}, u32[]{:S(2)}) %collective-permute-start.18) | collective-permute-done | bytes 65568 | tf_op jit(solution)/shard_map/ppermute | solution.py:648
  105.2 1.2 advance_near.3
  106.4 3.7 %collide.10 = (f32[8,2,2,8,512]{4,3,2,1,0:T(8,128)S(1)}, f32[8,2,2,8,512]{4,3,2,1,0:T(8,128)S(1)}) custom-call(s32[2]{0:T(128)S(1)} %pad_add_fusion.place_ref, f32[2,2,2,8,512]{4,3,2,1,0:T(8,128)S(1)} %get-tuple-element.44.sigma_ref, f32[2,32,128]{2,1,0:T(8,128)S(1)} %broadcast_in_dim.5.causal_ref, bf16[2,4,4,2,32,512]{5,4,3,2,1,0:T(8,128)(2,1)S(1)} %copy-done.1, ...), custom_call_target="tpu_custom_call" | custom-call | flops 16777216 | bytes 4194304 | tf_op jit(solution)/shard_map/collide/pallas_call | solution.py:602
  110.2 1.6 %collective-permute-start.27 = (f32[2,2,2,8,512]{4,3,2,1,0:T(8,128)S(1)}, f32[2,2,2,8,512]{4,3,2,1,0:T(8,128)S(1)}, u32[]{:S(2)}, u32[]{:S(2)}) collective-permute-start(f32[2,2,2,8,512]{4,3,2,1,0:T(8,128)S(1)} %get-tuple-element.47), channel_id=1, source_target_pairs={{0,1},{1,0},{2,3},{3,2},{4,5},{5,4},{6,7},{7,6},{8,9},{9,8},{10,11... | collective-permute-start | bytes 393224 | tf_op jit(solution)/shard_map/ppermute | solution.py:617
  111.7 4.3 %collective-permute-done.27.sigma_ref = f32[2,2,2,8,512]{4,3,2,1,0:T(8,128)S(1)} collective-permute-done((f32[2,2,2,8,512]{4,3,2,1,0:T(8,128)S(1)}, f32[2,2,2,8,512]{4,3,2,1,0:T(8,128)S(1)}, u32[]{:S(2)}, u32[]{:S(2)}) %collective-permute-start.27) | collective-permute-done | bytes 131104 | tf_op jit(solution)/shard_map/ppermute | solution.py:617
  116.1 3.7 %collide.11 = (f32[8,2,2,8,512]{4,3,2,1,0:T(8,128)S(1)}, f32[8,2,2,8,512]{4,3,2,1,0:T(8,128)S(1)}) custom-call(s32[2]{0:T(128)S(1)} %pad_add_fusion.place_ref, f32[2,2,2,8,512]{4,3,2,1,0:T(8,128)S(1)} %collective-permute-done.27.sigma_ref, f32[2,32,128]{2,1,0:T(8,128)S(1)} %broadcast_in_dim.5.causal_ref, bf16[2,4,4,2,32,512]{5,4,3,2,1,0:T(8,128)(2,1)S(1)} %copy-done.1, ...), custom_call_target="tpu_custom_call" | custom-call | flops 16777216 | bytes 4194304 | tf_op jit(solution)/shard_map/collide/pallas_call | solution.py:602
  119.9 1.6 %collective-permute-start.24 = (f32[4,2,2,8,512]{4,3,2,1,0:T(8,128)S(1)}, f32[4,2,2,8,512]{4,3,2,1,0:T(8,128)S(1)}, u32[]{:S(2)}, u32[]{:S(2)}) collective-permute-start(f32[4,2,2,8,512]{4,3,2,1,0:T(8,128)S(1)} %get-tuple-element.53), channel_id=1, source_target_pairs={{0,4},{2,6},{4,0},{6,2},{8,12},{10,14},{12,8},{14,10},{16,20},{18,... | collective-permute-start | bytes 786440 | tf_op jit(solution)/shard_map/ppermute | solution.py:532
  121.8 1.6 %collective-permute-start.29 = (f32[4,2,2,8,512]{4,3,2,1,0:T(8,128)S(1)}, f32[4,2,2,8,512]{4,3,2,1,0:T(8,128)S(1)}, u32[]{:S(2)}, u32[]{:S(2)}) collective-permute-start(f32[4,2,2,8,512]{4,3,2,1,0:T(8,128)S(1)} %get-tuple-element.51), channel_id=1, source_target_pairs={{0,4},{2,6},{4,0},{6,2},{8,12},{10,14},{12,8},{14,10},{16,20},{18,... | collective-permute-start | bytes 786440 | tf_op jit(solution)/shard_map/ppermute | solution.py:532
  123.4 5.8 %collective-permute-done.24 = f32[4,2,2,8,512]{4,3,2,1,0:T(8,128)S(1)} collective-permute-done((f32[4,2,2,8,512]{4,3,2,1,0:T(8,128)S(1)}, f32[4,2,2,8,512]{4,3,2,1,0:T(8,128)S(1)}, u32[]{:S(2)}, u32[]{:S(2)}) %collective-permute-start.24) | collective-permute-done | bytes 262176 | tf_op jit(solution)/shard_map/ppermute | solution.py:532
  130.4 3.9 %collective-permute-done.29 = f32[4,2,2,8,512]{4,3,2,1,0:T(8,128)S(1)} collective-permute-done((f32[4,2,2,8,512]{4,3,2,1,0:T(8,128)S(1)}, f32[4,2,2,8,512]{4,3,2,1,0:T(8,128)S(1)}, u32[]{:S(2)}, u32[]{:S(2)}) %collective-permute-start.29) | collective-permute-done | bytes 262176 | tf_op jit(solution)/shard_map/ppermute | solution.py:532
  134.3 2.5 %collective-permute-start.32 = (f32[2,2,8,512]{3,2,1,0:T(8,128)S(1)}, f32[2,2,8,512]{3,2,1,0:T(8,128)S(1)}, u32[]{:S(2)}, u32[]{:S(2)}) collective-permute-start(f32[2,2,8,512]{3,2,1,0:T(8,128)S(1)} %get-tuple-element.62), channel_id=1, source_target_pairs={{0,24},{2,26},{4,28},{6,30},{8,16},{10,18},{12,20},{14,22},{16,8},... | collective-permute-start | bytes 196616 | tf_op jit(solution)/shard_map/ppermute | solution.py:540
  136.9 1.9 %collective-permute-start.30 = (f32[2,2,8,512]{3,2,1,0:T(8,128)S(1)}, f32[2,2,8,512]{3,2,1,0:T(8,128)S(1)}, u32[]{:S(2)}, u32[]{:S(2)}) collective-permute-start(f32[2,2,8,512]{3,2,1,0:T(8,128)S(1)} %get-tuple-element.64), channel_id=1, source_target_pairs={{0,8},{2,10},{4,12},{6,14},{8,0},{10,2},{12,4},{14,6},{16,24},{18,... | collective-permute-start | bytes 196616 | tf_op jit(solution)/shard_map/ppermute | solution.py:540
  139.0 1.7 %collective-permute-done.32.refs_5_ = f32[2,2,8,512]{3,2,1,0:T(8,128)S(1)} collective-permute-done((f32[2,2,8,512]{3,2,1,0:T(8,128)S(1)}, f32[2,2,8,512]{3,2,1,0:T(8,128)S(1)}, u32[]{:S(2)}, u32[]{:S(2)}) %collective-permute-start.32) | collective-permute-done | bytes 65568 | tf_op jit(solution)/shard_map/ppermute | solution.py:540
  140.7 2.7 %collective-permute-done.31.refs_4_ = f32[2,2,8,512]{3,2,1,0:T(8,128)S(1)} collective-permute-done((f32[2,2,8,512]{3,2,1,0:T(8,128)S(1)}, f32[2,2,8,512]{3,2,1,0:T(8,128)S(1)}, u32[]{:S(2)}, u32[]{:S(2)}) %collective-permute-start.31) | collective-permute-done | bytes 65568 | tf_op jit(solution)/shard_map/ppermute | solution.py:540
  144.2 1.5 %closing.1 = (f32[2,4,4,2,512]{4,3,2,1,0:T(2,128)}, f32[2,4,4,2,512]{4,3,2,1,0:T(2,128)}) custom-call(s32[2]{0:T(128)S(1)} %pad_add_fusion.place_ref, f32[2,4,4]{2,1,0:T(4,128)S(1)} %copy-done.9, f32[1,512]{1,0:T(1,128)S(1)} %fusion.19.energy_ref, f32[2,2,8,512]{3,2,1,0:T(8,128)S(1)} %get-tuple-element.43.near_ref, f32[2,2,8,512]{3,2,1,0:T(8,128)S(1)} %advance_far.3.far_ref, ...), custom_call_target="tpu_custom_call" | custom-call | tf_op jit(solution)/shard_map/closing/pallas_call | solution.py:664
  (81 shorter events, 17.7 us)
Async XLA Ops:
  0.7 0.9 copy-start.6
  1.6 0.9 copy-start.7
  2.5 0.9 copy-start.8
  4.0 7.9 %collective-permute-start = (f32[3,2,2,8,512]{4,3,2,1,0:T(8,128)S(1)}, f32[3,2,2,8,512]{4,3,2,1,0:T(8,128)S(1)}, u32[]{:S(2)}, u32[]{:S(2)}) collective-permute-start(f32[3,2,2,8,512]{4,3,2,1,0:T(8,128)S(1)} %pack.3), channel_id=1, source_target_pairs={{0,1},{1,0},{2,3},{3,2},{4,5},{5,4},{6,7},{7,6},{8,9},{9,8},{10,11... | collective-permute-start | bytes 589832 | tf_op jit(solution)/shard_map/ppermute | solution.py:583
  12.0 1.0 copy-start.4
  12.9 0.7 copy-start.10
  14.9 1.6 %copy-start = (bf16[2,4,4,2,32,512]{5,4,3,2,1,0:T(8,128)(2,1)S(1)}, bf16[2,4,4,2,32,512]{5,4,3,2,1,0:T(8,128)(2,1)}, u32[]{:S(2)}) copy-start(bf16[2,4,4,2,32,512]{5,4,3,2,1,0:T(8,128)(2,1)} %lesser_ref.15) | copy-start | bytes 6291460
  16.5 1.6 %copy-start.2 = (bf16[2,4,4,2,32,512]{5,4,3,2,1,0:T(8,128)(2,1)S(1)}, bf16[2,4,4,2,32,512]{5,4,3,2,1,0:T(8,128)(2,1)}, u32[]{:S(2)}) copy-start(bf16[2,4,4,2,32,512]{5,4,3,2,1,0:T(8,128)(2,1)} %advanced_ref.11) | copy-start | bytes 6291460
  21.8 10.5 %collective-permute-start.8 = (f32[8,2,2,8,512]{4,3,2,1,0:T(8,128)S(1)}, f32[8,2,2,8,512]{4,3,2,1,0:T(8,128)S(1)}, u32[]{:S(2)}, u32[]{:S(2)}) collective-permute-start(f32[8,2,2,8,512]{4,3,2,1,0:T(8,128)S(1)} %get-tuple-element.33), channel_id=1, source_target_pairs={{0,2},{2,0},{4,6},{6,4},{8,10},{10,8},{12,14},{14,12},{16,18},{18,... | collective-permute-start | bytes 1572872 | tf_op jit(solution)/shard_map/ppermute | solution.py:528
  21.8 5.9 %collective-permute-start.1 = (f32[2,2,2,8,512]{4,3,2,1,0:T(8,128)S(1)}, f32[2,2,2,8,512]{4,3,2,1,0:T(8,128)S(1)}, u32[]{:S(2)}, u32[]{:S(2)}) collective-permute-start(f32[2,2,2,8,512]{4,3,2,1,0:T(8,128)S(1)} %get-tuple-element.26), channel_id=1, source_target_pairs={{0,1},{1,0},{2,3},{3,2},{4,5},{5,4},{6,7},{7,6},{8,9},{9,8},{10,11... | collective-permute-start | bytes 393224 | tf_op jit(solution)/shard_map/ppermute | solution.py:617
  31.4 2.8 %collective-permute-start.2 = (f32[8,2,2,8,512]{4,3,2,1,0:T(8,128)S(1)}, f32[8,2,2,8,512]{4,3,2,1,0:T(8,128)}, u32[]{:S(2)}, u32[]{:S(2)}) collective-permute-start(f32[8,2,2,8,512]{4,3,2,1,0:T(8,128)S(1)} %get-tuple-element.28), channel_id=1, source_target_pairs={{0,2},{2,0},{4,6},{6,4},{8,10},{10,8},{12,14},{14,12},{16,18},{18,... | collective-permute-start | bytes 1572872 | tf_op jit(solution)/shard_map/ppermute | solution.py:528
  32.3 24.2 %copy-start.9 = (f32[2,4,4]{2,1,0:T(4,128)S(1)}, f32[2,4,4]{2,1,0:T(4,128)}, u32[]{:S(2)}) copy-start(f32[2,4,4]{2,1,0:T(4,128)} %onsite_ref.9) | copy-start | bytes 388
  32.3 29.2 %copy-start.5 = (bf16[2,256,256]{2,1,0:T(8,128)(2,1)S(1)}, bf16[2,256,256]{2,1,0:T(8,128)(2,1)}, u32[]{:S(2)}) copy-start(bf16[2,256,256]{2,1,0:T(8,128)(2,1)} %constant.59.clone.table_ref) | copy-start | bytes 786436
  32.4 29.2 %copy-start.11 = (f32[8,2,128]{2,1,0:T(2,128)S(1)}, f32[8,2,128]{2,1,0:T(2,128)}, u32[]{:S(2)}) copy-start(f32[8,2,128]{2,1,0:T(2,128)} %constant.60.clone.twiddle_ref) | copy-start | bytes 24580
  32.4 9.2 %collective-permute-start.9 = (f32[4,2,2,8,512]{4,3,2,1,0:T(8,128)S(1)}, f32[4,2,2,8,512]{4,3,2,1,0:T(8,128)S(1)}, u32[]{:S(2)}, u32[]{:S(2)}) collective-permute-start(f32[4,2,2,8,512]{4,3,2,1,0:T(8,128)S(1)} %get-tuple-element.59), channel_id=1, source_target_pairs={{0,4},{2,6},{4,0},{6,2},{8,12},{10,14},{12,8},{14,10},{16,20},{18,... | collective-permute-start | bytes 786440 | tf_op jit(solution)/shard_map/ppermute | solution.py:532
  34.2 28.6 %copy-start.1 = (bf16[2,4,4,2,32,512]{5,4,3,2,1,0:T(8,128)(2,1)S(1)}, bf16[2,4,4,2,32,512]{5,4,3,2,1,0:T(8,128)(2,1)}, u32[]{:S(2)}) copy-start(bf16[2,4,4,2,32,512]{5,4,3,2,1,0:T(8,128)(2,1)} %lesser_ref.15) | copy-start | bytes 6291460
  34.2 28.6 %copy-start.3 = (bf16[2,4,4,2,32,512]{5,4,3,2,1,0:T(8,128)(2,1)S(1)}, bf16[2,4,4,2,32,512]{5,4,3,2,1,0:T(8,128)(2,1)}, u32[]{:S(2)}) copy-start(bf16[2,4,4,2,32,512]{5,4,3,2,1,0:T(8,128)(2,1)} %advanced_ref.11) | copy-start | bytes 6291460
  35.5 11.3 %collective-permute-start.3 = (f32[4,2,2,8,512]{4,3,2,1,0:T(8,128)S(1)}, f32[4,2,2,8,512]{4,3,2,1,0:T(8,128)S(1)}, u32[]{:S(2)}, u32[]{:S(2)}) collective-permute-start(f32[4,2,2,8,512]{4,3,2,1,0:T(8,128)S(1)} %get-tuple-element.61), channel_id=1, source_target_pairs={{0,4},{2,6},{4,0},{6,2},{8,12},{10,14},{12,8},{14,10},{16,20},{18,... | collective-permute-start | bytes 786440 | tf_op jit(solution)/shard_map/ppermute | solution.py:532
  41.7 9.7 %collective-permute-start.10 = (f32[2,2,2,8,512]{4,3,2,1,0:T(8,128)S(1)}, f32[2,2,2,8,512]{4,3,2,1,0:T(8,128)S(1)}, u32[]{:S(2)}, u32[]{:S(2)}) collective-permute-start(f32[2,2,2,8,512]{4,3,2,1,0:T(8,128)S(1)} %get-tuple-element.75), channel_id=1, source_target_pairs={{0,16},{2,18},{4,20},{6,22},{8,24},{10,26},{12,28},{14,30},{16,0},... | collective-permute-start | bytes 393224 | tf_op jit(solution)/shard_map/ppermute | solution.py:532
  46.8 6.5 %collective-permute-start.6 = (f32[2,2,8,512]{3,2,1,0:T(8,128)S(1)}, f32[2,2,8,512]{3,2,1,0:T(8,128)S(1)}, u32[]{:S(2)}, u32[]{:S(2)}) collective-permute-start(f32[2,2,8,512]{3,2,1,0:T(8,128)S(1)} %get-tuple-element.76), channel_id=1, source_target_pairs={{0,24},{2,26},{4,28},{6,30},{8,16},{10,18},{12,20},{14,22},{16,8},... | collective-permute-start | bytes 196616 | tf_op jit(solution)/shard_map/ppermute | solution.py:540
  50.7 5.5 %collective-permute-start.5 = (f32[2,2,8,512]{3,2,1,0:T(8,128)S(1)}, f32[2,2,8,512]{3,2,1,0:T(8,128)S(1)}, u32[]{:S(2)}, u32[]{:S(2)}) collective-permute-start(f32[2,2,8,512]{3,2,1,0:T(8,128)S(1)} %get-tuple-element.77), channel_id=1, source_target_pairs={{0,16},{2,18},{4,20},{6,22},{8,24},{10,26},{12,28},{14,30},{16,0},... | collective-permute-start | bytes 196616 | tf_op jit(solution)/shard_map/ppermute | solution.py:540
  50.7 5.8 %collective-permute-start.4 = (f32[2,2,8,512]{3,2,1,0:T(8,128)S(1)}, f32[2,2,8,512]{3,2,1,0:T(8,128)S(1)}, u32[]{:S(2)}, u32[]{:S(2)}) collective-permute-start(f32[2,2,8,512]{3,2,1,0:T(8,128)S(1)} %get-tuple-element.78), channel_id=1, source_target_pairs={{0,8},{2,10},{4,12},{6,14},{8,0},{10,2},{12,4},{14,6},{16,24},{18,... | collective-permute-start | bytes 196616 | tf_op jit(solution)/shard_map/ppermute | solution.py:540
  51.4 7.7 %collective-permute-start.11 = (f32[1,2,2,8,512]{4,3,2,1,0:T(8,128)S(1)}, f32[1,2,2,8,512]{4,3,2,1,0:T(8,128)S(1)}, u32[]{:S(2)}, u32[]{:S(2)}) collective-permute-start(f32[1,2,2,8,512]{4,3,2,1,0:T(8,128)S(1)} %get-tuple-element.84), channel_id=1, source_target_pairs={{0,8},{2,10},{4,12},{6,14},{8,0},{10,2},{12,4},{14,6},{16,24},{18,... | collective-permute-start | bytes 196616 | tf_op jit(solution)/shard_map/ppermute | solution.py:532
  57.2 4.3 %collective-permute-start.7 = (f32[2,2,8,512]{3,2,1,0:T(8,128)S(1)}, f32[2,2,8,512]{3,2,1,0:T(8,128)S(1)}, u32[]{:S(2)}, u32[]{:S(2)}) collective-permute-start(f32[2,2,8,512]{3,2,1,0:T(8,128)S(1)} %get-tuple-element.29.far_ref), channel_id=1, source_target_pairs={{0,1},{1,0},{2,3},{3,2},{4,5},{5,4},{6,7},{7,6},{8,9},{9,8},{10,11... | collective-permute-start | bytes 196616 | tf_op jit(solution)/shard_map/ppermute | solution.py:648
  66.5 9.8 %collective-permute-start.19 = (f32[8,2,2,8,512]{4,3,2,1,0:T(8,128)S(1)}, f32[8,2,2,8,512]{4,3,2,1,0:T(8,128)S(1)}, u32[]{:S(2)}, u32[]{:S(2)}) collective-permute-start(f32[8,2,2,8,512]{4,3,2,1,0:T(8,128)S(1)} %get-tuple-element.41), channel_id=1, source_target_pairs={{0,2},{2,0},{4,6},{6,4},{8,10},{10,8},{12,14},{14,12},{16,18},{18,... | collective-permute-start | bytes 1572872 | tf_op jit(solution)/shard_map/ppermute | solution.py:528
  66.6 5.9 %collective-permute-start.12 = (f32[2,2,2,8,512]{4,3,2,1,0:T(8,128)S(1)}, f32[2,2,2,8,512]{4,3,2,1,0:T(8,128)S(1)}, u32[]{:S(2)}, u32[]{:S(2)}) collective-permute-start(f32[2,2,2,8,512]{4,3,2,1,0:T(8,128)S(1)} %get-tuple-element.35), channel_id=1, source_target_pairs={{0,1},{1,0},{2,3},{3,2},{4,5},{5,4},{6,7},{7,6},{8,9},{9,8},{10,11... | collective-permute-start | bytes 393224 | tf_op jit(solution)/shard_map/ppermute | solution.py:617
  76.1 2.0 %collective-permute-start.13 = (f32[8,2,2,8,512]{4,3,2,1,0:T(8,128)S(1)}, f32[8,2,2,8,512]{4,3,2,1,0:T(8,128)S(1)}, u32[]{:S(2)}, u32[]{:S(2)}) collective-permute-start(f32[8,2,2,8,512]{4,3,2,1,0:T(8,128)S(1)} %get-tuple-element.37), channel_id=1, source_target_pairs={{0,2},{2,0},{4,6},{6,4},{8,10},{10,8},{12,14},{14,12},{16,18},{18,... | collective-permute-start | bytes 1572872 | tf_op jit(solution)/shard_map/ppermute | solution.py:528
  76.3 9.2 %collective-permute-start.20 = (f32[4,2,2,8,512]{4,3,2,1,0:T(8,128)S(1)}, f32[4,2,2,8,512]{4,3,2,1,0:T(8,128)S(1)}, u32[]{:S(2)}, u32[]{:S(2)}) collective-permute-start(f32[4,2,2,8,512]{4,3,2,1,0:T(8,128)S(1)} %get-tuple-element.55), channel_id=1, source_target_pairs={{0,4},{2,6},{4,0},{6,2},{8,12},{10,14},{12,8},{14,10},{16,20},{18,... | collective-permute-start | bytes 786440 | tf_op jit(solution)/shard_map/ppermute | solution.py:532
  78.3 12.5 %collective-permute-start.14 = (f32[4,2,2,8,512]{4,3,2,1,0:T(8,128)S(1)}, f32[4,2,2,8,512]{4,3,2,1,0:T(8,128)S(1)}, u32[]{:S(2)}, u32[]{:S(2)}) collective-permute-start(f32[4,2,2,8,512]{4,3,2,1,0:T(8,128)S(1)} %get-tuple-element.57), channel_id=1, source_target_pairs={{0,4},{2,6},{4,0},{6,2},{8,12},{10,14},{12,8},{14,10},{16,20},{18,... | collective-permute-start | bytes 786440 | tf_op jit(solution)/shard_map/ppermute | solution.py:532
  85.6 9.6 %collective-permute-start.21 = (f32[2,2,2,8,512]{4,3,2,1,0:T(8,128)S(1)}, f32[2,2,2,8,512]{4,3,2,1,0:T(8,128)S(1)}, u32[]{:S(2)}, u32[]{:S(2)}) collective-permute-start(f32[2,2,2,8,512]{4,3,2,1,0:T(8,128)S(1)} %get-tuple-element.69), channel_id=1, source_target_pairs={{0,16},{2,18},{4,20},{6,22},{8,24},{10,26},{12,28},{14,30},{16,0},... | collective-permute-start | bytes 393224 | tf_op jit(solution)/shard_map/ppermute | solution.py:532
  90.8 6.4 %collective-permute-start.17 = (f32[2,2,8,512]{3,2,1,0:T(8,128)S(1)}, f32[2,2,8,512]{3,2,1,0:T(8,128)S(1)}, u32[]{:S(2)}, u32[]{:S(2)}) collective-permute-start(f32[2,2,8,512]{3,2,1,0:T(8,128)S(1)} %get-tuple-element.70), channel_id=1, source_target_pairs={{0,24},{2,26},{4,28},{6,30},{8,16},{10,18},{12,20},{14,22},{16,8},... | collective-permute-start | bytes 196616 | tf_op jit(solution)/shard_map/ppermute | solution.py:540
  94.0 5.9 %collective-permute-start.16 = (f32[2,2,8,512]{3,2,1,0:T(8,128)S(1)}, f32[2,2,8,512]{3,2,1,0:T(8,128)S(1)}, u32[]{:S(2)}, u32[]{:S(2)}) collective-permute-start(f32[2,2,8,512]{3,2,1,0:T(8,128)S(1)} %get-tuple-element.71), channel_id=1, source_target_pairs={{0,16},{2,18},{4,20},{6,22},{8,24},{10,26},{12,28},{14,30},{16,0},... | collective-permute-start | bytes 196616 | tf_op jit(solution)/shard_map/ppermute | solution.py:540
  94.0 6.2 %collective-permute-start.15 = (f32[2,2,8,512]{3,2,1,0:T(8,128)S(1)}, f32[2,2,8,512]{3,2,1,0:T(8,128)S(1)}, u32[]{:S(2)}, u32[]{:S(2)}) collective-permute-start(f32[2,2,8,512]{3,2,1,0:T(8,128)S(1)} %get-tuple-element.72), channel_id=1, source_target_pairs={{0,8},{2,10},{4,12},{6,14},{8,0},{10,2},{12,4},{14,6},{16,24},{18,... | collective-permute-start | bytes 196616 | tf_op jit(solution)/shard_map/ppermute | solution.py:540
  95.3 7.2 %collective-permute-start.22 = (f32[1,2,2,8,512]{4,3,2,1,0:T(8,128)S(1)}, f32[1,2,2,8,512]{4,3,2,1,0:T(8,128)S(1)}, u32[]{:S(2)}, u32[]{:S(2)}) collective-permute-start(f32[1,2,2,8,512]{4,3,2,1,0:T(8,128)S(1)} %get-tuple-element.82), channel_id=1, source_target_pairs={{0,8},{2,10},{4,12},{6,14},{8,0},{10,2},{12,4},{14,6},{16,24},{18,... | collective-permute-start | bytes 196616 | tf_op jit(solution)/shard_map/ppermute | solution.py:532
  100.9 4.3 %collective-permute-start.18 = (f32[2,2,8,512]{3,2,1,0:T(8,128)S(1)}, f32[2,2,8,512]{3,2,1,0:T(8,128)S(1)}, u32[]{:S(2)}, u32[]{:S(2)}) collective-permute-start(f32[2,2,8,512]{3,2,1,0:T(8,128)S(1)} %advance_far.3.far_ref), channel_id=1, source_target_pairs={{0,1},{1,0},{2,3},{3,2},{4,5},{5,4},{6,7},{7,6},{8,9},{9,8},{10,11... | collective-permute-start | bytes 196616 | tf_op jit(solution)/shard_map/ppermute | solution.py:648
  110.1 9.7 %collective-permute-start.23 = (f32[8,2,2,8,512]{4,3,2,1,0:T(8,128)S(1)}, f32[8,2,2,8,512]{4,3,2,1,0:T(8,128)S(1)}, u32[]{:S(2)}, u32[]{:S(2)}) collective-permute-start(f32[8,2,2,8,512]{4,3,2,1,0:T(8,128)S(1)} %get-tuple-element.46), channel_id=1, source_target_pairs={{0,2},{2,0},{4,6},{6,4},{8,10},{10,8},{12,14},{14,12},{16,18},{18,... | collective-permute-start | bytes 1572872 | tf_op jit(solution)/shard_map/ppermute | solution.py:528
  110.2 5.9 %collective-permute-start.27 = (f32[2,2,2,8,512]{4,3,2,1,0:T(8,128)S(1)}, f32[2,2,2,8,512]{4,3,2,1,0:T(8,128)S(1)}, u32[]{:S(2)}, u32[]{:S(2)}) collective-permute-start(f32[2,2,2,8,512]{4,3,2,1,0:T(8,128)S(1)} %get-tuple-element.47), channel_id=1, source_target_pairs={{0,1},{1,0},{2,3},{3,2},{4,5},{5,4},{6,7},{7,6},{8,9},{9,8},{10,11... | collective-permute-start | bytes 393224 | tf_op jit(solution)/shard_map/ppermute | solution.py:617
  119.7 2.0 %collective-permute-start.28 = (f32[8,2,2,8,512]{4,3,2,1,0:T(8,128)S(1)}, f32[8,2,2,8,512]{4,3,2,1,0:T(8,128)S(1)}, u32[]{:S(2)}, u32[]{:S(2)}) collective-permute-start(f32[8,2,2,8,512]{4,3,2,1,0:T(8,128)S(1)} %get-tuple-element.49), channel_id=1, source_target_pairs={{0,2},{2,0},{4,6},{6,4},{8,10},{10,8},{12,14},{14,12},{16,18},{18,... | collective-permute-start | bytes 1572872 | tf_op jit(solution)/shard_map/ppermute | solution.py:528
  119.9 9.2 %collective-permute-start.24 = (f32[4,2,2,8,512]{4,3,2,1,0:T(8,128)S(1)}, f32[4,2,2,8,512]{4,3,2,1,0:T(8,128)S(1)}, u32[]{:S(2)}, u32[]{:S(2)}) collective-permute-start(f32[4,2,2,8,512]{4,3,2,1,0:T(8,128)S(1)} %get-tuple-element.53), channel_id=1, source_target_pairs={{0,4},{2,6},{4,0},{6,2},{8,12},{10,14},{12,8},{14,10},{16,20},{18,... | collective-permute-start | bytes 786440 | tf_op jit(solution)/shard_map/ppermute | solution.py:532
  121.8 12.5 %collective-permute-start.29 = (f32[4,2,2,8,512]{4,3,2,1,0:T(8,128)S(1)}, f32[4,2,2,8,512]{4,3,2,1,0:T(8,128)S(1)}, u32[]{:S(2)}, u32[]{:S(2)}) collective-permute-start(f32[4,2,2,8,512]{4,3,2,1,0:T(8,128)S(1)} %get-tuple-element.51), channel_id=1, source_target_pairs={{0,4},{2,6},{4,0},{6,2},{8,12},{10,14},{12,8},{14,10},{16,20},{18,... | collective-permute-start | bytes 786440 | tf_op jit(solution)/shard_map/ppermute | solution.py:532
  129.2 9.6 %collective-permute-start.25 = (f32[2,2,2,8,512]{4,3,2,1,0:T(8,128)S(1)}, f32[2,2,2,8,512]{4,3,2,1,0:T(8,128)S(1)}, u32[]{:S(2)}, u32[]{:S(2)}) collective-permute-start(f32[2,2,2,8,512]{4,3,2,1,0:T(8,128)S(1)} %get-tuple-element.67), channel_id=1, source_target_pairs={{0,16},{2,18},{4,20},{6,22},{8,24},{10,26},{12,28},{14,30},{16,0},... | collective-permute-start | bytes 393224 | tf_op jit(solution)/shard_map/ppermute | solution.py:532
  134.3 6.3 %collective-permute-start.32 = (f32[2,2,8,512]{3,2,1,0:T(8,128)S(1)}, f32[2,2,8,512]{3,2,1,0:T(8,128)S(1)}, u32[]{:S(2)}, u32[]{:S(2)}) collective-permute-start(f32[2,2,8,512]{3,2,1,0:T(8,128)S(1)} %get-tuple-element.62), channel_id=1, source_target_pairs={{0,24},{2,26},{4,28},{6,30},{8,16},{10,18},{12,20},{14,22},{16,8},... | collective-permute-start | bytes 196616 | tf_op jit(solution)/shard_map/ppermute | solution.py:540
  136.8 6.5 %collective-permute-start.31 = (f32[2,2,8,512]{3,2,1,0:T(8,128)S(1)}, f32[2,2,8,512]{3,2,1,0:T(8,128)S(1)}, u32[]{:S(2)}, u32[]{:S(2)}) collective-permute-start(f32[2,2,8,512]{3,2,1,0:T(8,128)S(1)} %get-tuple-element.63), channel_id=1, source_target_pairs={{0,16},{2,18},{4,20},{6,22},{8,24},{10,26},{12,28},{14,30},{16,0},... | collective-permute-start | bytes 196616 | tf_op jit(solution)/shard_map/ppermute | solution.py:540
  136.9 6.5 %collective-permute-start.30 = (f32[2,2,8,512]{3,2,1,0:T(8,128)S(1)}, f32[2,2,8,512]{3,2,1,0:T(8,128)S(1)}, u32[]{:S(2)}, u32[]{:S(2)}) collective-permute-start(f32[2,2,8,512]{3,2,1,0:T(8,128)S(1)} %get-tuple-element.64), channel_id=1, source_target_pairs={{0,8},{2,10},{4,12},{6,14},{8,0},{10,2},{12,4},{14,6},{16,24},{18,... | collective-permute-start | bytes 196616 | tf_op jit(solution)/shard_map/ppermute | solution.py:540
  138.8 5.3 %collective-permute-start.26 = (f32[1,2,2,8,512]{4,3,2,1,0:T(8,128)S(1)}, f32[1,2,2,8,512]{4,3,2,1,0:T(8,128)S(1)}, u32[]{:S(2)}, u32[]{:S(2)}) collective-permute-start(f32[1,2,2,8,512]{4,3,2,1,0:T(8,128)S(1)} %get-tuple-element.80), channel_id=1, source_target_pairs={{0,8},{2,10},{4,12},{6,14},{8,0},{10,2},{12,4},{14,6},{16,24},{18,... | collective-permute-start | bytes 196616 | tf_op jit(solution)/shard_map/ppermute | solution.py:532
where the time goes:
time: 146 us
  waiting for transfers between devices  58.3 us (40%)
  starting transfers between devices  43.3 us (30%)
  Pallas kernels  29.7 us (20%)
  local copies, waits for them, and re-layouts  8.98 us (6%)
  other arithmetic  2.99 us (2%)
  between operations  2.34 us (2%)
    ppermute x12, waiting for transfers between devices, halved_sum(): arriving = lax.ppermute(outgoing, 'ta', flip(1 << bit, ta_count))  26.6 us
    pallas_call x6, Pallas kernels, collide(): pl.pallas_call(functools.partial(collide_kernel, order), out_shape=(float...  22 us
    ppermute x12, starting transfers between devices, halved_sum(): arriving = lax.ppermute(outgoing, 'ta', flip(1 << bit, ta_count))  17.9 us
    ppermute x9, starting transfers between devices, halved_sum(): lax.ppermute(pieces[place], 'ta', flip(place << shift, ta_count))  13.4 us
    ppermute x3, waiting for transfers between devices, collisions(): sigma_far = lax.ppermute(sigma_send, 'ka', flip(1, ka_count))  12.5 us
    ppermute x9, waiting for transfers between devices, halved_sum(): lax.ppermute(pieces[place], 'ta', flip(place << shift, ta_count))  12.2 us
    unnamed x24, local copies, waits for them, and re-layouts  7.57 us
    ppermute x2, waiting for transfers between devices, fast(): arrived = lax.ppermute(far_result[-1], 'ka', flip(1, ka_count))  5.28 us
  transfers between devices with their start and end apart: 33, of which 23 were waited for; matrix products, arithmetic and copies ran while one was open for 3% of the time, Pallas kernels for 9%

commit v1 on v0

--- a/solution.py
+++ b/solution.py
@@ -282,21 +282,49 @@
                     send_ref[field, plane, half, :, where_to] = jnp.where(ka == 0, far, near)
 
 
-def pack_kernel(own_side, place_ref, lesser_ref, retarded_ref, green_ref, packed_ref):
-    halves, inner, local_rows = packed_ref.shape[2], lesser_ref.shape[2], lesser_ref.shape[3]
-    side = place_ref[1] if own_side else 1 - place_ref[1]
-    for field, ref in enumerate((lesser_ref, retarded_ref, green_ref)):
-        for plane in range(2):
-            for half in range(halves):
-                for column in range(inner):
-                    begin = column * local_rows
-                    packed_ref[field, plane, half, begin : begin + local_rows, :] = ref[
-                        plane, side * halves + half, column
-                    ]
+def pack_kernel(lesser_ref, retarded_ref, green_ref, near_ref, far_ref):
+    ka = lax.axis_index("ka")
+    halves, inner, local_rows = near_ref.shape[2], lesser_ref.shape[2], lesser_ref.shape[3]
+    for side, packed_ref in ((1 - ka, far_ref), (ka, near_ref)):
+        for field, ref in enumerate((lesser_ref, retarded_ref, green_ref)):
+            for plane in range(2):
+                for half in range(halves):
+                    for column in range(inner):
+                        begin = column * local_rows
+                        packed_ref[field, plane, half, begin : begin + local_rows, :] = ref[
+                            plane, side * halves + half, column
+                        ]
+
+
+def stage_kernel(
+    blocks_ref, onsite_ref, energies_ref, table_in_ref, twiddle_in_ref,
+    causal_ref, energy_ref, onsite_out_ref, table_ref, twiddle_ref
+):
+    ta, ka = lax.axis_index("ta"), lax.axis_index("ka")
+    table_ref[...] = table_in_ref[...]
+    twiddle_ref[...] = twiddle_in_ref[...]
+    local_rows, all_times, k_local = causal_ref.shape[0], causal_ref.shape[1], energy_ref.shape[1]
+    energy_ref[...] = energies_ref[:, pl.ds(pl.multiple_of(ka * k_local, LANES), k_local)]
+    orbitals = onsite_ref.shape[1]
+    halves = orbitals // 2
+    for row in range(orbitals):
+        for column in range(orbitals):
+            for plane in range(2):
+                value = onsite_ref[
+                    plane, (row + ka * halves) % orbitals, (column + ka * halves) % orbitals
+                ]
+                place = (plane * orbitals + row) * orbitals + column
+                onsite_out_ref[place : place + 1, :] = jnp.full((1, LANES), value)
+    for stored in range(local_rows):
+        row_time = blocks_ref[ta] * local_rows + stored
+        for column in range(all_times):
+            column_time = blocks_ref[column // local_rows] * local_rows + column % local_rows
+            seen = jnp.where(row_time <= column_time, jnp.float32(1.0), jnp.float32(0.0))
+            causal_ref[stored, column : column + 1, :] = jnp.full((1, LANES), seen)
 
 
 def opening_kernel(
-    place_ref, own_ref, other_ref, table_ref, twiddle_ref, screens_ref, sigma_ref, send_ref
+    own_ref, other_ref, table_ref, twiddle_ref, screens_ref, sigma_ref, send_ref
 ):
     halves, k_local = own_ref.shape[2], own_ref.shape[4]
     local_tiles = k_local // LANES
@@ -311,25 +339,27 @@
     screens_ref[0] = spaces[0]
     screens_ref[1] = spaces[1]
     emit_sigma(
-        place_ref[1], spaces[2], screens_ref, table_ref, twiddle_ref, sigma_ref, send_ref
-    )
-
-
-def rate_pieces(own_side, ka, half, tile, onsite_ref, energy_ref, near_ref, far_ref, sums_refs):
+        lax.axis_index("ka"), spaces[2], screens_ref, table_ref, twiddle_ref, sigma_ref, send_ref
+    )
+
+
+def rate_pieces(own_side, half, tile, onsite_ref, energy_ref, near_ref, far_ref, sums_refs):
     halves = near_ref.shape[1]
+    orbitals = 2 * halves
     lanes = pl.ds(tile * LANES, LANES)
-    mine = ka if own_side else 1 - ka
-    row = mine * halves + half
+    row = half if own_side else halves + half
     here = near_ref if own_side else far_ref
     real_part = functools.reduce(jnp.add, [ref[0, half, :, lanes] for ref in sums_refs])
     imag_part = functools.reduce(jnp.add, [ref[1, half, :, lanes] for ref in sums_refs])
     energy = energy_ref[0:1, lanes]
     real_part = real_part + energy * here[0, half, :, lanes]
     imag_part = imag_part + energy * here[1, half, :, lanes]
-    for side, ref in ((ka, near_ref), (1 - ka, far_ref)):
+    for side, ref in enumerate((near_ref, far_ref)):
         for column in range(halves):
-            coupling_real = onsite_ref[0, row, side * halves + column]
-            coupling_imag = onsite_ref[1, row, side * halves + column]
+            place = row * orbitals + side * halves + column
+            coupling_real = onsite_ref[place : place + 1, :]
+            place += orbitals * orbitals
+            coupling_imag = onsite_ref[place : place + 1, :]
             value_real, value_imag = ref[0, column, :, lanes], ref[1, column, :, lanes]
             real_part = real_part + coupling_real * value_real - coupling_imag * value_imag
             imag_part = imag_part + coupling_real * value_imag + coupling_imag * value_real
@@ -337,16 +367,15 @@
 
 
 def advance_far_kernel(
-    is_first, sums_count, place_ref, onsite_ref, energy_ref, near_ref, far_ref, green_ref, *refs
+    is_first, sums_count, onsite_ref, energy_ref, near_ref, far_ref, green_ref, *refs
 ):
-    ka = place_ref[1]
     sums_refs, (first_ref, estimate_ref) = refs[:sums_count], refs[sums_count:]
     halves, k_local = far_ref.shape[1], far_ref.shape[3]
     for half in range(halves):
         for tile in range(k_local // LANES):
             lanes = pl.ds(tile * LANES, LANES)
             rates = rate_pieces(
-                False, ka, half, tile, onsite_ref, energy_ref, near_ref, far_ref, sums_refs
+                False, half, tile, onsite_ref, energy_ref, near_ref, far_ref, sums_refs
             )
             for plane in range(2):
                 start = green_ref[plane, half, :, lanes]
@@ -360,10 +389,10 @@
 
 
 def advance_near_kernel(
-    is_first, sums_count, place_ref, onsite_ref, energy_ref, near_ref, far_ref, green_ref,
+    is_first, sums_count, onsite_ref, energy_ref, near_ref, far_ref, green_ref,
     arrived_ref, screens_ref, table_ref, twiddle_ref, *refs
 ):
-    ka = place_ref[1]
+    ka = lax.axis_index("ka")
     sums_refs = refs[:sums_count]
     first_ref, estimate_ref, sigma_ref, send_ref = refs[sums_count:]
     halves, k_local = near_ref.shape[1], near_ref.shape[3]
@@ -374,7 +403,7 @@
         for tile in range(local_tiles):
             lanes = pl.ds(tile * LANES, LANES)
             rates = rate_pieces(
-                True, ka, half, tile, onsite_ref, energy_ref, near_ref, far_ref, sums_refs
+                True, half, tile, onsite_ref, energy_ref, near_ref, far_ref, sums_refs
             )
             pair = []
             for plane in range(2):
@@ -396,10 +425,10 @@
 
 
 def closing_kernel(
-    near_count, far_count, place_ref, onsite_ref, energy_ref, near_ref, far_ref, green_near_ref,
+    near_count, far_count, onsite_ref, energy_ref, near_ref, far_ref, green_near_ref,
     green_far_ref, first_near_ref, first_far_ref, *refs
 ):
-    ka = place_ref[1]
+    ka = lax.axis_index("ka")
     near_sums, far_sums = refs[:near_count], refs[near_count : near_count + far_count]
     next_ref, latest_ref = refs[near_count + far_count :]
     halves, k_local = near_ref.shape[1], near_ref.shape[3]
@@ -412,7 +441,7 @@
             for tile in range(k_local // LANES):
                 lanes = pl.ds(tile * LANES, LANES)
                 rates = rate_pieces(
-                    own_side, ka, half, tile, onsite_ref, energy_ref, near_ref, far_ref, sums_refs
+                    own_side, half, tile, onsite_ref, energy_ref, near_ref, far_ref, sums_refs
                 )
                 for plane in range(2):
                     value = green_ref[plane, half, :, lanes] + 0.5 * time_step * (
@@ -445,68 +474,63 @@
 
 
 def collide_kernel(
-    order, place_ref, sigma_ref, causal_ref, lesser_ref, advanced_ref, keep_ref, send_ref
+    order, sigma_ref, causal_ref, lesser_ref, advanced_ref, keep_ref, send_ref
 ):
     halves, k_local = sigma_ref.shape[2], sigma_ref.shape[4]
     orbitals, local_rows, times = lesser_ref.shape[1], lesser_ref.shape[3], lesser_ref.shape[4]
-    rows = 2 * SUBLANES
+    rows = SUBLANES
     time_steps = times // rows
-    me = place_ref[0]
+    me = lax.axis_index("ta")
 
     def gather(total, value):
         return value if total is None else total + value
 
     def step(counter, carried):
-        time_step_index = counter % time_steps
-        first_row = pl.multiple_of(time_step_index * rows, rows)
+        tile = counter % time_steps
+        here = pl.ds(pl.multiple_of(tile * rows, rows), rows)
         lanes = pl.ds(pl.multiple_of(counter // time_steps * LANES, LANES), LANES)
-        here = pl.ds(first_row, rows)
-        sums_real = [[None] * orbitals for _ in range(halves)]
-        sums_imag = [[None] * orbitals for _ in range(halves)]
+        sums = [[[None] * 3 for _ in range(orbitals)] for _ in range(halves)]
         for field, slab_ref in ((1, lesser_ref), (0, advanced_ref)):
             for stored in range(local_rows):
                 for inner in range(orbitals):
                     row = inner * local_rows + stored
-                    sigma_real, sigma_imag = [], []
+                    sigmas = []
                     for half in range(halves):
-                        for plane, found in ((0, sigma_real), (1, sigma_imag)):
-                            value = sigma_ref[field, plane, half, row : row + 1, lanes]
-                            value = jnp.broadcast_to(value, (rows, LANES))
-                            if field == 0:
-                                value = value * causal_ref[stored, here]
-                            found.append(value)
+                        triple = [
+                            jnp.broadcast_to(
+                                sigma_ref[field, plane, half, row : row + 1, lanes], (rows, LANES)
+                            )
+                            for plane in range(2)
+                        ]
+                        if field == 0:
+                            triple = [value * causal_ref[stored, here] for value in triple]
+                        sigmas.append(triple + [triple[0] + triple[1]])
                     for outer in range(orbitals):
-                        slab_real = slab_ref[0, inner, outer, stored, here, lanes]
-                        slab_imag = slab_ref[1, inner, outer, stored, here, lanes]
-                        slab_real = slab_real.astype(jnp.float32)
-                        slab_imag = slab_imag.astype(jnp.float32)
+                        slabs = [
+                            slab_ref[plane, inner, outer, stored, here, lanes].astype(jnp.float32)
+                            for plane in range(2)
+                        ]
+                        slabs.append(slabs[0] + slabs[1])
                         for half in range(halves):
-                            sums_real[half][outer] = (
-                                gather(sums_real[half][outer], sigma_real[half] * slab_real)
-                                - sigma_imag[half] * slab_imag
-                            )
-                            sums_imag[half][outer] = (
-                                gather(sums_imag[half][outer], sigma_real[half] * slab_imag)
-                                + sigma_imag[half] * slab_real
-                            )
+                            totals = sums[half][outer]
+                            for term in range(3):
+                                totals[term] = gather(
+                                    totals[term], sigmas[half][term] * slabs[term]
+                                )
         even = (me & 1) == 0
-        for piece in range(rows // SUBLANES):
-            tile = time_step_index * (rows // SUBLANES) + piece
-            begin = piece * SUBLANES
-            for half in range(halves):
-                for plane, sums in ((0, sums_real), (1, sums_imag)):
-                    owners = swap_rows(
-                        [sums[half][outer][begin : begin + SUBLANES] for outer in range(orbitals)],
-                        local_rows,
-                    )
-                    for pair in range(0, orbitals, 2):
-                        relative = (tile * orbitals + pair) ^ me
-                        where_to = 0
-                        for bit in order[1:]:
-                            where_to = where_to * 2 + ((relative >> bit) & 1)
-                        first, second = owners[pair], owners[pair + 1]
-                        keep_ref[where_to, plane, half, :, lanes] = jnp.where(even, first, second)
-                        send_ref[where_to, plane, half, :, lanes] = jnp.where(even, second, first)
+        for half in range(halves):
+            real_parts = [totals[0] - totals[1] for totals in sums[half]]
+            imag_parts = [totals[2] - (totals[0] + totals[1]) for totals in sums[half]]
+            for plane, parts in ((0, real_parts), (1, imag_parts)):
+                owners = swap_rows(parts, local_rows)
+                for pair in range(0, orbitals, 2):
+                    relative = (tile * orbitals + pair) ^ me
+                    where_to = 0
+                    for bit in order[1:]:
+                        where_to = where_to * 2 + ((relative >> bit) & 1)
+                    first, second = owners[pair], owners[pair + 1]
+                    keep_ref[where_to, plane, half, :, lanes] = jnp.where(even, first, second)
+                    send_ref[where_to, plane, half, :, lanes] = jnp.where(even, second, first)
         return carried
 
     lax.fori_loop(0, time_steps * (k_local // LANES), step, 0)
@@ -550,18 +574,10 @@
     all_times = local_rows * ta_count
     halves = orbitals // 2
     tiles = k_local * ka_count // LANES
-    ta_index, ka_index = lax.axis_index("ta"), lax.axis_index("ka")
-    place = jnp.stack([ta_index, ka_index]).astype(jnp.int32)
     table, twiddle = fourier_tables(tiles)
-    my_block = lax.dynamic_slice_in_dim(block_table, ta_index, 1)[0]
-    row_times = my_block * local_rows + jnp.arange(local_rows, dtype=jnp.int32)
-    col_times = jnp.repeat(block_table, local_rows) * local_rows + jnp.tile(
-        jnp.arange(local_rows, dtype=jnp.int32), ta_count
-    )
-    causal = (row_times[:, None] <= col_times[None, :]).astype(jnp.float32)
-    causal = jnp.broadcast_to(causal[:, :, None], (local_rows, all_times, LANES))
-    momenta = ka_index * k_local + jnp.arange(k_local, dtype=jnp.int32)
-    energy = dispersion(slab_start, all_times, momenta // KS, momenta % KS)[None]
+    momenta = jnp.arange(KS * KS, dtype=jnp.int32)
+    start = lax.optimization_barrier(jnp.broadcast_to(slab_start, momenta.shape))
+    energies = dispersion(start[None], all_times, momenta // KS, momenta % KS)[None]
 
     chunk = (2, halves, SUBLANES, k_local)
     scalar = whole(pltpu.SMEM)
@@ -569,40 +585,57 @@
     sigma_shape = float_like(2, *chunk)
     small = pltpu.CompilerParams(vmem_limit_bytes=8 * 1024 * 1024)
 
-    def packed(own_side):
-        return pl.pallas_call(
-            functools.partial(pack_kernel, own_side),
-            out_shape=float_like(3, *chunk),
-            in_specs=[scalar] + [whole()] * 3,
-            out_specs=whole(),
-            compiler_params=small,
-            name="pack",
-        )(place, screen_lesser, screen_retarded, green_row)
-
-    far_fields = packed(False)
+    hint = pl.CostEstimate(
+        flops=8 * lesser_slab.size, bytes_accessed=8 * lesser_slab.size, transcendentals=0
+    )
+    near_fields, far_fields = pl.pallas_call(
+        pack_kernel,
+        out_shape=(float_like(3, *chunk),) * 2,
+        in_specs=[whole()] * 3,
+        out_specs=(whole(),) * 2,
+        compiler_params=small,
+        cost_estimate=hint,
+        name="pack",
+    )(screen_lesser, screen_retarded, green_row)
     arrived_fields = lax.ppermute(far_fields, "ka", flip(1, ka_count))
-    near_fields = packed(True)
+    causal, energy, onsite, table, twiddle = pl.pallas_call(
+        stage_kernel,
+        out_shape=(
+            float_like(local_rows, all_times, LANES),
+            float_like(1, k_local),
+            float_like(2 * orbitals * orbitals, LANES),
+            jax.ShapeDtypeStruct(table.shape, table.dtype),
+            jax.ShapeDtypeStruct(twiddle.shape, twiddle.dtype),
+        ),
+        in_specs=[scalar] * 2 + [whole()] * 3,
+        out_specs=(whole(),) * 5,
+        compiler_params=small,
+        cost_estimate=hint,
+        name="stage",
+    )(block_table, onsite, energies, table, twiddle)
     green_near, green_far = near_fields[2], far_fields[2]
 
     screens, sigma_near, sigma_send = pl.pallas_call(
         opening_kernel,
         out_shape=(float_like(2, space_rows, 2 * LANES), sigma_shape, sigma_shape),
-        in_specs=[scalar] + [whole()] * 4,
+        in_specs=[whole()] * 4,
         out_specs=(whole(),) * 3,
         compiler_params=small,
+        cost_estimate=hint,
         name="opening",
-    )(place, near_fields, arrived_fields, table, twiddle)
+    )(near_fields, arrived_fields, table, twiddle)
 
     bits = ta_count.bit_length() - 1
     owner_bits = orbitals.bit_length() - 1
-    order = list(range(owner_bits)) + list(range(owner_bits, bits))[::-1]
+    near_order = list(range(bits))
+    far_order = list(range(owner_bits)) + list(range(owner_bits, bits))[::-1]
     direct_bits = bits - owner_bits
 
-    def collide(sigma):
+    def collide(sigma, order):
         return pl.pallas_call(
             functools.partial(collide_kernel, order),
             out_shape=(float_like(ta_count // 2, *chunk),) * 2,
-            in_specs=[scalar] + [whole()] * 4,
+            in_specs=[whole()] * 4,
             out_specs=(whole(),) * 2,
             compiler_params=small,
             cost_estimate=pl.CostEstimate(
@@ -611,23 +644,23 @@
                 transcendentals=0,
             ),
             name="collide",
-        )(place, sigma, causal, lesser_slab, advanced_slab)
+        )(sigma, causal, lesser_slab, advanced_slab)
 
     def collisions(sigma_near, sigma_send):
         sigma_far = lax.ppermute(sigma_send, "ka", flip(1, ka_count))
-        near = collide(sigma_near)
-        far = collide(sigma_far)
-        near_sums = halved_sum(*near, order, 0, ta_count)
-        far_sums = halved_sum(*far, order, direct_bits, ta_count)
+        near = collide(sigma_near, near_order)
+        far = collide(sigma_far, far_order)
+        near_sums = halved_sum(*near, near_order, 0, ta_count)
+        far_sums = halved_sum(*far, far_order, direct_bits, ta_count)
         return near_sums, far_sums
 
     estimate_near, estimate_far = green_near, green_far
     first_near = first_far = None
     chunk_shape = float_like(*chunk)
     for corrector in range(2):
+        is_first = corrector == 0
         near_sums, far_sums = collisions(sigma_near, sigma_send)
-        is_first = corrector == 0
-        common = (place, onsite, energy, estimate_near, estimate_far)
+        common = (onsite, energy, estimate_near, estimate_far)
         tables = (screens, table, twiddle)
         if is_first:
             far_out, near_out = (chunk_shape,) * 2, (chunk_shape,) * 2
@@ -640,7 +673,7 @@
         far_result = pl.pallas_call(
             functools.partial(advance_far_kernel, is_first, len(far_sums)),
             out_shape=far_out,
-            in_specs=[scalar, scalar] + [whole()] * (len(far_inputs) - 2),
+            in_specs=[whole()] * len(far_inputs),
             out_specs=(whole(),) * len(far_out),
             compiler_params=small,
             name="advance_far",
@@ -650,7 +683,7 @@
         near_result = pl.pallas_call(
             functools.partial(advance_near_kernel, is_first, len(near_sums)),
             out_shape=near_out,
-            in_specs=[scalar, scalar] + [whole()] * (len(near_inputs) - 2),
+            in_specs=[whole()] * len(near_inputs),
             out_specs=(whole(),) * len(near_out),
             compiler_params=small,
             name="advance_near",
@@ -664,12 +697,12 @@
     return pl.pallas_call(
         functools.partial(closing_kernel, len(near_sums), len(far_sums)),
         out_shape=(full, full),
-        in_specs=[scalar, scalar] + [whole()] * (7 + len(near_sums) + len(far_sums)),
+        in_specs=[whole()] * (8 + len(near_sums) + len(far_sums)),
         out_specs=(whole(), whole()),
         compiler_params=small,
         name="closing",
     )(
-        place, onsite, energy, estimate_near, estimate_far, green_near, green_far, first_near,
+        onsite, energy, estimate_near, estimate_far, green_near, green_far, first_near,
         first_far, *near_sums, *far_sums,
     )
 

time: 146 us -> 139 us (0.952)
  Pallas kernels: 29.7 us -> 22.1 us
  waiting for transfers between devices: 58.3 us -> 61.6 us
  other arithmetic: 2.99 us -> 0.88 us
    pallas_call x6, Pallas kernels: 22 us -> 18.5 us  [collide(): pl.pallas_call(functools.partial(collide_kernel, order), out_shape=(float...]
    ppermute x12, waiting for transfers between devices: 26.6 us -> 30.1 us  [halved_sum(): arriving = lax.ppermute(outgoing, 'ta', flip(1 << bit, ta_count))]
    unnamed x24 -> x22, local copies, waits for them, and re-layouts: 7.57 us -> 8.88 us
  transfers between devices with their start and end apart: 33 -> 33, of which waited for: 23 -> 19; matrix products, arithmetic and copies ran while one was open for 3% -> 1% of each run, Pallas kernels for 9% -> 7%
where the time goes in v1:
time: 139 us; the launch traced here: 138 us
  waiting for transfers between devices  61.6 us (44%)
  starting transfers between devices  43.3 us (31%)
  Pallas kernels  22.1 us (16%)
  local copies, waits for them, and re-layouts  8.89 us (6%)
  between operations  1.59 us (1%)
    ppermute x12, waiting for transfers between devices, halved_sum(): arriving = lax.ppermute(outgoing, 'ta', flip(1 << bit, ta_count))  30.1 us
    pallas_call x6, Pallas kernels, collide(): pl.pallas_call(functools.partial(collide_kernel, order), out_shape=(float...  18.5 us
    ppermute x12, starting transfers between devices, halved_sum(): arriving = lax.ppermute(outgoing, 'ta', flip(1 << bit, ta_count))  18.4 us
    ppermute x9, starting transfers between devices, halved_sum(): lax.ppermute(pieces[place], 'ta', flip(place << shift, ta_count))  13.4 us
    ppermute x3, waiting for transfers between devices, collisions(): sigma_far = lax.ppermute(sigma_send, 'ka', flip(1, ka_count))  12.8 us
    ppermute x9, waiting for transfers between devices, halved_sum(): lax.ppermute(pieces[place], 'ta', flip(place << shift, ta_count))  12.4 us
    unnamed x22, local copies, waits for them, and re-layouts  8.88 us
    ppermute x2, waiting for transfers between devices, fast(): arrived = lax.ppermute(far_result[-1], 'ka', flip(1, ka_count))  5.53 us
  transfers between devices with their start and end apart: 33, of which 19 were waited for; matrix products, arithmetic and copies ran while one was open for 1% of the time, Pallas kernels for 7%

profile of v1, /device:TPU:0, one launch (start us, length us, event | category | flops | bytes accessed | tf_op | source)
XLA Modules:
  0.0 138.4 jit_solution(8897508289413358426)
XLA Ops:
  0.6 0.9 copy-done.5
  1.5 0.9 copy-done.6
  2.4 0.9 copy-done.7
  3.5 3.0 %collective-permute-start = (f32[3,2,2,8,512]{4,3,2,1,0:T(8,128)S(1)}, f32[3,2,2,8,512]{4,3,2,1,0:T(8,128)S(1)}, u32[]{:S(2)}, u32[]{:S(2)}) collective-permute-start(f32[3,2,2,8,512]{4,3,2,1,0:T(8,128)S(1)} %get-tuple-element.36), channel_id=1, source_target_pairs={{0,1},{1,0},{2,3},{3,2},{4,5},{5,4},{6,7},{7,6},{8,9},{9,8},{10,11... | collective-permute-start | bytes 589832 | tf_op jit(solution)/shard_map/ppermute | solution.py:600
  7.3 0.9 copy-done.4
  12.1 1.6 %copy-done = bf16[2,4,4,2,32,512]{5,4,3,2,1,0:T(8,128)(2,1)S(1)} copy-done((bf16[2,4,4,2,32,512]{5,4,3,2,1,0:T(8,128)(2,1)S(1)}, bf16[2,4,4,2,32,512]{5,4,3,2,1,0:T(8,128)(2,1)}, u32[]{:S(2)}) %copy-start) | copy-done | bytes 2097176
  13.7 1.6 %copy-done.2 = bf16[2,4,4,2,32,512]{5,4,3,2,1,0:T(8,128)(2,1)S(1)} copy-done((bf16[2,4,4,2,32,512]{5,4,3,2,1,0:T(8,128)(2,1)S(1)}, bf16[2,4,4,2,32,512]{5,4,3,2,1,0:T(8,128)(2,1)}, u32[]{:S(2)}) %copy-start.2) | copy-done | bytes 2097176
  15.2 3.1 %collide.7 = (f32[8,2,2,8,512]{4,3,2,1,0:T(8,128)S(1)}, f32[8,2,2,8,512]{4,3,2,1,0:T(8,128)S(1)}) custom-call(f32[2,2,2,8,512]{4,3,2,1,0:T(8,128)S(1)} %get-tuple-element.45.sigma_ref, f32[2,32,128]{2,1,0:T(8,128)S(1)} %get-tuple-element.40.causal_ref, bf16[2,4,4,2,32,512]{5,4,3,2,1,0:T(8,128)(2,1)S(1)} %copy-done, bf16[2,4,4,2,32,512]{5,4,3,2,1,0:T(8,128)(2,1)S(1)} %copy-done.2), custom_call_target="tpu_custom_call" | custom-call | flops 16777216 | bytes 4194304 | tf_op jit(solution)/shard_map/collide/pallas_call | solution.py:635
  18.4 1.8 %collective-permute-start.1 = (f32[2,2,2,8,512]{4,3,2,1,0:T(8,128)S(1)}, f32[2,2,2,8,512]{4,3,2,1,0:T(8,128)S(1)}, u32[]{:S(2)}, u32[]{:S(2)}) collective-permute-start(f32[2,2,2,8,512]{4,3,2,1,0:T(8,128)S(1)} %get-tuple-element.39), channel_id=1, source_target_pairs={{0,1},{1,0},{2,3},{3,2},{4,5},{5,4},{6,7},{7,6},{8,9},{9,8},{10,11... | collective-permute-start | bytes 393224 | tf_op jit(solution)/shard_map/ppermute | solution.py:650
  20.2 4.1 %collective-permute-done.1.sigma_ref = f32[2,2,2,8,512]{4,3,2,1,0:T(8,128)S(1)} collective-permute-done((f32[2,2,2,8,512]{4,3,2,1,0:T(8,128)S(1)}, f32[2,2,2,8,512]{4,3,2,1,0:T(8,128)S(1)}, u32[]{:S(2)}, u32[]{:S(2)}) %collective-permute-start.1) | collective-permute-done | bytes 131104 | tf_op jit(solution)/shard_map/ppermute | solution.py:650
  24.3 3.1 %collide.6 = (f32[8,2,2,8,512]{4,3,2,1,0:T(8,128)S(1)}, f32[8,2,2,8,512]{4,3,2,1,0:T(8,128)S(1)}) custom-call(f32[2,2,2,8,512]{4,3,2,1,0:T(8,128)S(1)} %collective-permute-done.1.sigma_ref, f32[2,32,128]{2,1,0:T(8,128)S(1)} %get-tuple-element.40.causal_ref, bf16[2,4,4,2,32,512]{5,4,3,2,1,0:T(8,128)(2,1)S(1)} %copy-done, ...), custom_call_target="tpu_custom_call" | custom-call | flops 16777216 | bytes 4194304 | tf_op jit(solution)/shard_map/collide/pallas_call | solution.py:635
  27.6 1.8 %collective-permute-start.9 = (f32[4,2,2,8,512]{4,3,2,1,0:T(8,128)S(1)}, f32[4,2,2,8,512]{4,3,2,1,0:T(8,128)S(1)}, u32[]{:S(2)}, u32[]{:S(2)}) collective-permute-start(f32[4,2,2,8,512]{4,3,2,1,0:T(8,128)S(1)} %get-tuple-element.73), channel_id=1, source_target_pairs={{0,4},{2,6},{4,0},{6,2},{8,12},{10,14},{12,8},{14,10},{16,20},{18,... | collective-permute-start | bytes 786440 | tf_op jit(solution)/shard_map/ppermute | solution.py:556
  29.5 1.8 %collective-permute-start.3 = (f32[4,2,2,8,512]{4,3,2,1,0:T(8,128)S(1)}, f32[4,2,2,8,512]{4,3,2,1,0:T(8,128)S(1)}, u32[]{:S(2)}, u32[]{:S(2)}) collective-permute-start(f32[4,2,2,8,512]{4,3,2,1,0:T(8,128)S(1)} %get-tuple-element.75), channel_id=1, source_target_pairs={{0,4},{2,6},{4,0},{6,2},{8,12},{10,14},{12,8},{14,10},{16,20},{18,... | collective-permute-start | bytes 786440 | tf_op jit(solution)/shard_map/ppermute | solution.py:556
  31.3 5.5 %collective-permute-done.9 = f32[4,2,2,8,512]{4,3,2,1,0:T(8,128)S(1)} collective-permute-done((f32[4,2,2,8,512]{4,3,2,1,0:T(8,128)S(1)}, f32[4,2,2,8,512]{4,3,2,1,0:T(8,128)S(1)}, u32[]{:S(2)}, u32[]{:S(2)}) %collective-permute-start.9) | collective-permute-done | bytes 262176 | tf_op jit(solution)/shard_map/ppermute | solution.py:556
  36.8 1.9 %collective-permute-start.10 = (f32[2,2,2,8,512]{4,3,2,1,0:T(8,128)S(1)}, f32[2,2,2,8,512]{4,3,2,1,0:T(8,128)S(1)}, u32[]{:S(2)}, u32[]{:S(2)}) collective-permute-start(f32[2,2,2,8,512]{4,3,2,1,0:T(8,128)S(1)} %get-tuple-element.89), channel_id=1, source_target_pairs={{0,8},{2,10},{4,12},{6,14},{8,0},{10,2},{12,4},{14,6},{16,24},{18,... | collective-permute-start | bytes 393224 | tf_op jit(solution)/shard_map/ppermute | solution.py:556
  38.7 3.2 %collective-permute-done.3 = f32[4,2,2,8,512]{4,3,2,1,0:T(8,128)S(1)} collective-permute-done((f32[4,2,2,8,512]{4,3,2,1,0:T(8,128)S(1)}, f32[4,2,2,8,512]{4,3,2,1,0:T(8,128)S(1)}, u32[]{:S(2)}, u32[]{:S(2)}) %collective-permute-start.3) | collective-permute-done | bytes 262176 | tf_op jit(solution)/shard_map/ppermute | solution.py:556
  42.0 3.9 %collective-permute-start.6 = (f32[2,2,8,512]{3,2,1,0:T(8,128)S(1)}, f32[2,2,8,512]{3,2,1,0:T(8,128)S(1)}, u32[]{:S(2)}, u32[]{:S(2)}) collective-permute-start(f32[2,2,8,512]{3,2,1,0:T(8,128)S(1)} %get-tuple-element.90), channel_id=1, source_target_pairs={{0,24},{2,26},{4,28},{6,30},{8,16},{10,18},{12,20},{14,22},{16,8},... | collective-permute-start | bytes 196616 | tf_op jit(solution)/shard_map/ppermute | solution.py:564
  46.6 2.4 %collective-permute-start.11 = (f32[1,2,2,8,512]{4,3,2,1,0:T(8,128)S(1)}, f32[1,2,2,8,512]{4,3,2,1,0:T(8,128)S(1)}, u32[]{:S(2)}, u32[]{:S(2)}) collective-permute-start(f32[1,2,2,8,512]{4,3,2,1,0:T(8,128)S(1)} %get-tuple-element.98), channel_id=1, source_target_pairs={{0,16},{2,18},{4,20},{6,22},{8,24},{10,26},{12,28},{14,30},{16,0},... | collective-permute-start | bytes 196616 | tf_op jit(solution)/shard_map/ppermute | solution.py:556
  48.9 3.5 %collective-permute-done.5.refs_2_ = f32[2,2,8,512]{3,2,1,0:T(8,128)S(1)} collective-permute-done((f32[2,2,8,512]{3,2,1,0:T(8,128)S(1)}, f32[2,2,8,512]{3,2,1,0:T(8,128)S(1)}, u32[]{:S(2)}, u32[]{:S(2)}) %collective-permute-start.5) | collective-permute-done | bytes 65568 | tf_op jit(solution)/shard_map/ppermute | solution.py:564
  52.5 1.6 %collective-permute-start.7 = (f32[2,2,8,512]{3,2,1,0:T(8,128)S(1)}, f32[2,2,8,512]{3,2,1,0:T(8,128)S(1)}, u32[]{:S(2)}, u32[]{:S(2)}) collective-permute-start(f32[2,2,8,512]{3,2,1,0:T(8,128)S(1)} %get-tuple-element.43.far_ref), channel_id=1, source_target_pairs={{0,1},{1,0},{2,3},{3,2},{4,5},{5,4},{6,7},{7,6},{8,9},{9,8},{10,11... | collective-permute-start | bytes 196616 | tf_op jit(solution)/shard_map/ppermute | solution.py:681
  54.1 2.8 %collective-permute-done.7.arrived_ref = f32[2,2,8,512]{3,2,1,0:T(8,128)S(1)} collective-permute-done((f32[2,2,8,512]{3,2,1,0:T(8,128)S(1)}, f32[2,2,8,512]{3,2,1,0:T(8,128)S(1)}, u32[]{:S(2)}, u32[]{:S(2)}) %collective-permute-start.7) | collective-permute-done | bytes 65568 | tf_op jit(solution)/shard_map/ppermute | solution.py:681
  57.5 3.1 %collide.9 = (f32[8,2,2,8,512]{4,3,2,1,0:T(8,128)S(1)}, f32[8,2,2,8,512]{4,3,2,1,0:T(8,128)S(1)}) custom-call(f32[2,2,2,8,512]{4,3,2,1,0:T(8,128)S(1)} %get-tuple-element.53.sigma_ref, f32[2,32,128]{2,1,0:T(8,128)S(1)} %get-tuple-element.40.causal_ref, bf16[2,4,4,2,32,512]{5,4,3,2,1,0:T(8,128)(2,1)S(1)} %copy-done.1, ...), custom_call_target="tpu_custom_call" | custom-call | flops 16777216 | bytes 4194304 | tf_op jit(solution)/shard_map/collide/pallas_call | solution.py:635
  60.6 1.6 %collective-permute-start.12 = (f32[2,2,2,8,512]{4,3,2,1,0:T(8,128)S(1)}, f32[2,2,2,8,512]{4,3,2,1,0:T(8,128)S(1)}, u32[]{:S(2)}, u32[]{:S(2)}) collective-permute-start(f32[2,2,2,8,512]{4,3,2,1,0:T(8,128)S(1)} %get-tuple-element.49), channel_id=1, source_target_pairs={{0,1},{1,0},{2,3},{3,2},{4,5},{5,4},{6,7},{7,6},{8,9},{9,8},{10,11... | collective-permute-start | bytes 393224 | tf_op jit(solution)/shard_map/ppermute | solution.py:650
  62.2 4.3 %collective-permute-done.12.sigma_ref = f32[2,2,2,8,512]{4,3,2,1,0:T(8,128)S(1)} collective-permute-done((f32[2,2,2,8,512]{4,3,2,1,0:T(8,128)S(1)}, f32[2,2,2,8,512]{4,3,2,1,0:T(8,128)S(1)}, u32[]{:S(2)}, u32[]{:S(2)}) %collective-permute-start.12) | collective-permute-done | bytes 131104 | tf_op jit(solution)/shard_map/ppermute | solution.py:650
  66.5 3.1 %collide.8 = (f32[8,2,2,8,512]{4,3,2,1,0:T(8,128)S(1)}, f32[8,2,2,8,512]{4,3,2,1,0:T(8,128)S(1)}) custom-call(f32[2,2,2,8,512]{4,3,2,1,0:T(8,128)S(1)} %collective-permute-done.12.sigma_ref, f32[2,32,128]{2,1,0:T(8,128)S(1)} %get-tuple-element.40.causal_ref, bf16[2,4,4,2,32,512]{5,4,3,2,1,0:T(8,128)(2,1)S(1)} %copy-done.1, ...), custom_call_target="tpu_custom_call" | custom-call | flops 16777216 | bytes 4194304 | tf_op jit(solution)/shard_map/collide/pallas_call | solution.py:635
  69.8 1.6 %collective-permute-start.20 = (f32[4,2,2,8,512]{4,3,2,1,0:T(8,128)S(1)}, f32[4,2,2,8,512]{4,3,2,1,0:T(8,128)S(1)}, u32[]{:S(2)}, u32[]{:S(2)}) collective-permute-start(f32[4,2,2,8,512]{4,3,2,1,0:T(8,128)S(1)} %get-tuple-element.69), channel_id=1, source_target_pairs={{0,4},{2,6},{4,0},{6,2},{8,12},{10,14},{12,8},{14,10},{16,20},{18,... | collective-permute-start | bytes 786440 | tf_op jit(solution)/shard_map/ppermute | solution.py:556
  71.7 1.6 %collective-permute-start.14 = (f32[4,2,2,8,512]{4,3,2,1,0:T(8,128)S(1)}, f32[4,2,2,8,512]{4,3,2,1,0:T(8,128)S(1)}, u32[]{:S(2)}, u32[]{:S(2)}) collective-permute-start(f32[4,2,2,8,512]{4,3,2,1,0:T(8,128)S(1)} %get-tuple-element.71), channel_id=1, source_target_pairs={{0,4},{2,6},{4,0},{6,2},{8,12},{10,14},{12,8},{14,10},{16,20},{18,... | collective-permute-start | bytes 786440 | tf_op jit(solution)/shard_map/ppermute | solution.py:556
  73.3 5.8 %collective-permute-done.20 = f32[4,2,2,8,512]{4,3,2,1,0:T(8,128)S(1)} collective-permute-done((f32[4,2,2,8,512]{4,3,2,1,0:T(8,128)S(1)}, f32[4,2,2,8,512]{4,3,2,1,0:T(8,128)S(1)}, u32[]{:S(2)}, u32[]{:S(2)}) %collective-permute-start.20) | collective-permute-done | bytes 262176 | tf_op jit(solution)/shard_map/ppermute | solution.py:556
  79.8 4.4 %collective-permute-done.14 = f32[4,2,2,8,512]{4,3,2,1,0:T(8,128)S(1)} collective-permute-done((f32[4,2,2,8,512]{4,3,2,1,0:T(8,128)S(1)}, f32[4,2,2,8,512]{4,3,2,1,0:T(8,128)S(1)}, u32[]{:S(2)}, u32[]{:S(2)}) %collective-permute-start.14) | collective-permute-done | bytes 262176 | tf_op jit(solution)/shard_map/ppermute | solution.py:556
  84.2 3.7 %collective-permute-start.17 = (f32[2,2,8,512]{3,2,1,0:T(8,128)S(1)}, f32[2,2,8,512]{3,2,1,0:T(8,128)S(1)}, u32[]{:S(2)}, u32[]{:S(2)}) collective-permute-start(f32[2,2,8,512]{3,2,1,0:T(8,128)S(1)} %get-tuple-element.84), channel_id=1, source_target_pairs={{0,24},{2,26},{4,28},{6,30},{8,16},{10,18},{12,20},{14,22},{16,8},... | collective-permute-start | bytes 196616 | tf_op jit(solution)/shard_map/ppermute | solution.py:564
  88.7 2.2 %collective-permute-start.22 = (f32[1,2,2,8,512]{4,3,2,1,0:T(8,128)S(1)}, f32[1,2,2,8,512]{4,3,2,1,0:T(8,128)S(1)}, u32[]{:S(2)}, u32[]{:S(2)}) collective-permute-start(f32[1,2,2,8,512]{4,3,2,1,0:T(8,128)S(1)} %get-tuple-element.96), channel_id=1, source_target_pairs={{0,16},{2,18},{4,20},{6,22},{8,24},{10,26},{12,28},{14,30},{16,0},... | collective-permute-start | bytes 196616 | tf_op jit(solution)/shard_map/ppermute | solution.py:556
  90.9 3.4 %collective-permute-done.16.refs_2_ = f32[2,2,8,512]{3,2,1,0:T(8,128)S(1)} collective-permute-done((f32[2,2,8,512]{3,2,1,0:T(8,128)S(1)}, f32[2,2,8,512]{3,2,1,0:T(8,128)S(1)}, u32[]{:S(2)}, u32[]{:S(2)}) %collective-permute-start.16) | collective-permute-done | bytes 65568 | tf_op jit(solution)/shard_map/ppermute | solution.py:564
  94.4 1.6 %collective-permute-start.18 = (f32[2,2,8,512]{3,2,1,0:T(8,128)S(1)}, f32[2,2,8,512]{3,2,1,0:T(8,128)S(1)}, u32[]{:S(2)}, u32[]{:S(2)}) collective-permute-start(f32[2,2,8,512]{3,2,1,0:T(8,128)S(1)} %advance_far.3.far_ref), channel_id=1, source_target_pairs={{0,1},{1,0},{2,3},{3,2},{4,5},{5,4},{6,7},{7,6},{8,9},{9,8},{10,11... | collective-permute-start | bytes 196616 | tf_op jit(solution)/shard_map/ppermute | solution.py:681
  95.9 2.8 %collective-permute-done.18.arrived_ref = f32[2,2,8,512]{3,2,1,0:T(8,128)S(1)} collective-permute-done((f32[2,2,8,512]{3,2,1,0:T(8,128)S(1)}, f32[2,2,8,512]{3,2,1,0:T(8,128)S(1)}, u32[]{:S(2)}, u32[]{:S(2)}) %collective-permute-start.18) | collective-permute-done | bytes 65568 | tf_op jit(solution)/shard_map/ppermute | solution.py:681
  99.3 3.1 %collide.10 = (f32[8,2,2,8,512]{4,3,2,1,0:T(8,128)S(1)}, f32[8,2,2,8,512]{4,3,2,1,0:T(8,128)S(1)}) custom-call(f32[2,2,2,8,512]{4,3,2,1,0:T(8,128)S(1)} %get-tuple-element.58.sigma_ref, f32[2,32,128]{2,1,0:T(8,128)S(1)} %get-tuple-element.40.causal_ref, bf16[2,4,4,2,32,512]{5,4,3,2,1,0:T(8,128)(2,1)S(1)} %copy-done.1, ...), custom_call_target="tpu_custom_call" | custom-call | flops 16777216 | bytes 4194304 | tf_op jit(solution)/shard_map/collide/pallas_call | solution.py:635
  102.5 1.6 %collective-permute-start.27 = (f32[2,2,2,8,512]{4,3,2,1,0:T(8,128)S(1)}, f32[2,2,2,8,512]{4,3,2,1,0:T(8,128)S(1)}, u32[]{:S(2)}, u32[]{:S(2)}) collective-permute-start(f32[2,2,2,8,512]{4,3,2,1,0:T(8,128)S(1)} %get-tuple-element.61), channel_id=1, source_target_pairs={{0,1},{1,0},{2,3},{3,2},{4,5},{5,4},{6,7},{7,6},{8,9},{9,8},{10,11... | collective-permute-start | bytes 393224 | tf_op jit(solution)/shard_map/ppermute | solution.py:650
  104.0 4.3 %collective-permute-done.27.sigma_ref = f32[2,2,2,8,512]{4,3,2,1,0:T(8,128)S(1)} collective-permute-done((f32[2,2,2,8,512]{4,3,2,1,0:T(8,128)S(1)}, f32[2,2,2,8,512]{4,3,2,1,0:T(8,128)S(1)}, u32[]{:S(2)}, u32[]{:S(2)}) %collective-permute-start.27) | collective-permute-done | bytes 131104 | tf_op jit(solution)/shard_map/ppermute | solution.py:650
  108.4 3.1 %collide.11 = (f32[8,2,2,8,512]{4,3,2,1,0:T(8,128)S(1)}, f32[8,2,2,8,512]{4,3,2,1,0:T(8,128)S(1)}) custom-call(f32[2,2,2,8,512]{4,3,2,1,0:T(8,128)S(1)} %collective-permute-done.27.sigma_ref, f32[2,32,128]{2,1,0:T(8,128)S(1)} %get-tuple-element.40.causal_ref, bf16[2,4,4,2,32,512]{5,4,3,2,1,0:T(8,128)(2,1)S(1)} %copy-done.1, ...), custom_call_target="tpu_custom_call" | custom-call | flops 16777216 | bytes 4194304 | tf_op jit(solution)/shard_map/collide/pallas_call | solution.py:635
  111.6 1.6 %collective-permute-start.24 = (f32[4,2,2,8,512]{4,3,2,1,0:T(8,128)S(1)}, f32[4,2,2,8,512]{4,3,2,1,0:T(8,128)S(1)}, u32[]{:S(2)}, u32[]{:S(2)}) collective-permute-start(f32[4,2,2,8,512]{4,3,2,1,0:T(8,128)S(1)} %get-tuple-element.67), channel_id=1, source_target_pairs={{0,4},{2,6},{4,0},{6,2},{8,12},{10,14},{12,8},{14,10},{16,20},{18,... | collective-permute-start | bytes 786440 | tf_op jit(solution)/shard_map/ppermute | solution.py:556
  113.5 1.6 %collective-permute-start.29 = (f32[4,2,2,8,512]{4,3,2,1,0:T(8,128)S(1)}, f32[4,2,2,8,512]{4,3,2,1,0:T(8,128)S(1)}, u32[]{:S(2)}, u32[]{:S(2)}) collective-permute-start(f32[4,2,2,8,512]{4,3,2,1,0:T(8,128)S(1)} %get-tuple-element.65), channel_id=1, source_target_pairs={{0,4},{2,6},{4,0},{6,2},{8,12},{10,14},{12,8},{14,10},{16,20},{18,... | collective-permute-start | bytes 786440 | tf_op jit(solution)/shard_map/ppermute | solution.py:556
  115.1 5.8 %collective-permute-done.24 = f32[4,2,2,8,512]{4,3,2,1,0:T(8,128)S(1)} collective-permute-done((f32[4,2,2,8,512]{4,3,2,1,0:T(8,128)S(1)}, f32[4,2,2,8,512]{4,3,2,1,0:T(8,128)S(1)}, u32[]{:S(2)}, u32[]{:S(2)}) %collective-permute-start.24) | collective-permute-done | bytes 262176 | tf_op jit(solution)/shard_map/ppermute | solution.py:556
  121.7 4.3 %collective-permute-done.29 = f32[4,2,2,8,512]{4,3,2,1,0:T(8,128)S(1)} collective-permute-done((f32[4,2,2,8,512]{4,3,2,1,0:T(8,128)S(1)}, f32[4,2,2,8,512]{4,3,2,1,0:T(8,128)S(1)}, u32[]{:S(2)}, u32[]{:S(2)}) %collective-permute-start.29) | collective-permute-done | bytes 262176 | tf_op jit(solution)/shard_map/ppermute | solution.py:556
  126.0 2.0 %collective-permute-start.32 = (f32[2,2,8,512]{3,2,1,0:T(8,128)S(1)}, f32[2,2,8,512]{3,2,1,0:T(8,128)S(1)}, u32[]{:S(2)}, u32[]{:S(2)}) collective-permute-start(f32[2,2,8,512]{3,2,1,0:T(8,128)S(1)} %get-tuple-element.76), channel_id=1, source_target_pairs={{0,24},{2,26},{4,28},{6,30},{8,16},{10,18},{12,20},{14,22},{16,8},... | collective-permute-start | bytes 196616 | tf_op jit(solution)/shard_map/ppermute | solution.py:564
  128.3 2.2 %collective-permute-start.30 = (f32[2,2,8,512]{3,2,1,0:T(8,128)S(1)}, f32[2,2,8,512]{3,2,1,0:T(8,128)S(1)}, u32[]{:S(2)}, u32[]{:S(2)}) collective-permute-start(f32[2,2,8,512]{3,2,1,0:T(8,128)S(1)} %get-tuple-element.78), channel_id=1, source_target_pairs={{0,8},{2,10},{4,12},{6,14},{8,0},{10,2},{12,4},{14,6},{16,24},{18,... | collective-permute-start | bytes 196616 | tf_op jit(solution)/shard_map/ppermute | solution.py:564
  131.0 1.5 %collective-permute-done.32.refs_5_ = f32[2,2,8,512]{3,2,1,0:T(8,128)S(1)} collective-permute-done((f32[2,2,8,512]{3,2,1,0:T(8,128)S(1)}, f32[2,2,8,512]{3,2,1,0:T(8,128)S(1)}, u32[]{:S(2)}, u32[]{:S(2)}) %collective-permute-start.32) | collective-permute-done | bytes 65568 | tf_op jit(solution)/shard_map/ppermute | solution.py:564
  132.5 3.9 %collective-permute-done.31.refs_4_ = f32[2,2,8,512]{3,2,1,0:T(8,128)S(1)} collective-permute-done((f32[2,2,8,512]{3,2,1,0:T(8,128)S(1)}, f32[2,2,8,512]{3,2,1,0:T(8,128)S(1)}, u32[]{:S(2)}, u32[]{:S(2)}) %collective-permute-start.31) | collective-permute-done | bytes 65568 | tf_op jit(solution)/shard_map/ppermute | solution.py:564
  136.5 1.1 collective-permute-done.26
  137.6 0.9 closing.1
  (72 shorter events, 10.8 us)
Async XLA Ops:
  0.6 0.9 copy-start.5
  1.5 0.9 copy-start.6
  2.4 0.9 copy-start.7
  3.5 7.9 %collective-permute-start = (f32[3,2,2,8,512]{4,3,2,1,0:T(8,128)S(1)}, f32[3,2,2,8,512]{4,3,2,1,0:T(8,128)S(1)}, u32[]{:S(2)}, u32[]{:S(2)}) collective-permute-start(f32[3,2,2,8,512]{4,3,2,1,0:T(8,128)S(1)} %get-tuple-element.36), channel_id=1, source_target_pairs={{0,1},{1,0},{2,3},{3,2},{4,5},{5,4},{6,7},{7,6},{8,9},{9,8},{10,11... | collective-permute-start | bytes 589832 | tf_op jit(solution)/shard_map/ppermute | solution.py:600
  7.3 1.0 copy-start.4
  8.2 0.7 copy-start.8
  8.9 0.7 copy-start.9
  9.6 0.7 copy-start.10
  12.1 1.6 %copy-start = (bf16[2,4,4,2,32,512]{5,4,3,2,1,0:T(8,128)(2,1)S(1)}, bf16[2,4,4,2,32,512]{5,4,3,2,1,0:T(8,128)(2,1)}, u32[]{:S(2)}) copy-start(bf16[2,4,4,2,32,512]{5,4,3,2,1,0:T(8,128)(2,1)} %lesser_ref.13) | copy-start | bytes 6291460
  13.7 1.6 %copy-start.2 = (bf16[2,4,4,2,32,512]{5,4,3,2,1,0:T(8,128)(2,1)S(1)}, bf16[2,4,4,2,32,512]{5,4,3,2,1,0:T(8,128)(2,1)}, u32[]{:S(2)}) copy-start(bf16[2,4,4,2,32,512]{5,4,3,2,1,0:T(8,128)(2,1)} %advanced_ref.11) | copy-start | bytes 6291460
  18.3 9.1 %collective-permute-start.8 = (f32[8,2,2,8,512]{4,3,2,1,0:T(8,128)S(1)}, f32[8,2,2,8,512]{4,3,2,1,0:T(8,128)S(1)}, u32[]{:S(2)}, u32[]{:S(2)}) collective-permute-start(f32[8,2,2,8,512]{4,3,2,1,0:T(8,128)S(1)} %get-tuple-element.47), channel_id=1, source_target_pairs={{0,2},{2,0},{4,6},{6,4},{8,10},{10,8},{12,14},{14,12},{16,18},{18,... | collective-permute-start | bytes 1572872 | tf_op jit(solution)/shard_map/ppermute | solution.py:552
  18.4 5.9 %collective-permute-start.1 = (f32[2,2,2,8,512]{4,3,2,1,0:T(8,128)S(1)}, f32[2,2,2,8,512]{4,3,2,1,0:T(8,128)S(1)}, u32[]{:S(2)}, u32[]{:S(2)}) collective-permute-start(f32[2,2,2,8,512]{4,3,2,1,0:T(8,128)S(1)} %get-tuple-element.39), channel_id=1, source_target_pairs={{0,1},{1,0},{2,3},{3,2},{4,5},{5,4},{6,7},{7,6},{8,9},{9,8},{10,11... | collective-permute-start | bytes 393224 | tf_op jit(solution)/shard_map/ppermute | solution.py:650
  27.4 2.0 %collective-permute-start.2 = (f32[8,2,2,8,512]{4,3,2,1,0:T(8,128)S(1)}, f32[8,2,2,8,512]{4,3,2,1,0:T(8,128)S(1)}, u32[]{:S(2)}, u32[]{:S(2)}) collective-permute-start(f32[8,2,2,8,512]{4,3,2,1,0:T(8,128)S(1)} %get-tuple-element.42), channel_id=1, source_target_pairs={{0,2},{2,0},{4,6},{6,4},{8,10},{10,8},{12,14},{14,12},{16,18},{18,... | collective-permute-start | bytes 1572872 | tf_op jit(solution)/shard_map/ppermute | solution.py:552
  27.6 9.2 %collective-permute-start.9 = (f32[4,2,2,8,512]{4,3,2,1,0:T(8,128)S(1)}, f32[4,2,2,8,512]{4,3,2,1,0:T(8,128)S(1)}, u32[]{:S(2)}, u32[]{:S(2)}) collective-permute-start(f32[4,2,2,8,512]{4,3,2,1,0:T(8,128)S(1)} %get-tuple-element.73), channel_id=1, source_target_pairs={{0,4},{2,6},{4,0},{6,2},{8,12},{10,14},{12,8},{14,10},{16,20},{18,... | collective-permute-start | bytes 786440 | tf_op jit(solution)/shard_map/ppermute | solution.py:556
  29.4 28.1 %copy-start.3 = (bf16[2,4,4,2,32,512]{5,4,3,2,1,0:T(8,128)(2,1)S(1)}, bf16[2,4,4,2,32,512]{5,4,3,2,1,0:T(8,128)(2,1)}, u32[]{:S(2)}) copy-start(bf16[2,4,4,2,32,512]{5,4,3,2,1,0:T(8,128)(2,1)} %advanced_ref.11) | copy-start | bytes 6291460
  29.5 28.0 %copy-start.1 = (bf16[2,4,4,2,32,512]{5,4,3,2,1,0:T(8,128)(2,1)S(1)}, bf16[2,4,4,2,32,512]{5,4,3,2,1,0:T(8,128)(2,1)}, u32[]{:S(2)}) copy-start(bf16[2,4,4,2,32,512]{5,4,3,2,1,0:T(8,128)(2,1)} %lesser_ref.13) | copy-start | bytes 6291460
  29.5 12.5 %collective-permute-start.3 = (f32[4,2,2,8,512]{4,3,2,1,0:T(8,128)S(1)}, f32[4,2,2,8,512]{4,3,2,1,0:T(8,128)S(1)}, u32[]{:S(2)}, u32[]{:S(2)}) collective-permute-start(f32[4,2,2,8,512]{4,3,2,1,0:T(8,128)S(1)} %get-tuple-element.75), channel_id=1, source_target_pairs={{0,4},{2,6},{4,0},{6,2},{8,12},{10,14},{12,8},{14,10},{16,20},{18,... | collective-permute-start | bytes 786440 | tf_op jit(solution)/shard_map/ppermute | solution.py:556
  36.8 9.7 %collective-permute-start.10 = (f32[2,2,2,8,512]{4,3,2,1,0:T(8,128)S(1)}, f32[2,2,2,8,512]{4,3,2,1,0:T(8,128)S(1)}, u32[]{:S(2)}, u32[]{:S(2)}) collective-permute-start(f32[2,2,2,8,512]{4,3,2,1,0:T(8,128)S(1)} %get-tuple-element.89), channel_id=1, source_target_pairs={{0,8},{2,10},{4,12},{6,14},{8,0},{10,2},{12,4},{14,6},{16,24},{18,... | collective-permute-start | bytes 393224 | tf_op jit(solution)/shard_map/ppermute | solution.py:556
  42.0 6.9 %collective-permute-start.6 = (f32[2,2,8,512]{3,2,1,0:T(8,128)S(1)}, f32[2,2,8,512]{3,2,1,0:T(8,128)S(1)}, u32[]{:S(2)}, u32[]{:S(2)}) collective-permute-start(f32[2,2,8,512]{3,2,1,0:T(8,128)S(1)} %get-tuple-element.90), channel_id=1, source_target_pairs={{0,24},{2,26},{4,28},{6,30},{8,16},{10,18},{12,20},{14,22},{16,8},... | collective-permute-start | bytes 196616 | tf_op jit(solution)/shard_map/ppermute | solution.py:564
  45.9 6.6 %collective-permute-start.5 = (f32[2,2,8,512]{3,2,1,0:T(8,128)S(1)}, f32[2,2,8,512]{3,2,1,0:T(8,128)S(1)}, u32[]{:S(2)}, u32[]{:S(2)}) collective-permute-start(f32[2,2,8,512]{3,2,1,0:T(8,128)S(1)} %get-tuple-element.91), channel_id=1, source_target_pairs={{0,16},{2,18},{4,20},{6,22},{8,24},{10,26},{12,28},{14,30},{16,0},... | collective-permute-start | bytes 196616 | tf_op jit(solution)/shard_map/ppermute | solution.py:564
  45.9 6.6 %collective-permute-start.4 = (f32[2,2,8,512]{3,2,1,0:T(8,128)S(1)}, f32[2,2,8,512]{3,2,1,0:T(8,128)S(1)}, u32[]{:S(2)}, u32[]{:S(2)}) collective-permute-start(f32[2,2,8,512]{3,2,1,0:T(8,128)S(1)} %get-tuple-element.92), channel_id=1, source_target_pairs={{0,8},{2,10},{4,12},{6,14},{8,0},{10,2},{12,4},{14,6},{16,24},{18,... | collective-permute-start | bytes 196616 | tf_op jit(solution)/shard_map/ppermute | solution.py:564
  46.6 7.5 %collective-permute-start.11 = (f32[1,2,2,8,512]{4,3,2,1,0:T(8,128)S(1)}, f32[1,2,2,8,512]{4,3,2,1,0:T(8,128)S(1)}, u32[]{:S(2)}, u32[]{:S(2)}) collective-permute-start(f32[1,2,2,8,512]{4,3,2,1,0:T(8,128)S(1)} %get-tuple-element.98), channel_id=1, source_target_pairs={{0,16},{2,18},{4,20},{6,22},{8,24},{10,26},{12,28},{14,30},{16,0},... | collective-permute-start | bytes 196616 | tf_op jit(solution)/shard_map/ppermute | solution.py:556
  52.5 4.3 %collective-permute-start.7 = (f32[2,2,8,512]{3,2,1,0:T(8,128)S(1)}, f32[2,2,8,512]{3,2,1,0:T(8,128)S(1)}, u32[]{:S(2)}, u32[]{:S(2)}) collective-permute-start(f32[2,2,8,512]{3,2,1,0:T(8,128)S(1)} %get-tuple-element.43.far_ref), channel_id=1, source_target_pairs={{0,1},{1,0},{2,3},{3,2},{4,5},{5,4},{6,7},{7,6},{8,9},{9,8},{10,11... | collective-permute-start | bytes 196616 | tf_op jit(solution)/shard_map/ppermute | solution.py:681
  60.6 9.1 %collective-permute-start.19 = (f32[8,2,2,8,512]{4,3,2,1,0:T(8,128)S(1)}, f32[8,2,2,8,512]{4,3,2,1,0:T(8,128)S(1)}, u32[]{:S(2)}, u32[]{:S(2)}) collective-permute-start(f32[8,2,2,8,512]{4,3,2,1,0:T(8,128)S(1)} %get-tuple-element.55), channel_id=1, source_target_pairs={{0,2},{2,0},{4,6},{6,4},{8,10},{10,8},{12,14},{14,12},{16,18},{18,... | collective-permute-start | bytes 1572872 | tf_op jit(solution)/shard_map/ppermute | solution.py:552
  60.6 5.9 %collective-permute-start.12 = (f32[2,2,2,8,512]{4,3,2,1,0:T(8,128)S(1)}, f32[2,2,2,8,512]{4,3,2,1,0:T(8,128)S(1)}, u32[]{:S(2)}, u32[]{:S(2)}) collective-permute-start(f32[2,2,2,8,512]{4,3,2,1,0:T(8,128)S(1)} %get-tuple-element.49), channel_id=1, source_target_pairs={{0,1},{1,0},{2,3},{3,2},{4,5},{5,4},{6,7},{7,6},{8,9},{9,8},{10,11... | collective-permute-start | bytes 393224 | tf_op jit(solution)/shard_map/ppermute | solution.py:650
  69.6 2.0 %collective-permute-start.13 = (f32[8,2,2,8,512]{4,3,2,1,0:T(8,128)S(1)}, f32[8,2,2,8,512]{4,3,2,1,0:T(8,128)S(1)}, u32[]{:S(2)}, u32[]{:S(2)}) collective-permute-start(f32[8,2,2,8,512]{4,3,2,1,0:T(8,128)S(1)} %get-tuple-element.51), channel_id=1, source_target_pairs={{0,2},{2,0},{4,6},{6,4},{8,10},{10,8},{12,14},{14,12},{16,18},{18,... | collective-permute-start | bytes 1572872 | tf_op jit(solution)/shard_map/ppermute | solution.py:552
  69.8 9.2 %collective-permute-start.20 = (f32[4,2,2,8,512]{4,3,2,1,0:T(8,128)S(1)}, f32[4,2,2,8,512]{4,3,2,1,0:T(8,128)S(1)}, u32[]{:S(2)}, u32[]{:S(2)}) collective-permute-start(f32[4,2,2,8,512]{4,3,2,1,0:T(8,128)S(1)} %get-tuple-element.69), channel_id=1, source_target_pairs={{0,4},{2,6},{4,0},{6,2},{8,12},{10,14},{12,8},{14,10},{16,20},{18,... | collective-permute-start | bytes 786440 | tf_op jit(solution)/shard_map/ppermute | solution.py:556
  71.7 12.5 %collective-permute-start.14 = (f32[4,2,2,8,512]{4,3,2,1,0:T(8,128)S(1)}, f32[4,2,2,8,512]{4,3,2,1,0:T(8,128)S(1)}, u32[]{:S(2)}, u32[]{:S(2)}) collective-permute-start(f32[4,2,2,8,512]{4,3,2,1,0:T(8,128)S(1)} %get-tuple-element.71), channel_id=1, source_target_pairs={{0,4},{2,6},{4,0},{6,2},{8,12},{10,14},{12,8},{14,10},{16,20},{18,... | collective-permute-start | bytes 786440 | tf_op jit(solution)/shard_map/ppermute | solution.py:556
  79.1 9.6 %collective-permute-start.21 = (f32[2,2,2,8,512]{4,3,2,1,0:T(8,128)S(1)}, f32[2,2,2,8,512]{4,3,2,1,0:T(8,128)S(1)}, u32[]{:S(2)}, u32[]{:S(2)}) collective-permute-start(f32[2,2,2,8,512]{4,3,2,1,0:T(8,128)S(1)} %get-tuple-element.83), channel_id=1, source_target_pairs={{0,8},{2,10},{4,12},{6,14},{8,0},{10,2},{12,4},{14,6},{16,24},{18,... | collective-permute-start | bytes 393224 | tf_op jit(solution)/shard_map/ppermute | solution.py:556
  84.2 6.7 %collective-permute-start.17 = (f32[2,2,8,512]{3,2,1,0:T(8,128)S(1)}, f32[2,2,8,512]{3,2,1,0:T(8,128)S(1)}, u32[]{:S(2)}, u32[]{:S(2)}) collective-permute-start(f32[2,2,8,512]{3,2,1,0:T(8,128)S(1)} %get-tuple-element.84), channel_id=1, source_target_pairs={{0,24},{2,26},{4,28},{6,30},{8,16},{10,18},{12,20},{14,22},{16,8},... | collective-permute-start | bytes 196616 | tf_op jit(solution)/shard_map/ppermute | solution.py:564
  87.9 6.4 %collective-permute-start.16 = (f32[2,2,8,512]{3,2,1,0:T(8,128)S(1)}, f32[2,2,8,512]{3,2,1,0:T(8,128)S(1)}, u32[]{:S(2)}, u32[]{:S(2)}) collective-permute-start(f32[2,2,8,512]{3,2,1,0:T(8,128)S(1)} %get-tuple-element.85), channel_id=1, source_target_pairs={{0,16},{2,18},{4,20},{6,22},{8,24},{10,26},{12,28},{14,30},{16,0},... | collective-permute-start | bytes 196616 | tf_op jit(solution)/shard_map/ppermute | solution.py:564
  87.9 6.4 %collective-permute-start.15 = (f32[2,2,8,512]{3,2,1,0:T(8,128)S(1)}, f32[2,2,8,512]{3,2,1,0:T(8,128)S(1)}, u32[]{:S(2)}, u32[]{:S(2)}) collective-permute-start(f32[2,2,8,512]{3,2,1,0:T(8,128)S(1)} %get-tuple-element.86), channel_id=1, source_target_pairs={{0,8},{2,10},{4,12},{6,14},{8,0},{10,2},{12,4},{14,6},{16,24},{18,... | collective-permute-start | bytes 196616 | tf_op jit(solution)/shard_map/ppermute | solution.py:564
  88.7 7.2 %collective-permute-start.22 = (f32[1,2,2,8,512]{4,3,2,1,0:T(8,128)S(1)}, f32[1,2,2,8,512]{4,3,2,1,0:T(8,128)S(1)}, u32[]{:S(2)}, u32[]{:S(2)}) collective-permute-start(f32[1,2,2,8,512]{4,3,2,1,0:T(8,128)S(1)} %get-tuple-element.96), channel_id=1, source_target_pairs={{0,16},{2,18},{4,20},{6,22},{8,24},{10,26},{12,28},{14,30},{16,0},... | collective-permute-start | bytes 196616 | tf_op jit(solution)/shard_map/ppermute | solution.py:556
  94.4 4.3 %collective-permute-start.18 = (f32[2,2,8,512]{3,2,1,0:T(8,128)S(1)}, f32[2,2,8,512]{3,2,1,0:T(8,128)S(1)}, u32[]{:S(2)}, u32[]{:S(2)}) collective-permute-start(f32[2,2,8,512]{3,2,1,0:T(8,128)S(1)} %advance_far.3.far_ref), channel_id=1, source_target_pairs={{0,1},{1,0},{2,3},{3,2},{4,5},{5,4},{6,7},{7,6},{8,9},{9,8},{10,11... | collective-permute-start | bytes 196616 | tf_op jit(solution)/shard_map/ppermute | solution.py:681
  102.4 9.1 %collective-permute-start.23 = (f32[8,2,2,8,512]{4,3,2,1,0:T(8,128)S(1)}, f32[8,2,2,8,512]{4,3,2,1,0:T(8,128)S(1)}, u32[]{:S(2)}, u32[]{:S(2)}) collective-permute-start(f32[8,2,2,8,512]{4,3,2,1,0:T(8,128)S(1)} %get-tuple-element.60), channel_id=1, source_target_pairs={{0,2},{2,0},{4,6},{6,4},{8,10},{10,8},{12,14},{14,12},{16,18},{18,... | collective-permute-start | bytes 1572872 | tf_op jit(solution)/shard_map/ppermute | solution.py:552
  102.5 5.9 %collective-permute-start.27 = (f32[2,2,2,8,512]{4,3,2,1,0:T(8,128)S(1)}, f32[2,2,2,8,512]{4,3,2,1,0:T(8,128)S(1)}, u32[]{:S(2)}, u32[]{:S(2)}) collective-permute-start(f32[2,2,2,8,512]{4,3,2,1,0:T(8,128)S(1)} %get-tuple-element.61), channel_id=1, source_target_pairs={{0,1},{1,0},{2,3},{3,2},{4,5},{5,4},{6,7},{7,6},{8,9},{9,8},{10,11... | collective-permute-start | bytes 393224 | tf_op jit(solution)/shard_map/ppermute | solution.py:650
  111.4 2.0 %collective-permute-start.28 = (f32[8,2,2,8,512]{4,3,2,1,0:T(8,128)S(1)}, f32[8,2,2,8,512]{4,3,2,1,0:T(8,128)S(1)}, u32[]{:S(2)}, u32[]{:S(2)}) collective-permute-start(f32[8,2,2,8,512]{4,3,2,1,0:T(8,128)S(1)} %get-tuple-element.63), channel_id=1, source_target_pairs={{0,2},{2,0},{4,6},{6,4},{8,10},{10,8},{12,14},{14,12},{16,18},{18,... | collective-permute-start | bytes 1572872 | tf_op jit(solution)/shard_map/ppermute | solution.py:552
  111.6 9.2 %collective-permute-start.24 = (f32[4,2,2,8,512]{4,3,2,1,0:T(8,128)S(1)}, f32[4,2,2,8,512]{4,3,2,1,0:T(8,128)S(1)}, u32[]{:S(2)}, u32[]{:S(2)}) collective-permute-start(f32[4,2,2,8,512]{4,3,2,1,0:T(8,128)S(1)} %get-tuple-element.67), channel_id=1, source_target_pairs={{0,4},{2,6},{4,0},{6,2},{8,12},{10,14},{12,8},{14,10},{16,20},{18,... | collective-permute-start | bytes 786440 | tf_op jit(solution)/shard_map/ppermute | solution.py:556
  113.5 12.5 %collective-permute-start.29 = (f32[4,2,2,8,512]{4,3,2,1,0:T(8,128)S(1)}, f32[4,2,2,8,512]{4,3,2,1,0:T(8,128)S(1)}, u32[]{:S(2)}, u32[]{:S(2)}) collective-permute-start(f32[4,2,2,8,512]{4,3,2,1,0:T(8,128)S(1)} %get-tuple-element.65), channel_id=1, source_target_pairs={{0,4},{2,6},{4,0},{6,2},{8,12},{10,14},{12,8},{14,10},{16,20},{18,... | collective-permute-start | bytes 786440 | tf_op jit(solution)/shard_map/ppermute | solution.py:556
  120.9 9.6 %collective-permute-start.25 = (f32[2,2,2,8,512]{4,3,2,1,0:T(8,128)S(1)}, f32[2,2,2,8,512]{4,3,2,1,0:T(8,128)S(1)}, u32[]{:S(2)}, u32[]{:S(2)}) collective-permute-start(f32[2,2,2,8,512]{4,3,2,1,0:T(8,128)S(1)} %get-tuple-element.81), channel_id=1, source_target_pairs={{0,8},{2,10},{4,12},{6,14},{8,0},{10,2},{12,4},{14,6},{16,24},{18,... | collective-permute-start | bytes 393224 | tf_op jit(solution)/shard_map/ppermute | solution.py:556
  126.0 6.5 %collective-permute-start.32 = (f32[2,2,8,512]{3,2,1,0:T(8,128)S(1)}, f32[2,2,8,512]{3,2,1,0:T(8,128)S(1)}, u32[]{:S(2)}, u32[]{:S(2)}) collective-permute-start(f32[2,2,8,512]{3,2,1,0:T(8,128)S(1)} %get-tuple-element.76), channel_id=1, source_target_pairs={{0,24},{2,26},{4,28},{6,30},{8,16},{10,18},{12,20},{14,22},{16,8},... | collective-permute-start | bytes 196616 | tf_op jit(solution)/shard_map/ppermute | solution.py:564
  128.0 8.5 %collective-permute-start.31 = (f32[2,2,8,512]{3,2,1,0:T(8,128)S(1)}, f32[2,2,8,512]{3,2,1,0:T(8,128)S(1)}, u32[]{:S(2)}, u32[]{:S(2)}) collective-permute-start(f32[2,2,8,512]{3,2,1,0:T(8,128)S(1)} %get-tuple-element.77), channel_id=1, source_target_pairs={{0,16},{2,18},{4,20},{6,22},{8,24},{10,26},{12,28},{14,30},{16,0},... | collective-permute-start | bytes 196616 | tf_op jit(solution)/shard_map/ppermute | solution.py:564
  128.3 8.2 %collective-permute-start.30 = (f32[2,2,8,512]{3,2,1,0:T(8,128)S(1)}, f32[2,2,8,512]{3,2,1,0:T(8,128)S(1)}, u32[]{:S(2)}, u32[]{:S(2)}) collective-permute-start(f32[2,2,8,512]{3,2,1,0:T(8,128)S(1)} %get-tuple-element.78), channel_id=1, source_target_pairs={{0,8},{2,10},{4,12},{6,14},{8,0},{10,2},{12,4},{14,6},{16,24},{18,... | collective-permute-start | bytes 196616 | tf_op jit(solution)/shard_map/ppermute | solution.py:564
  130.5 7.0 %collective-permute-start.26 = (f32[1,2,2,8,512]{4,3,2,1,0:T(8,128)S(1)}, f32[1,2,2,8,512]{4,3,2,1,0:T(8,128)S(1)}, u32[]{:S(2)}, u32[]{:S(2)}) collective-permute-start(f32[1,2,2,8,512]{4,3,2,1,0:T(8,128)S(1)} %get-tuple-element.94), channel_id=1, source_target_pairs={{0,16},{2,18},{4,20},{6,22},{8,24},{10,26},{12,28},{14,30},{16,0},... | collective-permute-start | bytes 196616 | tf_op jit(solution)/shard_map/ppermute | solution.py:556

commit v2 on v1

--- a/solution.py
+++ b/solution.py
@@ -304,7 +304,10 @@
     table_ref[...] = table_in_ref[...]
     twiddle_ref[...] = twiddle_in_ref[...]
     local_rows, all_times, k_local = causal_ref.shape[0], causal_ref.shape[1], energy_ref.shape[1]
-    energy_ref[...] = energies_ref[:, pl.ds(pl.multiple_of(ka * k_local, LANES), k_local)]
+    for side, begin in enumerate((ka * k_local, (1 - ka) * k_local)):
+        energy_ref[side : side + 1, :] = energies_ref[
+            :, pl.ds(pl.multiple_of(begin, LANES), k_local)
+        ]
     orbitals = onsite_ref.shape[1]
     halves = orbitals // 2
     for row in range(orbitals):
@@ -343,7 +346,7 @@
     )
 
 
-def rate_pieces(own_side, half, tile, onsite_ref, energy_ref, near_ref, far_ref, sums_refs):
+def rate_pieces(own_side, half, tile, onsite_ref, energy, near_ref, far_ref, sums_refs):
     halves = near_ref.shape[1]
     orbitals = 2 * halves
     lanes = pl.ds(tile * LANES, LANES)
@@ -351,7 +354,6 @@
     here = near_ref if own_side else far_ref
     real_part = functools.reduce(jnp.add, [ref[0, half, :, lanes] for ref in sums_refs])
     imag_part = functools.reduce(jnp.add, [ref[1, half, :, lanes] for ref in sums_refs])
-    energy = energy_ref[0:1, lanes]
     real_part = real_part + energy * here[0, half, :, lanes]
     imag_part = imag_part + energy * here[1, half, :, lanes]
     for side, ref in enumerate((near_ref, far_ref)):
@@ -366,62 +368,50 @@
     return imag_part, -real_part
 
 
-def advance_far_kernel(
-    is_first, sums_count, onsite_ref, energy_ref, near_ref, far_ref, green_ref, *refs
+def advance_kernel(
+    is_first, near_count, far_count, onsite_ref, energy_ref, near_here_ref, far_here_ref,
+    near_there_ref, far_there_ref, green_here_ref, green_there_ref, screens_ref, table_ref,
+    twiddle_ref, *refs
 ):
-    sums_refs, (first_ref, estimate_ref) = refs[:sums_count], refs[sums_count:]
-    halves, k_local = far_ref.shape[1], far_ref.shape[3]
-    for half in range(halves):
-        for tile in range(k_local // LANES):
-            lanes = pl.ds(tile * LANES, LANES)
-            rates = rate_pieces(
-                False, half, tile, onsite_ref, energy_ref, near_ref, far_ref, sums_refs
-            )
-            for plane in range(2):
-                start = green_ref[plane, half, :, lanes]
-                if is_first:
-                    first_ref[plane, half, :, lanes] = rates[plane]
-                    estimate_ref[plane, half, :, lanes] = start + time_step * rates[plane]
-                else:
-                    estimate_ref[plane, half, :, lanes] = start + 0.5 * time_step * (
-                        first_ref[plane, half, :, lanes] + rates[plane]
-                    )
-
-
-def advance_near_kernel(
-    is_first, sums_count, onsite_ref, energy_ref, near_ref, far_ref, green_ref,
-    arrived_ref, screens_ref, table_ref, twiddle_ref, *refs
-):
-    ka = lax.axis_index("ka")
-    sums_refs = refs[:sums_count]
-    first_ref, estimate_ref, sigma_ref, send_ref = refs[sums_count:]
-    halves, k_local = near_ref.shape[1], near_ref.shape[3]
+    sums_here, refs = refs[:near_count], refs[near_count:]
+    sums_there, refs = refs[:far_count], refs[far_count:]
+    first_here_ref, first_there_ref, estimate_ref, sigma_ref, send_ref = refs
+    halves, k_local = near_here_ref.shape[1], near_here_ref.shape[3]
     local_tiles = k_local // LANES
     fields = []
+    places = (
+        (0, near_here_ref, far_here_ref, green_here_ref, first_here_ref, sums_here),
+        (1, near_there_ref, far_there_ref, green_there_ref, first_there_ref, sums_there),
+    )
     for half in range(halves):
         parts = []
-        for tile in range(local_tiles):
-            lanes = pl.ds(tile * LANES, LANES)
-            rates = rate_pieces(
-                True, half, tile, onsite_ref, energy_ref, near_ref, far_ref, sums_refs
-            )
-            pair = []
-            for plane in range(2):
-                start = green_ref[plane, half, :, lanes]
-                if is_first:
-                    first_ref[plane, half, :, lanes] = rates[plane]
-                    value = start + time_step * rates[plane]
-                else:
-                    value = start + 0.5 * time_step * (
-                        first_ref[plane, half, :, lanes] + rates[plane]
-                    )
-                estimate_ref[plane, half, :, lanes] = value
-                pair.append(value)
-            parts.append(tuple(pair))
-        parts += tiles_of(lambda p, ds: arrived_ref[p, half, :, ds], local_tiles)
+        for side, near_ref, far_ref, green_ref, first_ref, sums_refs in places:
+            for tile in range(local_tiles):
+                lanes = pl.ds(tile * LANES, LANES)
+                energy = energy_ref[side : side + 1, lanes]
+                rates = rate_pieces(
+                    True, half, tile, onsite_ref, energy, near_ref, far_ref, sums_refs
+                )
+                pair = []
+                for plane in range(2):
+                    start = green_ref[plane, half, :, lanes]
+                    if is_first:
+                        first_ref[plane, half, :, lanes] = rates[plane]
+                        value = start + time_step * rates[plane]
+                    else:
+                        value = start + 0.5 * time_step * (
+                            first_ref[plane, half, :, lanes] + rates[plane]
+                        )
+                    estimate_ref[side, plane, half, :, lanes] = value
+                    if side == 1 and not is_first:
+                        estimate_ref[2, plane, half, :, lanes] = first_ref[plane, half, :, lanes]
+                    pair.append(value)
+                parts.append(tuple(pair))
         fields.append(parts)
     space = to_sites(fields, table_ref, twiddle_ref)
-    emit_sigma(ka, space, screens_ref, table_ref, twiddle_ref, sigma_ref, send_ref)
+    emit_sigma(
+        lax.axis_index("ka"), space, screens_ref, table_ref, twiddle_ref, sigma_ref, send_ref
+    )
 
 
 def closing_kernel(
@@ -440,8 +430,9 @@
         for half in range(halves):
             for tile in range(k_local // LANES):
                 lanes = pl.ds(tile * LANES, LANES)
+                energy = energy_ref[0:1, lanes]
                 rates = rate_pieces(
-                    own_side, half, tile, onsite_ref, energy_ref, near_ref, far_ref, sums_refs
+                    own_side, half, tile, onsite_ref, energy, near_ref, far_ref, sums_refs
                 )
                 for plane in range(2):
                     value = green_ref[plane, half, :, lanes] + 0.5 * time_step * (
@@ -548,21 +539,27 @@
     return [(place, place ^ bit) for place in range(count)]
 
 
-def halved_sum(keep, send, order, direct_bits, ta_count):
+def halved_sum(keep, send, order, direct_bits, ta_count, ka_count=None):
     got = lax.ppermute(send, "ta", flip(1 << order[0], ta_count))
     for bit in order[1 : len(order) - direct_bits]:
         half = keep.shape[0] // 2
-        outgoing = keep[half:] + got[half:]
-        arriving = lax.ppermute(outgoing, "ta", flip(1 << bit, ta_count))
-        keep, got = keep[:half] + got[:half], arriving
+        outgoing, keep = keep[half:] + got[half:], keep[:half] + got[:half]
+        got = lax.ppermute(outgoing, "ta", flip(1 << bit, ta_count))
     if direct_bits == 0:
         return keep[0], got[0]
     shift = order[-1]
     pieces = [keep[place] + got[place] for place in range(1 << direct_bits)]
     results = []
-    for place in range(1, 1 << direct_bits):
-        results.append(lax.ppermute(pieces[place], "ta", flip(place << shift, ta_count)))
-    return (pieces[0], *results)
+    for place in range(1 << direct_bits):
+        across = place << shift
+        if ka_count is not None:
+            pairs = flip(across * ka_count + 1, ta_count * ka_count)
+            results.append(lax.ppermute(pieces[place], ("ta", "ka"), pairs))
+        elif place == 0:
+            results.append(pieces[0])
+        else:
+            results.append(lax.ppermute(pieces[place], "ta", flip(across, ta_count)))
+    return tuple(results)
 
 
 def fast(
@@ -602,7 +599,7 @@
         stage_kernel,
         out_shape=(
             float_like(local_rows, all_times, LANES),
-            float_like(1, k_local),
+            float_like(2, k_local),
             float_like(2 * orbitals * orbitals, LANES),
             jax.ShapeDtypeStruct(table.shape, table.dtype),
             jax.ShapeDtypeStruct(twiddle.shape, twiddle.dtype),
@@ -613,7 +610,7 @@
         cost_estimate=hint,
         name="stage",
     )(block_table, onsite, energies, table, twiddle)
-    green_near, green_far = near_fields[2], far_fields[2]
+    green_near, green_far, green_there = near_fields[2], far_fields[2], arrived_fields[2]
 
     screens, sigma_near, sigma_send = pl.pallas_call(
         opening_kernel,
@@ -627,11 +624,10 @@
 
     bits = ta_count.bit_length() - 1
     owner_bits = orbitals.bit_length() - 1
-    near_order = list(range(bits))
-    far_order = list(range(owner_bits)) + list(range(owner_bits, bits))[::-1]
+    order = list(range(owner_bits)) + list(range(owner_bits, bits))[::-1]
     direct_bits = bits - owner_bits
 
-    def collide(sigma, order):
+    def collide(sigma):
         return pl.pallas_call(
             functools.partial(collide_kernel, order),
             out_shape=(float_like(ta_count // 2, *chunk),) * 2,
@@ -646,53 +642,53 @@
             name="collide",
         )(sigma, causal, lesser_slab, advanced_slab)
 
-    def collisions(sigma_near, sigma_send):
-        sigma_far = lax.ppermute(sigma_send, "ka", flip(1, ka_count))
-        near = collide(sigma_near, near_order)
-        far = collide(sigma_far, far_order)
-        near_sums = halved_sum(*near, near_order, 0, ta_count)
-        far_sums = halved_sum(*far, far_order, direct_bits, ta_count)
+    def exchanged(value):
+        return lax.ppermute(value, "ka", flip(1, ka_count))
+
+    def collisions(sigma_near, sigma_send, crossing):
+        sigma_far = exchanged(sigma_send)
+        near = collide(sigma_near)
+        far = collide(sigma_far)
+        near_sums = halved_sum(*near, order, 0, ta_count)
+        far_sums = halved_sum(*far, order, direct_bits, ta_count, crossing)
         return near_sums, far_sums
 
-    estimate_near, estimate_far = green_near, green_far
-    first_near = first_far = None
     chunk_shape = float_like(*chunk)
+    near_here, near_there, far_here = green_near, green_there, green_far
+    far_there = None
+    first_here = first_there = None
     for corrector in range(2):
         is_first = corrector == 0
-        near_sums, far_sums = collisions(sigma_near, sigma_send)
-        common = (onsite, energy, estimate_near, estimate_far)
-        tables = (screens, table, twiddle)
+        near_sums, far_sums = collisions(sigma_near, sigma_send, ka_count)
         if is_first:
-            far_out, near_out = (chunk_shape,) * 2, (chunk_shape,) * 2
-            extra_far, extra_near = (), ()
+            far_there = exchanged(green_near)
         else:
-            far_out, near_out = (chunk_shape,), (chunk_shape,)
-            extra_far, extra_near = (first_far,), (first_near,)
-        near_out = near_out + (sigma_shape,) * 2
-        far_inputs = common + (green_far,) + far_sums + extra_far
-        far_result = pl.pallas_call(
-            functools.partial(advance_far_kernel, is_first, len(far_sums)),
-            out_shape=far_out,
-            in_specs=[whole()] * len(far_inputs),
-            out_specs=(whole(),) * len(far_out),
+            swapped = exchanged(estimate)
+            far_here, far_there = swapped[1], swapped[0]
+        outputs = (float_like(2 if is_first else 3, *chunk), sigma_shape, sigma_shape)
+        inputs = (
+            onsite, energy, near_here, far_here, near_there, far_there, green_near,
+            green_there, screens, table, twiddle, *near_sums, *far_sums,
+        )
+        if is_first:
+            outputs = (chunk_shape,) * 2 + outputs
+        else:
+            inputs = inputs + (first_here, first_there)
+        result = pl.pallas_call(
+            functools.partial(advance_kernel, is_first, len(near_sums), len(far_sums)),
+            out_shape=outputs,
+            in_specs=[whole()] * len(inputs),
+            out_specs=(whole(),) * len(outputs),
             compiler_params=small,
-            name="advance_far",
-        )(*far_inputs)
-        arrived = lax.ppermute(far_result[-1], "ka", flip(1, ka_count))
-        near_inputs = common + (green_near, arrived) + tables + near_sums + extra_near
-        near_result = pl.pallas_call(
-            functools.partial(advance_near_kernel, is_first, len(near_sums)),
-            out_shape=near_out,
-            in_specs=[whole()] * len(near_inputs),
-            out_specs=(whole(),) * len(near_out),
-            compiler_params=small,
-            name="advance_near",
-        )(*near_inputs)
+            name="advance",
+        )(*inputs)
         if is_first:
-            first_far, first_near = far_result[0], near_result[0]
-        estimate_far = far_result[-1]
-        estimate_near, sigma_near, sigma_send = near_result[-3:]
-    near_sums, far_sums = collisions(sigma_near, sigma_send)
+            first_here, first_there = result[:2]
+        estimate, sigma_near, sigma_send = result[-3:]
+        near_here, near_there = estimate[0], estimate[1]
+    near_sums, far_sums = collisions(sigma_near, sigma_send, None)
+    swapped = exchanged(estimate[1:])
+    far_here, first_far = swapped[0], swapped[1]
     full = float_like(*green_row.shape)
     return pl.pallas_call(
         functools.partial(closing_kernel, len(near_sums), len(far_sums)),
@@ -702,8 +698,8 @@
         compiler_params=small,
         name="closing",
     )(
-        onsite, energy, estimate_near, estimate_far, green_near, green_far, first_near,
-        first_far, *near_sums, *far_sums,
+        onsite, energy, near_here, far_here, green_near, green_far, first_here, first_far,
+        *near_sums, *far_sums,
     )
 
 

time: 139 us -> 143 us (1.029)
  waiting for transfers between devices: 61.6 us -> 63.8 us
  starting transfers between devices: 43.3 us -> 44.8 us
    ppermute x26 -> x29, waiting for transfers between devices: 60.8 us -> 62.9 us  [the longest x12 33.4 us: halved_sum(): got = lax.ppermute(outgoing, 'ta', flip(1 << bit, ta_count))]
    ppermute x26 -> x29, starting transfers between devices: 39.9 us -> 41.4 us  [the longest x12 15.1 us: halved_sum(): got = lax.ppermute(outgoing, 'ta', flip(1 << bit, ta_count))]
  transfers between devices with their start and end apart: 33 -> 36, of which waited for: 19 -> 17; matrix products, arithmetic and copies ran while one was open for 1% -> 1% of each run, Pallas kernels for 7% -> 7%
where the time goes in v2:
time: 143 us; the launch traced here: 142 us
  waiting for transfers between devices  63.8 us (45%)
  starting transfers between devices  44.8 us (31%)
  Pallas kernels  22.1 us (15%)
  local copies, waits for them, and re-layouts  8.93 us (6%)
  between operations  1.65 us (1%)
    ppermute x12, waiting for transfers between devices, halved_sum(): got = lax.ppermute(outgoing, 'ta', flip(1 << bit, ta_count))  33.4 us
    pallas_call x6, Pallas kernels, collide(): pl.pallas_call(functools.partial(collide_kernel, order), out_shape=(float...  18.5 us
    ppermute x12, starting transfers between devices, halved_sum(): got = lax.ppermute(outgoing, 'ta', flip(1 << bit, ta_count))  15.1 us
    ppermute x6, waiting for transfers between devices, exchanged(): return lax.ppermute(value, 'ka', flip(1, ka_count))  14.7 us
    ppermute x8, starting transfers between devices, halved_sum(): results.append(lax.ppermute(pieces[place], ('ta', 'ka'), pairs))  14.1 us
    ppermute x8, waiting for transfers between devices, halved_sum(): results.append(lax.ppermute(pieces[place], ('ta', 'ka'), pairs))  10.2 us
    unnamed x22, local copies, waits for them, and re-layouts  8.87 us
    ppermute x6, starting transfers between devices, exchanged(): return lax.ppermute(value, 'ka', flip(1, ka_count))  7.67 us
  transfers between devices with their start and end apart: 36, of which 17 were waited for; matrix products, arithmetic and copies ran while one was open for 1% of the time, Pallas kernels for 7%

profile of v2, /device:TPU:0, one launch (start us, length us, event | category | flops | bytes accessed | tf_op | source)
XLA Modules:
  0.0 142.2 jit_solution(4481719539625916371)
XLA Ops:
  0.6 0.9 copy-done.5
  1.5 0.9 copy-done.6
  2.4 0.9 copy-done.7
  3.5 3.0 %collective-permute-start = (f32[3,2,2,8,512]{4,3,2,1,0:T(8,128)S(1)}, f32[3,2,2,8,512]{4,3,2,1,0:T(8,128)S(1)}, u32[]{:S(2)}, u32[]{:S(2)}) collective-permute-start(f32[3,2,2,8,512]{4,3,2,1,0:T(8,128)S(1)} %get-tuple-element.35), channel_id=1, source_target_pairs={{0,1},{1,0},{2,3},{3,2},{4,5},{5,4},{6,7},{7,6},{8,9},{9,8},{10,11... | collective-permute-start | bytes 589832 | tf_op jit(solution)/shard_map/ppermute | solution.py:597
  7.3 0.9 copy-done.4
  12.1 1.6 %copy-done = bf16[2,4,4,2,32,512]{5,4,3,2,1,0:T(8,128)(2,1)S(1)} copy-done((bf16[2,4,4,2,32,512]{5,4,3,2,1,0:T(8,128)(2,1)S(1)}, bf16[2,4,4,2,32,512]{5,4,3,2,1,0:T(8,128)(2,1)}, u32[]{:S(2)}) %copy-start) | copy-done | bytes 2097176
  13.7 1.6 %copy-done.2 = bf16[2,4,4,2,32,512]{5,4,3,2,1,0:T(8,128)(2,1)S(1)} copy-done((bf16[2,4,4,2,32,512]{5,4,3,2,1,0:T(8,128)(2,1)S(1)}, bf16[2,4,4,2,32,512]{5,4,3,2,1,0:T(8,128)(2,1)}, u32[]{:S(2)}) %copy-start.2) | copy-done | bytes 2097176
  15.3 3.1 %collide.6 = (f32[8,2,2,8,512]{4,3,2,1,0:T(8,128)S(1)}, f32[8,2,2,8,512]{4,3,2,1,0:T(8,128)S(1)}) custom-call(f32[2,2,2,8,512]{4,3,2,1,0:T(8,128)S(1)} %get-tuple-element.39.sigma_ref, f32[2,32,128]{2,1,0:T(8,128)S(1)} %get-tuple-element.40.causal_ref, bf16[2,4,4,2,32,512]{5,4,3,2,1,0:T(8,128)(2,1)S(1)} %copy-done, bf16[2,4,4,2,32,512]{5,4,3,2,1,0:T(8,128)(2,1)S(1)} %copy-done.2), custom_call_target="tpu_custom_call" | custom-call | flops 16777216 | bytes 4194304 | tf_op jit(solution)/shard_map/collide/pallas_call | solution.py:631
  18.4 1.8 %collective-permute-start.6 = (f32[2,2,2,8,512]{4,3,2,1,0:T(8,128)S(1)}, f32[2,2,2,8,512]{4,3,2,1,0:T(8,128)S(1)}, u32[]{:S(2)}, u32[]{:S(2)}) collective-permute-start(f32[2,2,2,8,512]{4,3,2,1,0:T(8,128)S(1)} %get-tuple-element.43), channel_id=1, source_target_pairs={{0,1},{1,0},{2,3},{3,2},{4,5},{5,4},{6,7},{7,6},{8,9},{9,8},{10,11... | collective-permute-start | bytes 393224 | tf_op jit(solution)/shard_map/ppermute | solution.py:646
  20.2 4.1 %collective-permute-done.6.sigma_ref = f32[2,2,2,8,512]{4,3,2,1,0:T(8,128)S(1)} collective-permute-done((f32[2,2,2,8,512]{4,3,2,1,0:T(8,128)S(1)}, f32[2,2,2,8,512]{4,3,2,1,0:T(8,128)S(1)}, u32[]{:S(2)}, u32[]{:S(2)}) %collective-permute-start.6) | collective-permute-done | bytes 131104 | tf_op jit(solution)/shard_map/ppermute | solution.py:646
  24.3 3.1 %collide.7 = (f32[8,2,2,8,512]{4,3,2,1,0:T(8,128)S(1)}, f32[8,2,2,8,512]{4,3,2,1,0:T(8,128)S(1)}) custom-call(f32[2,2,2,8,512]{4,3,2,1,0:T(8,128)S(1)} %collective-permute-done.6.sigma_ref, f32[2,32,128]{2,1,0:T(8,128)S(1)} %get-tuple-element.40.causal_ref, bf16[2,4,4,2,32,512]{5,4,3,2,1,0:T(8,128)(2,1)S(1)} %copy-done.1, ...), custom_call_target="tpu_custom_call" | custom-call | flops 16777216 | bytes 4194304 | tf_op jit(solution)/shard_map/collide/pallas_call | solution.py:631
  27.6 1.8 %collective-permute-start.3 = (f32[4,2,2,8,512]{4,3,2,1,0:T(8,128)S(1)}, f32[4,2,2,8,512]{4,3,2,1,0:T(8,128)S(1)}, u32[]{:S(2)}, u32[]{:S(2)}) collective-permute-start(f32[4,2,2,8,512]{4,3,2,1,0:T(8,128)S(1)} %get-tuple-element.73), channel_id=1, source_target_pairs={{0,4},{2,6},{4,0},{6,2},{8,12},{10,14},{12,8},{14,10},{16,20},{18,... | collective-permute-start | bytes 786440 | tf_op jit(solution)/shard_map/ppermute | solution.py:547
  29.4 1.5 %collective-permute-start.1 = (f32[2,2,8,512]{3,2,1,0:T(8,128)S(1)}, f32[2,2,8,512]{3,2,1,0:T(8,128)S(1)}, u32[]{:S(2)}, u32[]{:S(2)}) collective-permute-start(f32[2,2,8,512]{3,2,1,0:T(8,128)S(1)} %slice_bitcast_fusion.9.near_here_ref.green_here_ref.green_near_ref), channel_id=1, source_target_pairs={{0,1},{1,0},{2,3},{3,2},{4,5},{5,4},{6,7},{7,6},{8,9},{9,8},{10,11... | collective-permute-start | bytes 196616 | tf_op jit(solution)/shard_map/ppermute | solution.py:646
  31.6 5.2 %collective-permute-done.3 = f32[4,2,2,8,512]{4,3,2,1,0:T(8,128)S(1)} collective-permute-done((f32[4,2,2,8,512]{4,3,2,1,0:T(8,128)S(1)}, f32[4,2,2,8,512]{4,3,2,1,0:T(8,128)S(1)}, u32[]{:S(2)}, u32[]{:S(2)}) %collective-permute-start.3) | collective-permute-done | bytes 262176 | tf_op jit(solution)/shard_map/ppermute | solution.py:547
  36.9 2.9 %collective-permute-start.4 = (f32[2,2,2,8,512]{4,3,2,1,0:T(8,128)S(1)}, f32[2,2,2,8,512]{4,3,2,1,0:T(8,128)S(1)}, u32[]{:S(2)}, u32[]{:S(2)}) collective-permute-start(f32[2,2,2,8,512]{4,3,2,1,0:T(8,128)S(1)} %get-tuple-element.91), channel_id=1, source_target_pairs={{0,16},{2,18},{4,20},{6,22},{8,24},{10,26},{12,28},{14,30},{16,0},... | collective-permute-start | bytes 393224 | tf_op jit(solution)/shard_map/ppermute | solution.py:547
  39.8 5.6 %collective-permute-done.4 = f32[2,2,2,8,512]{4,3,2,1,0:T(8,128)S(1)} collective-permute-done((f32[2,2,2,8,512]{4,3,2,1,0:T(8,128)S(1)}, f32[2,2,2,8,512]{4,3,2,1,0:T(8,128)S(1)}, u32[]{:S(2)}, u32[]{:S(2)}) %collective-permute-start.4) | collective-permute-done | bytes 131104 | tf_op jit(solution)/shard_map/ppermute | solution.py:547
  45.4 0.8 collective-permute-start.5
  46.2 1.6 %collective-permute-start.9 = (f32[2,2,8,512]{3,2,1,0:T(8,128)S(1)}, f32[2,2,8,512]{3,2,1,0:T(8,128)S(1)}, u32[]{:S(2)}, u32[]{:S(2)}) collective-permute-start(f32[2,2,8,512]{3,2,1,0:T(8,128)S(1)} %get-tuple-element.89), channel_id=1, source_target_pairs={{0,1},{1,0},{2,3},{3,2},{4,5},{5,4},{6,7},{7,6},{8,9},{9,8},{10,11... | collective-permute-start | bytes 196616 | tf_op jit(solution)/shard_map/ppermute | solution.py:557
  47.8 1.3 collective-permute-start.10
  49.1 3.0 %collective-permute-start.11 = (f32[2,2,8,512]{3,2,1,0:T(8,128)S(1)}, f32[2,2,8,512]{3,2,1,0:T(8,128)S(1)}, u32[]{:S(2)}, u32[]{:S(2)}) collective-permute-start(f32[2,2,8,512]{3,2,1,0:T(8,128)S(1)} %get-tuple-element.87), channel_id=1, source_target_pairs={{0,17},{1,16},{2,19},{3,18},{4,21},{5,20},{6,23},{7,22},{8,25},{9,... | collective-permute-start | bytes 196616 | tf_op jit(solution)/shard_map/ppermute | solution.py:557
  52.1 1.4 %collective-permute-start.12 = (f32[2,2,8,512]{3,2,1,0:T(8,128)S(1)}, f32[2,2,8,512]{3,2,1,0:T(8,128)S(1)}, u32[]{:S(2)}, u32[]{:S(2)}) collective-permute-start(f32[2,2,8,512]{3,2,1,0:T(8,128)S(1)} %get-tuple-element.86), channel_id=1, source_target_pairs={{0,25},{1,24},{2,27},{3,26},{4,29},{5,28},{6,31},{7,30},{8,17},{9,... | collective-permute-start | bytes 196616 | tf_op jit(solution)/shard_map/ppermute | solution.py:557
  53.6 1.8 %collective-permute-done.11.refs_4_ = f32[2,2,8,512]{3,2,1,0:T(8,128)S(1)} collective-permute-done((f32[2,2,8,512]{3,2,1,0:T(8,128)S(1)}, f32[2,2,8,512]{3,2,1,0:T(8,128)S(1)}, u32[]{:S(2)}, u32[]{:S(2)}) %collective-permute-start.11) | collective-permute-done | bytes 65568 | tf_op jit(solution)/shard_map/ppermute | solution.py:557
  55.4 3.8 %collective-permute-done.12.refs_5_ = f32[2,2,8,512]{3,2,1,0:T(8,128)S(1)} collective-permute-done((f32[2,2,8,512]{3,2,1,0:T(8,128)S(1)}, f32[2,2,8,512]{3,2,1,0:T(8,128)S(1)}, u32[]{:S(2)}, u32[]{:S(2)}) %collective-permute-start.12) | collective-permute-done | bytes 65568 | tf_op jit(solution)/shard_map/ppermute | solution.py:557
  59.8 3.1 %collide.8 = (f32[8,2,2,8,512]{4,3,2,1,0:T(8,128)S(1)}, f32[8,2,2,8,512]{4,3,2,1,0:T(8,128)S(1)}) custom-call(f32[2,2,2,8,512]{4,3,2,1,0:T(8,128)S(1)} %get-tuple-element.47.sigma_ref, f32[2,32,128]{2,1,0:T(8,128)S(1)} %get-tuple-element.40.causal_ref, bf16[2,4,4,2,32,512]{5,4,3,2,1,0:T(8,128)(2,1)S(1)} %copy-done.1, ...), custom_call_target="tpu_custom_call" | custom-call | flops 16777216 | bytes 4194304 | tf_op jit(solution)/shard_map/collide/pallas_call | solution.py:631
  63.6 5.3 %collective-permute-done.18.sigma_ref = f32[2,2,2,8,512]{4,3,2,1,0:T(8,128)S(1)} collective-permute-done((f32[2,2,2,8,512]{4,3,2,1,0:T(8,128)S(1)}, f32[2,2,2,8,512]{4,3,2,1,0:T(8,128)S(1)}, u32[]{:S(2)}, u32[]{:S(2)}) %collective-permute-start.18) | collective-permute-done | bytes 131104 | tf_op jit(solution)/shard_map/ppermute | solution.py:646
  68.9 3.1 %collide.9 = (f32[8,2,2,8,512]{4,3,2,1,0:T(8,128)S(1)}, f32[8,2,2,8,512]{4,3,2,1,0:T(8,128)S(1)}) custom-call(f32[2,2,2,8,512]{4,3,2,1,0:T(8,128)S(1)} %collective-permute-done.18.sigma_ref, f32[2,32,128]{2,1,0:T(8,128)S(1)} %get-tuple-element.40.causal_ref, bf16[2,4,4,2,32,512]{5,4,3,2,1,0:T(8,128)(2,1)S(1)} %copy-done.1, ...), custom_call_target="tpu_custom_call" | custom-call | flops 16777216 | bytes 4194304 | tf_op jit(solution)/shard_map/collide/pallas_call | solution.py:631
  72.1 1.6 %collective-permute-start.15 = (f32[4,2,2,8,512]{4,3,2,1,0:T(8,128)S(1)}, f32[4,2,2,8,512]{4,3,2,1,0:T(8,128)S(1)}, u32[]{:S(2)}, u32[]{:S(2)}) collective-permute-start(f32[4,2,2,8,512]{4,3,2,1,0:T(8,128)S(1)} %get-tuple-element.69), channel_id=1, source_target_pairs={{0,4},{2,6},{4,0},{6,2},{8,12},{10,14},{12,8},{14,10},{16,20},{18,... | collective-permute-start | bytes 786440 | tf_op jit(solution)/shard_map/ppermute | solution.py:547
  74.0 1.6 %collective-permute-start.20 = (f32[4,2,2,8,512]{4,3,2,1,0:T(8,128)S(1)}, f32[4,2,2,8,512]{4,3,2,1,0:T(8,128)S(1)}, u32[]{:S(2)}, u32[]{:S(2)}) collective-permute-start(f32[4,2,2,8,512]{4,3,2,1,0:T(8,128)S(1)} %get-tuple-element.67), channel_id=1, source_target_pairs={{0,4},{2,6},{4,0},{6,2},{8,12},{10,14},{12,8},{14,10},{16,20},{18,... | collective-permute-start | bytes 786440 | tf_op jit(solution)/shard_map/ppermute | solution.py:547
  75.6 5.8 %collective-permute-done.15 = f32[4,2,2,8,512]{4,3,2,1,0:T(8,128)S(1)} collective-permute-done((f32[4,2,2,8,512]{4,3,2,1,0:T(8,128)S(1)}, f32[4,2,2,8,512]{4,3,2,1,0:T(8,128)S(1)}, u32[]{:S(2)}, u32[]{:S(2)}) %collective-permute-start.15) | collective-permute-done | bytes 262176 | tf_op jit(solution)/shard_map/ppermute | solution.py:547
  81.4 1.4 collective-permute-start.16
  82.8 1.4 %collective-permute-start.13 = (f32[2,2,2,8,512]{4,3,2,1,0:T(8,128)S(1)}, f32[2,2,2,8,512]{4,3,2,1,0:T(8,128)S(1)}, u32[]{:S(2)}, u32[]{:S(2)}) collective-permute-start(f32[2,2,2,8,512]{4,3,2,1,0:T(8,128)S(1)} %get-tuple-element.46), channel_id=1, source_target_pairs={{0,1},{1,0},{2,3},{3,2},{4,5},{5,4},{6,7},{7,6},{8,9},{9,8},{10,11... | collective-permute-start | bytes 393224 | tf_op jit(solution)/shard_map/ppermute | solution.py:646
  84.2 5.5 %collective-permute-done.16 = f32[2,2,2,8,512]{4,3,2,1,0:T(8,128)S(1)} collective-permute-done((f32[2,2,2,8,512]{4,3,2,1,0:T(8,128)S(1)}, f32[2,2,2,8,512]{4,3,2,1,0:T(8,128)S(1)}, u32[]{:S(2)}, u32[]{:S(2)}) %collective-permute-start.16) | collective-permute-done | bytes 131104 | tf_op jit(solution)/shard_map/ppermute | solution.py:547
  90.5 2.9 %collective-permute-start.22 = (f32[2,2,8,512]{3,2,1,0:T(8,128)S(1)}, f32[2,2,8,512]{3,2,1,0:T(8,128)S(1)}, u32[]{:S(2)}, u32[]{:S(2)}) collective-permute-start(f32[2,2,8,512]{3,2,1,0:T(8,128)S(1)} %get-tuple-element.82), channel_id=1, source_target_pairs={{0,9},{1,8},{2,11},{3,10},{4,13},{5,12},{6,15},{7,14},{8,1},{9,0},... | collective-permute-start | bytes 196616 | tf_op jit(solution)/shard_map/ppermute | solution.py:557
  94.0 2.7 %collective-permute-start.24 = (f32[2,2,8,512]{3,2,1,0:T(8,128)S(1)}, f32[2,2,8,512]{3,2,1,0:T(8,128)S(1)}, u32[]{:S(2)}, u32[]{:S(2)}) collective-permute-start(f32[2,2,8,512]{3,2,1,0:T(8,128)S(1)} %get-tuple-element.80), channel_id=1, source_target_pairs={{0,25},{1,24},{2,27},{3,26},{4,29},{5,28},{6,31},{7,30},{8,17},{9,... | collective-permute-start | bytes 196616 | tf_op jit(solution)/shard_map/ppermute | solution.py:557
  96.8 4.6 %collective-permute-done.23.refs_4_ = f32[2,2,8,512]{3,2,1,0:T(8,128)S(1)} collective-permute-done((f32[2,2,8,512]{3,2,1,0:T(8,128)S(1)}, f32[2,2,8,512]{3,2,1,0:T(8,128)S(1)}, u32[]{:S(2)}, u32[]{:S(2)}) %collective-permute-start.23) | collective-permute-done | bytes 65568 | tf_op jit(solution)/shard_map/ppermute | solution.py:557
  102.0 3.1 %collide.10 = (f32[8,2,2,8,512]{4,3,2,1,0:T(8,128)S(1)}, f32[8,2,2,8,512]{4,3,2,1,0:T(8,128)S(1)}) custom-call(f32[2,2,2,8,512]{4,3,2,1,0:T(8,128)S(1)} %get-tuple-element.56.sigma_ref, f32[2,32,128]{2,1,0:T(8,128)S(1)} %get-tuple-element.40.causal_ref, bf16[2,4,4,2,32,512]{5,4,3,2,1,0:T(8,128)(2,1)S(1)} %copy-done.1, ...), custom_call_target="tpu_custom_call" | custom-call | flops 16777216 | bytes 4194304 | tf_op jit(solution)/shard_map/collide/pallas_call | solution.py:631
  105.8 5.3 %collective-permute-done.30.sigma_ref = f32[2,2,2,8,512]{4,3,2,1,0:T(8,128)S(1)} collective-permute-done((f32[2,2,2,8,512]{4,3,2,1,0:T(8,128)S(1)}, f32[2,2,2,8,512]{4,3,2,1,0:T(8,128)S(1)}, u32[]{:S(2)}, u32[]{:S(2)}) %collective-permute-start.30) | collective-permute-done | bytes 131104 | tf_op jit(solution)/shard_map/ppermute | solution.py:646
  111.1 3.1 %collide.11 = (f32[8,2,2,8,512]{4,3,2,1,0:T(8,128)S(1)}, f32[8,2,2,8,512]{4,3,2,1,0:T(8,128)S(1)}) custom-call(f32[2,2,2,8,512]{4,3,2,1,0:T(8,128)S(1)} %collective-permute-done.30.sigma_ref, f32[2,32,128]{2,1,0:T(8,128)S(1)} %get-tuple-element.40.causal_ref, bf16[2,4,4,2,32,512]{5,4,3,2,1,0:T(8,128)(2,1)S(1)} %copy-done.1, ...), custom_call_target="tpu_custom_call" | custom-call | flops 16777216 | bytes 4194304 | tf_op jit(solution)/shard_map/collide/pallas_call | solution.py:631
  114.3 1.6 %collective-permute-start.27 = (f32[4,2,2,8,512]{4,3,2,1,0:T(8,128)S(1)}, f32[4,2,2,8,512]{4,3,2,1,0:T(8,128)S(1)}, u32[]{:S(2)}, u32[]{:S(2)}) collective-permute-start(f32[4,2,2,8,512]{4,3,2,1,0:T(8,128)S(1)} %get-tuple-element.65), channel_id=1, source_target_pairs={{0,4},{2,6},{4,0},{6,2},{8,12},{10,14},{12,8},{14,10},{16,20},{18,... | collective-permute-start | bytes 786440 | tf_op jit(solution)/shard_map/ppermute | solution.py:547
  116.2 1.6 %collective-permute-start.32 = (f32[4,2,2,8,512]{4,3,2,1,0:T(8,128)S(1)}, f32[4,2,2,8,512]{4,3,2,1,0:T(8,128)S(1)}, u32[]{:S(2)}, u32[]{:S(2)}) collective-permute-start(f32[4,2,2,8,512]{4,3,2,1,0:T(8,128)S(1)} %get-tuple-element.63), channel_id=1, source_target_pairs={{0,4},{2,6},{4,0},{6,2},{8,12},{10,14},{12,8},{14,10},{16,20},{18,... | collective-permute-start | bytes 786440 | tf_op jit(solution)/shard_map/ppermute | solution.py:547
  117.8 5.8 %collective-permute-done.27 = f32[4,2,2,8,512]{4,3,2,1,0:T(8,128)S(1)} collective-permute-done((f32[4,2,2,8,512]{4,3,2,1,0:T(8,128)S(1)}, f32[4,2,2,8,512]{4,3,2,1,0:T(8,128)S(1)}, u32[]{:S(2)}, u32[]{:S(2)}) %collective-permute-start.27) | collective-permute-done | bytes 262176 | tf_op jit(solution)/shard_map/ppermute | solution.py:547
  123.6 1.2 collective-permute-start.28
  124.8 1.7 %collective-permute-start.25 = (f32[2,2,2,8,512]{4,3,2,1,0:T(8,128)S(1)}, f32[2,2,2,8,512]{4,3,2,1,0:T(8,128)S(1)}, u32[]{:S(2)}, u32[]{:S(2)}) collective-permute-start(f32[2,2,2,8,512]{4,3,2,1,0:T(8,128)S(1)} %slice.305), channel_id=1, source_target_pairs={{0,1},{1,0},{2,3},{3,2},{4,5},{5,4},{6,7},{7,6},{8,9},{9,8},{10,11... | collective-permute-start | bytes 393224 | tf_op jit(solution)/shard_map/ppermute | solution.py:646
  126.5 5.4 %collective-permute-done.28 = f32[2,2,2,8,512]{4,3,2,1,0:T(8,128)S(1)} collective-permute-done((f32[2,2,2,8,512]{4,3,2,1,0:T(8,128)S(1)}, f32[2,2,2,8,512]{4,3,2,1,0:T(8,128)S(1)}, u32[]{:S(2)}, u32[]{:S(2)}) %collective-permute-start.28) | collective-permute-done | bytes 131104 | tf_op jit(solution)/shard_map/ppermute | solution.py:547
  132.1 2.1 %collective-permute-start.33 = (f32[2,2,8,512]{3,2,1,0:T(8,128)S(1)}, f32[2,2,8,512]{3,2,1,0:T(8,128)S(1)}, u32[]{:S(2)}, u32[]{:S(2)}) collective-permute-start(f32[2,2,8,512]{3,2,1,0:T(8,128)S(1)} %get-tuple-element.76), channel_id=1, source_target_pairs={{0,8},{2,10},{4,12},{6,14},{8,0},{10,2},{12,4},{14,6},{16,24},{18,... | collective-permute-start | bytes 196616 | tf_op jit(solution)/shard_map/ppermute | solution.py:561
  134.3 2.3 %collective-permute-start.35 = (f32[2,2,8,512]{3,2,1,0:T(8,128)S(1)}, f32[2,2,8,512]{3,2,1,0:T(8,128)S(1)}, u32[]{:S(2)}, u32[]{:S(2)}) collective-permute-start(f32[2,2,8,512]{3,2,1,0:T(8,128)S(1)} %get-tuple-element.74), channel_id=1, source_target_pairs={{0,24},{2,26},{4,28},{6,30},{8,16},{10,18},{12,20},{14,22},{16,8},... | collective-permute-start | bytes 196616 | tf_op jit(solution)/shard_map/ppermute | solution.py:561
  137.2 4.1 %collective-permute-done.34.refs_4_ = f32[2,2,8,512]{3,2,1,0:T(8,128)S(1)} collective-permute-done((f32[2,2,8,512]{3,2,1,0:T(8,128)S(1)}, f32[2,2,8,512]{3,2,1,0:T(8,128)S(1)}, u32[]{:S(2)}, u32[]{:S(2)}) %collective-permute-start.34) | collective-permute-done | bytes 65568 | tf_op jit(solution)/shard_map/ppermute | solution.py:561
  141.3 0.9 closing.1
  (83 shorter events, 10.9 us)
Async XLA Ops:
  0.6 0.9 copy-start.5
  1.5 0.9 copy-start.6
  2.4 0.9 copy-start.7
  3.5 7.9 %collective-permute-start = (f32[3,2,2,8,512]{4,3,2,1,0:T(8,128)S(1)}, f32[3,2,2,8,512]{4,3,2,1,0:T(8,128)S(1)}, u32[]{:S(2)}, u32[]{:S(2)}) collective-permute-start(f32[3,2,2,8,512]{4,3,2,1,0:T(8,128)S(1)} %get-tuple-element.35), channel_id=1, source_target_pairs={{0,1},{1,0},{2,3},{3,2},{4,5},{5,4},{6,7},{7,6},{8,9},{9,8},{10,11... | collective-permute-start | bytes 589832 | tf_op jit(solution)/shard_map/ppermute | solution.py:597
  7.3 1.0 copy-start.4
  8.2 0.7 copy-start.8
  8.9 0.7 copy-start.9
  9.6 0.7 copy-start.10
  12.1 1.6 %copy-start = (bf16[2,4,4,2,32,512]{5,4,3,2,1,0:T(8,128)(2,1)S(1)}, bf16[2,4,4,2,32,512]{5,4,3,2,1,0:T(8,128)(2,1)}, u32[]{:S(2)}) copy-start(bf16[2,4,4,2,32,512]{5,4,3,2,1,0:T(8,128)(2,1)} %lesser_ref.13) | copy-start | bytes 6291460
  13.7 1.6 %copy-start.2 = (bf16[2,4,4,2,32,512]{5,4,3,2,1,0:T(8,128)(2,1)S(1)}, bf16[2,4,4,2,32,512]{5,4,3,2,1,0:T(8,128)(2,1)}, u32[]{:S(2)}) copy-start(bf16[2,4,4,2,32,512]{5,4,3,2,1,0:T(8,128)(2,1)} %advanced_ref.11) | copy-start | bytes 6291460
  15.2 9.1 %copy-start.1 = (bf16[2,4,4,2,32,512]{5,4,3,2,1,0:T(8,128)(2,1)S(1)}, bf16[2,4,4,2,32,512]{5,4,3,2,1,0:T(8,128)(2,1)}, u32[]{:S(2)}) copy-start(bf16[2,4,4,2,32,512]{5,4,3,2,1,0:T(8,128)(2,1)} %lesser_ref.13) | copy-start | bytes 6291460
  15.2 9.1 %copy-start.3 = (bf16[2,4,4,2,32,512]{5,4,3,2,1,0:T(8,128)(2,1)S(1)}, bf16[2,4,4,2,32,512]{5,4,3,2,1,0:T(8,128)(2,1)}, u32[]{:S(2)}) copy-start(bf16[2,4,4,2,32,512]{5,4,3,2,1,0:T(8,128)(2,1)} %advanced_ref.11) | copy-start | bytes 6291460
  18.3 9.1 %collective-permute-start.2 = (f32[8,2,2,8,512]{4,3,2,1,0:T(8,128)S(1)}, f32[8,2,2,8,512]{4,3,2,1,0:T(8,128)S(1)}, u32[]{:S(2)}, u32[]{:S(2)}) collective-permute-start(f32[8,2,2,8,512]{4,3,2,1,0:T(8,128)S(1)} %get-tuple-element.42), channel_id=1, source_target_pairs={{0,2},{2,0},{4,6},{6,4},{8,10},{10,8},{12,14},{14,12},{16,18},{18,... | collective-permute-start | bytes 1572872 | tf_op jit(solution)/shard_map/ppermute | solution.py:543
  18.4 5.9 %collective-permute-start.6 = (f32[2,2,2,8,512]{4,3,2,1,0:T(8,128)S(1)}, f32[2,2,2,8,512]{4,3,2,1,0:T(8,128)S(1)}, u32[]{:S(2)}, u32[]{:S(2)}) collective-permute-start(f32[2,2,2,8,512]{4,3,2,1,0:T(8,128)S(1)} %get-tuple-element.43), channel_id=1, source_target_pairs={{0,1},{1,0},{2,3},{3,2},{4,5},{5,4},{6,7},{7,6},{8,9},{9,8},{10,11... | collective-permute-start | bytes 393224 | tf_op jit(solution)/shard_map/ppermute | solution.py:646
  27.4 3.5 %collective-permute-start.7 = (f32[8,2,2,8,512]{4,3,2,1,0:T(8,128)S(1)}, f32[8,2,2,8,512]{4,3,2,1,0:T(8,128)S(1)}, u32[]{:S(2)}, u32[]{:S(2)}) collective-permute-start(f32[8,2,2,8,512]{4,3,2,1,0:T(8,128)S(1)} %get-tuple-element.45), channel_id=1, source_target_pairs={{0,2},{2,0},{4,6},{6,4},{8,10},{10,8},{12,14},{14,12},{16,18},{18,... | collective-permute-start | bytes 1572872 | tf_op jit(solution)/shard_map/ppermute | solution.py:543
  27.6 9.2 %collective-permute-start.3 = (f32[4,2,2,8,512]{4,3,2,1,0:T(8,128)S(1)}, f32[4,2,2,8,512]{4,3,2,1,0:T(8,128)S(1)}, u32[]{:S(2)}, u32[]{:S(2)}) collective-permute-start(f32[4,2,2,8,512]{4,3,2,1,0:T(8,128)S(1)} %get-tuple-element.73), channel_id=1, source_target_pairs={{0,4},{2,6},{4,0},{6,2},{8,12},{10,14},{12,8},{14,10},{16,20},{18,... | collective-permute-start | bytes 786440 | tf_op jit(solution)/shard_map/ppermute | solution.py:547
  29.4 22.7 %collective-permute-start.1 = (f32[2,2,8,512]{3,2,1,0:T(8,128)S(1)}, f32[2,2,8,512]{3,2,1,0:T(8,128)S(1)}, u32[]{:S(2)}, u32[]{:S(2)}) collective-permute-start(f32[2,2,8,512]{3,2,1,0:T(8,128)S(1)} %slice_bitcast_fusion.9.near_here_ref.green_here_ref.green_near_ref), channel_id=1, source_target_pairs={{0,1},{1,0},{2,3},{3,2},{4,5},{5,4},{6,7},{7,6},{8,9},{9,8},{10,11... | collective-permute-start | bytes 196616 | tf_op jit(solution)/shard_map/ppermute | solution.py:646
  31.0 15.2 %collective-permute-start.8 = (f32[4,2,2,8,512]{4,3,2,1,0:T(8,128)S(1)}, f32[4,2,2,8,512]{4,3,2,1,0:T(8,128)S(1)}, u32[]{:S(2)}, u32[]{:S(2)}) collective-permute-start(f32[4,2,2,8,512]{4,3,2,1,0:T(8,128)S(1)} %get-tuple-element.71), channel_id=1, source_target_pairs={{0,4},{2,6},{4,0},{6,2},{8,12},{10,14},{12,8},{14,10},{16,20},{18,... | collective-permute-start | bytes 786440 | tf_op jit(solution)/shard_map/ppermute | solution.py:547
  36.9 8.5 %collective-permute-start.4 = (f32[2,2,2,8,512]{4,3,2,1,0:T(8,128)S(1)}, f32[2,2,2,8,512]{4,3,2,1,0:T(8,128)S(1)}, u32[]{:S(2)}, u32[]{:S(2)}) collective-permute-start(f32[2,2,2,8,512]{4,3,2,1,0:T(8,128)S(1)} %get-tuple-element.91), channel_id=1, source_target_pairs={{0,16},{2,18},{4,20},{6,22},{8,24},{10,26},{12,28},{14,30},{16,0},... | collective-permute-start | bytes 393224 | tf_op jit(solution)/shard_map/ppermute | solution.py:547
  45.4 8.1 %collective-permute-start.5 = (f32[1,2,2,8,512]{4,3,2,1,0:T(8,128)S(1)}, f32[1,2,2,8,512]{4,3,2,1,0:T(8,128)S(1)}, u32[]{:S(2)}, u32[]{:S(2)}) collective-permute-start(f32[1,2,2,8,512]{4,3,2,1,0:T(8,128)S(1)} %get-tuple-element.96), channel_id=1, source_target_pairs={{0,8},{2,10},{4,12},{6,14},{8,0},{10,2},{12,4},{14,6},{16,24},{18,... | collective-permute-start | bytes 196616 | tf_op jit(solution)/shard_map/ppermute | solution.py:547
  46.2 7.3 %collective-permute-start.9 = (f32[2,2,8,512]{3,2,1,0:T(8,128)S(1)}, f32[2,2,8,512]{3,2,1,0:T(8,128)S(1)}, u32[]{:S(2)}, u32[]{:S(2)}) collective-permute-start(f32[2,2,8,512]{3,2,1,0:T(8,128)S(1)} %get-tuple-element.89), channel_id=1, source_target_pairs={{0,1},{1,0},{2,3},{3,2},{4,5},{5,4},{6,7},{7,6},{8,9},{9,8},{10,11... | collective-permute-start | bytes 196616 | tf_op jit(solution)/shard_map/ppermute | solution.py:557
  47.8 5.8 %collective-permute-start.10 = (f32[2,2,8,512]{3,2,1,0:T(8,128)S(1)}, f32[2,2,8,512]{3,2,1,0:T(8,128)S(1)}, u32[]{:S(2)}, u32[]{:S(2)}) collective-permute-start(f32[2,2,8,512]{3,2,1,0:T(8,128)S(1)} %get-tuple-element.88), channel_id=1, source_target_pairs={{0,9},{1,8},{2,11},{3,10},{4,13},{5,12},{6,15},{7,14},{8,1},{9,0},... | collective-permute-start | bytes 196616 | tf_op jit(solution)/shard_map/ppermute | solution.py:557
  49.1 6.3 %collective-permute-start.11 = (f32[2,2,8,512]{3,2,1,0:T(8,128)S(1)}, f32[2,2,8,512]{3,2,1,0:T(8,128)S(1)}, u32[]{:S(2)}, u32[]{:S(2)}) collective-permute-start(f32[2,2,8,512]{3,2,1,0:T(8,128)S(1)} %get-tuple-element.87), channel_id=1, source_target_pairs={{0,17},{1,16},{2,19},{3,18},{4,21},{5,20},{6,23},{7,22},{8,25},{9,... | collective-permute-start | bytes 196616 | tf_op jit(solution)/shard_map/ppermute | solution.py:557
  52.1 7.1 %collective-permute-start.12 = (f32[2,2,8,512]{3,2,1,0:T(8,128)S(1)}, f32[2,2,8,512]{3,2,1,0:T(8,128)S(1)}, u32[]{:S(2)}, u32[]{:S(2)}) collective-permute-start(f32[2,2,8,512]{3,2,1,0:T(8,128)S(1)} %get-tuple-element.86), channel_id=1, source_target_pairs={{0,25},{1,24},{2,27},{3,26},{4,29},{5,28},{6,31},{7,30},{8,17},{9,... | collective-permute-start | bytes 196616 | tf_op jit(solution)/shard_map/ppermute | solution.py:557
  62.9 9.1 %collective-permute-start.14 = (f32[8,2,2,8,512]{4,3,2,1,0:T(8,128)S(1)}, f32[8,2,2,8,512]{4,3,2,1,0:T(8,128)S(1)}, u32[]{:S(2)}, u32[]{:S(2)}) collective-permute-start(f32[8,2,2,8,512]{4,3,2,1,0:T(8,128)S(1)} %get-tuple-element.49), channel_id=1, source_target_pairs={{0,2},{2,0},{4,6},{6,4},{8,10},{10,8},{12,14},{14,12},{16,18},{18,... | collective-permute-start | bytes 1572872 | tf_op jit(solution)/shard_map/ppermute | solution.py:543
  63.0 5.9 %collective-permute-start.18 = (f32[2,2,2,8,512]{4,3,2,1,0:T(8,128)S(1)}, f32[2,2,2,8,512]{4,3,2,1,0:T(8,128)S(1)}, u32[]{:S(2)}, u32[]{:S(2)}) collective-permute-start(f32[2,2,2,8,512]{4,3,2,1,0:T(8,128)S(1)} %get-tuple-element.50), channel_id=1, source_target_pairs={{0,1},{1,0},{2,3},{3,2},{4,5},{5,4},{6,7},{7,6},{8,9},{9,8},{10,11... | collective-permute-start | bytes 393224 | tf_op jit(solution)/shard_map/ppermute | solution.py:646
  72.0 2.0 %collective-permute-start.19 = (f32[8,2,2,8,512]{4,3,2,1,0:T(8,128)S(1)}, f32[8,2,2,8,512]{4,3,2,1,0:T(8,128)S(1)}, u32[]{:S(2)}, u32[]{:S(2)}) collective-permute-start(f32[8,2,2,8,512]{4,3,2,1,0:T(8,128)S(1)} %get-tuple-element.52), channel_id=1, source_target_pairs={{0,2},{2,0},{4,6},{6,4},{8,10},{10,8},{12,14},{14,12},{16,18},{18,... | collective-permute-start | bytes 1572872 | tf_op jit(solution)/shard_map/ppermute | solution.py:543
  72.1 9.2 %collective-permute-start.15 = (f32[4,2,2,8,512]{4,3,2,1,0:T(8,128)S(1)}, f32[4,2,2,8,512]{4,3,2,1,0:T(8,128)S(1)}, u32[]{:S(2)}, u32[]{:S(2)}) collective-permute-start(f32[4,2,2,8,512]{4,3,2,1,0:T(8,128)S(1)} %get-tuple-element.69), channel_id=1, source_target_pairs={{0,4},{2,6},{4,0},{6,2},{8,12},{10,14},{12,8},{14,10},{16,20},{18,... | collective-permute-start | bytes 786440 | tf_op jit(solution)/shard_map/ppermute | solution.py:547
  74.0 15.8 %collective-permute-start.20 = (f32[4,2,2,8,512]{4,3,2,1,0:T(8,128)S(1)}, f32[4,2,2,8,512]{4,3,2,1,0:T(8,128)S(1)}, u32[]{:S(2)}, u32[]{:S(2)}) collective-permute-start(f32[4,2,2,8,512]{4,3,2,1,0:T(8,128)S(1)} %get-tuple-element.67), channel_id=1, source_target_pairs={{0,4},{2,6},{4,0},{6,2},{8,12},{10,14},{12,8},{14,10},{16,20},{18,... | collective-permute-start | bytes 786440 | tf_op jit(solution)/shard_map/ppermute | solution.py:547
  81.4 8.3 %collective-permute-start.16 = (f32[2,2,2,8,512]{4,3,2,1,0:T(8,128)S(1)}, f32[2,2,2,8,512]{4,3,2,1,0:T(8,128)S(1)}, u32[]{:S(2)}, u32[]{:S(2)}) collective-permute-start(f32[2,2,2,8,512]{4,3,2,1,0:T(8,128)S(1)} %get-tuple-element.85), channel_id=1, source_target_pairs={{0,16},{2,18},{4,20},{6,22},{8,24},{10,26},{12,28},{14,30},{16,0},... | collective-permute-start | bytes 393224 | tf_op jit(solution)/shard_map/ppermute | solution.py:547
  82.8 11.3 %collective-permute-start.13 = (f32[2,2,2,8,512]{4,3,2,1,0:T(8,128)S(1)}, f32[2,2,2,8,512]{4,3,2,1,0:T(8,128)S(1)}, u32[]{:S(2)}, u32[]{:S(2)}) collective-permute-start(f32[2,2,2,8,512]{4,3,2,1,0:T(8,128)S(1)} %get-tuple-element.46), channel_id=1, source_target_pairs={{0,1},{1,0},{2,3},{3,2},{4,5},{5,4},{6,7},{7,6},{8,9},{9,8},{10,11... | collective-permute-start | bytes 393224 | tf_op jit(solution)/shard_map/ppermute | solution.py:646
  89.8 7.0 %collective-permute-start.17 = (f32[1,2,2,8,512]{4,3,2,1,0:T(8,128)S(1)}, f32[1,2,2,8,512]{4,3,2,1,0:T(8,128)S(1)}, u32[]{:S(2)}, u32[]{:S(2)}) collective-permute-start(f32[1,2,2,8,512]{4,3,2,1,0:T(8,128)S(1)} %get-tuple-element.94), channel_id=1, source_target_pairs={{0,8},{2,10},{4,12},{6,14},{8,0},{10,2},{12,4},{14,6},{16,24},{18,... | collective-permute-start | bytes 196616 | tf_op jit(solution)/shard_map/ppermute | solution.py:547
  89.9 6.8 %collective-permute-start.21 = (f32[2,2,8,512]{3,2,1,0:T(8,128)S(1)}, f32[2,2,8,512]{3,2,1,0:T(8,128)S(1)}, u32[]{:S(2)}, u32[]{:S(2)}) collective-permute-start(f32[2,2,8,512]{3,2,1,0:T(8,128)S(1)} %get-tuple-element.83), channel_id=1, source_target_pairs={{0,1},{1,0},{2,3},{3,2},{4,5},{5,4},{6,7},{7,6},{8,9},{9,8},{10,11... | collective-permute-start | bytes 196616 | tf_op jit(solution)/shard_map/ppermute | solution.py:557
  90.5 6.3 %collective-permute-start.22 = (f32[2,2,8,512]{3,2,1,0:T(8,128)S(1)}, f32[2,2,8,512]{3,2,1,0:T(8,128)S(1)}, u32[]{:S(2)}, u32[]{:S(2)}) collective-permute-start(f32[2,2,8,512]{3,2,1,0:T(8,128)S(1)} %get-tuple-element.82), channel_id=1, source_target_pairs={{0,9},{1,8},{2,11},{3,10},{4,13},{5,12},{6,15},{7,14},{8,1},{9,0},... | collective-permute-start | bytes 196616 | tf_op jit(solution)/shard_map/ppermute | solution.py:557
  93.4 7.9 %collective-permute-start.23 = (f32[2,2,8,512]{3,2,1,0:T(8,128)S(1)}, f32[2,2,8,512]{3,2,1,0:T(8,128)S(1)}, u32[]{:S(2)}, u32[]{:S(2)}) collective-permute-start(f32[2,2,8,512]{3,2,1,0:T(8,128)S(1)} %get-tuple-element.81), channel_id=1, source_target_pairs={{0,17},{1,16},{2,19},{3,18},{4,21},{5,20},{6,23},{7,22},{8,25},{9,... | collective-permute-start | bytes 196616 | tf_op jit(solution)/shard_map/ppermute | solution.py:557
  94.0 7.3 %collective-permute-start.24 = (f32[2,2,8,512]{3,2,1,0:T(8,128)S(1)}, f32[2,2,8,512]{3,2,1,0:T(8,128)S(1)}, u32[]{:S(2)}, u32[]{:S(2)}) collective-permute-start(f32[2,2,8,512]{3,2,1,0:T(8,128)S(1)} %get-tuple-element.80), channel_id=1, source_target_pairs={{0,25},{1,24},{2,27},{3,26},{4,29},{5,28},{6,31},{7,30},{8,17},{9,... | collective-permute-start | bytes 196616 | tf_op jit(solution)/shard_map/ppermute | solution.py:557
  105.1 9.1 %collective-permute-start.26 = (f32[8,2,2,8,512]{4,3,2,1,0:T(8,128)S(1)}, f32[8,2,2,8,512]{4,3,2,1,0:T(8,128)S(1)}, u32[]{:S(2)}, u32[]{:S(2)}) collective-permute-start(f32[8,2,2,8,512]{4,3,2,1,0:T(8,128)S(1)} %get-tuple-element.58), channel_id=1, source_target_pairs={{0,2},{2,0},{4,6},{6,4},{8,10},{10,8},{12,14},{14,12},{16,18},{18,... | collective-permute-start | bytes 1572872 | tf_op jit(solution)/shard_map/ppermute | solution.py:543
  105.2 5.9 %collective-permute-start.30 = (f32[2,2,2,8,512]{4,3,2,1,0:T(8,128)S(1)}, f32[2,2,2,8,512]{4,3,2,1,0:T(8,128)S(1)}, u32[]{:S(2)}, u32[]{:S(2)}) collective-permute-start(f32[2,2,2,8,512]{4,3,2,1,0:T(8,128)S(1)} %get-tuple-element.59), channel_id=1, source_target_pairs={{0,1},{1,0},{2,3},{3,2},{4,5},{5,4},{6,7},{7,6},{8,9},{9,8},{10,11... | collective-permute-start | bytes 393224 | tf_op jit(solution)/shard_map/ppermute | solution.py:646
  114.2 2.0 %collective-permute-start.31 = (f32[8,2,2,8,512]{4,3,2,1,0:T(8,128)S(1)}, f32[8,2,2,8,512]{4,3,2,1,0:T(8,128)S(1)}, u32[]{:S(2)}, u32[]{:S(2)}) collective-permute-start(f32[8,2,2,8,512]{4,3,2,1,0:T(8,128)S(1)} %get-tuple-element.61), channel_id=1, source_target_pairs={{0,2},{2,0},{4,6},{6,4},{8,10},{10,8},{12,14},{14,12},{16,18},{18,... | collective-permute-start | bytes 1572872 | tf_op jit(solution)/shard_map/ppermute | solution.py:543
  114.3 9.2 %collective-permute-start.27 = (f32[4,2,2,8,512]{4,3,2,1,0:T(8,128)S(1)}, f32[4,2,2,8,512]{4,3,2,1,0:T(8,128)S(1)}, u32[]{:S(2)}, u32[]{:S(2)}) collective-permute-start(f32[4,2,2,8,512]{4,3,2,1,0:T(8,128)S(1)} %get-tuple-element.65), channel_id=1, source_target_pairs={{0,4},{2,6},{4,0},{6,2},{8,12},{10,14},{12,8},{14,10},{16,20},{18,... | collective-permute-start | bytes 786440 | tf_op jit(solution)/shard_map/ppermute | solution.py:547
  116.2 15.8 %collective-permute-start.32 = (f32[4,2,2,8,512]{4,3,2,1,0:T(8,128)S(1)}, f32[4,2,2,8,512]{4,3,2,1,0:T(8,128)S(1)}, u32[]{:S(2)}, u32[]{:S(2)}) collective-permute-start(f32[4,2,2,8,512]{4,3,2,1,0:T(8,128)S(1)} %get-tuple-element.63), channel_id=1, source_target_pairs={{0,4},{2,6},{4,0},{6,2},{8,12},{10,14},{12,8},{14,10},{16,20},{18,... | collective-permute-start | bytes 786440 | tf_op jit(solution)/shard_map/ppermute | solution.py:547
  123.6 8.3 %collective-permute-start.28 = (f32[2,2,2,8,512]{4,3,2,1,0:T(8,128)S(1)}, f32[2,2,2,8,512]{4,3,2,1,0:T(8,128)S(1)}, u32[]{:S(2)}, u32[]{:S(2)}) collective-permute-start(f32[2,2,2,8,512]{4,3,2,1,0:T(8,128)S(1)} %get-tuple-element.79), channel_id=1, source_target_pairs={{0,16},{2,18},{4,20},{6,22},{8,24},{10,26},{12,28},{14,30},{16,0},... | collective-permute-start | bytes 393224 | tf_op jit(solution)/shard_map/ppermute | solution.py:547
  124.8 11.8 %collective-permute-start.25 = (f32[2,2,2,8,512]{4,3,2,1,0:T(8,128)S(1)}, f32[2,2,2,8,512]{4,3,2,1,0:T(8,128)S(1)}, u32[]{:S(2)}, u32[]{:S(2)}) collective-permute-start(f32[2,2,2,8,512]{4,3,2,1,0:T(8,128)S(1)} %slice.305), channel_id=1, source_target_pairs={{0,1},{1,0},{2,3},{3,2},{4,5},{5,4},{6,7},{7,6},{8,9},{9,8},{10,11... | collective-permute-start | bytes 393224 | tf_op jit(solution)/shard_map/ppermute | solution.py:646
  132.0 4.7 %collective-permute-start.29 = (f32[1,2,2,8,512]{4,3,2,1,0:T(8,128)S(1)}, f32[1,2,2,8,512]{4,3,2,1,0:T(8,128)S(1)}, u32[]{:S(2)}, u32[]{:S(2)}) collective-permute-start(f32[1,2,2,8,512]{4,3,2,1,0:T(8,128)S(1)} %get-tuple-element.92), channel_id=1, source_target_pairs={{0,8},{2,10},{4,12},{6,14},{8,0},{10,2},{12,4},{14,6},{16,24},{18,... | collective-permute-start | bytes 196616 | tf_op jit(solution)/shard_map/ppermute | solution.py:547
  132.1 5.1 %collective-permute-start.33 = (f32[2,2,8,512]{3,2,1,0:T(8,128)S(1)}, f32[2,2,8,512]{3,2,1,0:T(8,128)S(1)}, u32[]{:S(2)}, u32[]{:S(2)}) collective-permute-start(f32[2,2,8,512]{3,2,1,0:T(8,128)S(1)} %get-tuple-element.76), channel_id=1, source_target_pairs={{0,8},{2,10},{4,12},{6,14},{8,0},{10,2},{12,4},{14,6},{16,24},{18,... | collective-permute-start | bytes 196616 | tf_op jit(solution)/shard_map/ppermute | solution.py:561
  134.2 7.2 %collective-permute-start.34 = (f32[2,2,8,512]{3,2,1,0:T(8,128)S(1)}, f32[2,2,8,512]{3,2,1,0:T(8,128)S(1)}, u32[]{:S(2)}, u32[]{:S(2)}) collective-permute-start(f32[2,2,8,512]{3,2,1,0:T(8,128)S(1)} %get-tuple-element.75), channel_id=1, source_target_pairs={{0,16},{2,18},{4,20},{6,22},{8,24},{10,26},{12,28},{14,30},{16,0},... | collective-permute-start | bytes 196616 | tf_op jit(solution)/shard_map/ppermute | solution.py:561
  134.3 7.0 %collective-permute-start.35 = (f32[2,2,8,512]{3,2,1,0:T(8,128)S(1)}, f32[2,2,8,512]{3,2,1,0:T(8,128)S(1)}, u32[]{:S(2)}, u32[]{:S(2)}) collective-permute-start(f32[2,2,8,512]{3,2,1,0:T(8,128)S(1)} %get-tuple-element.74), channel_id=1, source_target_pairs={{0,24},{2,26},{4,28},{6,30},{8,16},{10,18},{12,20},{14,22},{16,8},... | collective-permute-start | bytes 196616 | tf_op jit(solution)/shard_map/ppermute | solution.py:561

commit v3 on v2

--- a/solution.py
+++ b/solution.py
@@ -190,11 +190,12 @@
     )
     cosine, sine = np.cos(angle) / KS, np.sin(angle) / KS
     full = np.block([[cosine, sine], [-sine, cosine]]).astype(np.float32)
+    turn = 2.0 * np.pi * (outer[None, :] * np.arange(tiles)[:, None]) / KS
+    twiddle = np.concatenate([np.cos(turn), np.sin(turn)], axis=1).astype(np.float32)
+    full = np.concatenate([full, twiddle])
     high = full.astype(jnp.bfloat16)
     low = (full - high.astype(np.float32)).astype(jnp.bfloat16)
-    turn = 2.0 * np.pi * (outer[None, :] * np.arange(tiles)[:, None]) / KS
-    twiddle = np.stack([np.cos(turn), np.sin(turn)], axis=1).astype(np.float32)
-    return jnp.asarray(np.stack([high, low])), jnp.asarray(twiddle)
+    return jnp.asarray(np.stack([high, low]))
 
 
 def radix(values):
@@ -222,7 +223,7 @@
 def turned(pair, twiddle_ref, tile):
     if tile == 0:
         return pair
-    cosine, sine = twiddle_ref[tile, 0:1, :], twiddle_ref[tile, 1:2, :]
+    cosine, sine = twiddle_ref[tile : tile + 1, :LANES], twiddle_ref[tile : tile + 1, LANES:]
     return (pair[0] * cosine - pair[1] * sine, pair[0] * sine + pair[1] * cosine)
 
 
@@ -297,18 +298,20 @@
 
 
 def stage_kernel(
-    blocks_ref, onsite_ref, energies_ref, table_in_ref, twiddle_in_ref,
-    causal_ref, energy_ref, onsite_out_ref, table_ref, twiddle_ref
+    blocks_ref, onsite_ref, lesser_ref, advanced_ref, energies_ref, tables_ref, held_ref, masked_ref,
+    energy_ref, onsite_out_ref, table_ref, twiddle_ref
 ):
     ta, ka = lax.axis_index("ta"), lax.axis_index("ka")
-    table_ref[...] = table_in_ref[...]
-    twiddle_ref[...] = twiddle_in_ref[...]
-    local_rows, all_times, k_local = causal_ref.shape[0], causal_ref.shape[1], energy_ref.shape[1]
+    table_rows = table_ref.shape[1]
+    table_ref[...] = tables_ref[:, :table_rows]
+    turns = tables_ref[:, table_rows:].astype(jnp.float32)
+    twiddle_ref[...] = turns[0] + turns[1]
+    k_local = energy_ref.shape[1]
+    planes, orbitals, _, local_rows, all_times, _ = lesser_ref.shape
     for side, begin in enumerate((ka * k_local, (1 - ka) * k_local)):
         energy_ref[side : side + 1, :] = energies_ref[
             :, pl.ds(pl.multiple_of(begin, LANES), k_local)
         ]
-    orbitals = onsite_ref.shape[1]
     halves = orbitals // 2
     for row in range(orbitals):
         for column in range(orbitals):
@@ -318,12 +321,36 @@
                 ]
                 place = (plane * orbitals + row) * orbitals + column
                 onsite_out_ref[place : place + 1, :] = jnp.full((1, LANES), value)
-    for stored in range(local_rows):
-        row_time = blocks_ref[ta] * local_rows + stored
-        for column in range(all_times):
-            column_time = blocks_ref[column // local_rows] * local_rows + column % local_rows
-            seen = jnp.where(row_time <= column_time, jnp.float32(1.0), jnp.float32(0.0))
-            causal_ref[stored, column : column + 1, :] = jnp.full((1, LANES), seen)
+    position = lax.broadcasted_iota(jnp.int32, (all_times, LANES), 0)
+    column_times = jnp.zeros((all_times, LANES), jnp.int32)
+    for block in range(all_times // local_rows):
+        column_times = jnp.where(
+            position // local_rows == block, blocks_ref[block] * local_rows, column_times
+        )
+    column_times = column_times + position % local_rows
+    seen = [
+        (blocks_ref[ta] * local_rows + stored <= column_times)
+        .astype(jnp.float32)
+        .astype(advanced_ref.dtype)
+        for stored in range(local_rows)
+    ]
+
+    def move(counter, carried):
+        plane = counter // (orbitals * orbitals)
+        inner = counter // orbitals % orbitals
+        outer = counter % orbitals
+        for stored in range(local_rows):
+            for tile in range(k_local // LANES):
+                lanes = pl.ds(tile * LANES, LANES)
+                held_ref[plane, inner, outer, stored, :, lanes] = lesser_ref[
+                    plane, inner, outer, stored, :, lanes
+                ]
+                masked_ref[plane, inner, outer, stored, :, lanes] = (
+                    advanced_ref[plane, inner, outer, stored, :, lanes] * seen[stored]
+                )
+        return carried
+
+    lax.fori_loop(0, planes * orbitals * orbitals, move, 0)
 
 
 def opening_kernel(
@@ -465,7 +492,7 @@
 
 
 def collide_kernel(
-    order, sigma_ref, causal_ref, lesser_ref, advanced_ref, keep_ref, send_ref
+    order, sigma_ref, lesser_ref, advanced_ref, keep_ref, send_ref
 ):
     halves, k_local = sigma_ref.shape[2], sigma_ref.shape[4]
     orbitals, local_rows, times = lesser_ref.shape[1], lesser_ref.shape[3], lesser_ref.shape[4]
@@ -493,8 +520,6 @@
                             )
                             for plane in range(2)
                         ]
-                        if field == 0:
-                            triple = [value * causal_ref[stored, here] for value in triple]
                         sigmas.append(triple + [triple[0] + triple[1]])
                     for outer in range(orbitals):
                         slabs = [
@@ -571,7 +596,7 @@
     all_times = local_rows * ta_count
     halves = orbitals // 2
     tiles = k_local * ka_count // LANES
-    table, twiddle = fourier_tables(tiles)
+    tables_in = fourier_tables(tiles)
     momenta = jnp.arange(KS * KS, dtype=jnp.int32)
     start = lax.optimization_barrier(jnp.broadcast_to(slab_start, momenta.shape))
     energies = dispersion(start[None], all_times, momenta // KS, momenta % KS)[None]
@@ -595,21 +620,22 @@
         name="pack",
     )(screen_lesser, screen_retarded, green_row)
     arrived_fields = lax.ppermute(far_fields, "ka", flip(1, ka_count))
-    causal, energy, onsite, table, twiddle = pl.pallas_call(
+    lesser_slab, advanced_slab, energy, onsite, table, twiddle = pl.pallas_call(
         stage_kernel,
         out_shape=(
-            float_like(local_rows, all_times, LANES),
+            jax.ShapeDtypeStruct(lesser_slab.shape, lesser_slab.dtype),
+            jax.ShapeDtypeStruct(advanced_slab.shape, advanced_slab.dtype),
             float_like(2, k_local),
             float_like(2 * orbitals * orbitals, LANES),
-            jax.ShapeDtypeStruct(table.shape, table.dtype),
-            jax.ShapeDtypeStruct(twiddle.shape, twiddle.dtype),
+            jax.ShapeDtypeStruct((2, 2 * LANES, 2 * LANES), tables_in.dtype),
+            float_like(tiles, 2 * LANES),
         ),
-        in_specs=[scalar] * 2 + [whole()] * 3,
-        out_specs=(whole(),) * 5,
+        in_specs=[scalar] * 2 + [whole()] * 4,
+        out_specs=(whole(),) * 6,
         compiler_params=small,
         cost_estimate=hint,
         name="stage",
-    )(block_table, onsite, energies, table, twiddle)
+    )(block_table, onsite, lesser_slab, advanced_slab, energies, tables_in)
     green_near, green_far, green_there = near_fields[2], far_fields[2], arrived_fields[2]
 
     screens, sigma_near, sigma_send = pl.pallas_call(
@@ -631,7 +657,7 @@
         return pl.pallas_call(
             functools.partial(collide_kernel, order),
             out_shape=(float_like(ta_count // 2, *chunk),) * 2,
-            in_specs=[whole()] * 4,
+            in_specs=[whole()] * 3,
             out_specs=(whole(),) * 2,
             compiler_params=small,
             cost_estimate=pl.CostEstimate(
@@ -640,7 +666,7 @@
                 transcendentals=0,
             ),
             name="collide",
-        )(sigma, causal, lesser_slab, advanced_slab)
+        )(sigma, lesser_slab, advanced_slab)
 
     def exchanged(value):
         return lax.ppermute(value, "ka", flip(1, ka_count))

time: 143 us -> 141 us (0.986)
    ppermute x6, starting transfers between devices: 7.67 us -> 4.87 us  [exchanged(): return lax.ppermute(value, 'ka', flip(1, ka_count))]
    ppermute x12, starting transfers between devices: 15.1 us -> 17.2 us  [halved_sum(): got = lax.ppermute(outgoing, 'ta', flip(1 << bit, ta_count))]
    unnamed x22 -> x16, local copies, waits for them, and re-layouts: 8.87 us -> 8.18 us
  transfers between devices with their start and end apart: 36 -> 36, of which waited for: 17 -> 16; matrix products, arithmetic and copies ran while one was open for 1% -> 1% of each run, Pallas kernels for 7% -> 8%
where the time goes in v3:
time: 141 us
  waiting for transfers between devices  63.7 us (45%)
  starting transfers between devices  43.6 us (31%)
  Pallas kernels  22.6 us (16%)
  local copies, waits for them, and re-layouts  8.24 us (6%)
  between operations  1.66 us (1%)
    ppermute x12, waiting for transfers between devices, halved_sum(): got = lax.ppermute(outgoing, 'ta', flip(1 << bit, ta_count))  34 us
    pallas_call x6, Pallas kernels, collide(): pl.pallas_call(functools.partial(collide_kernel, order), out_shape=(float...  18 us
    ppermute x12, starting transfers between devices, halved_sum(): got = lax.ppermute(outgoing, 'ta', flip(1 << bit, ta_count))  17.2 us
    ppermute x6, waiting for transfers between devices, exchanged(): return lax.ppermute(value, 'ka', flip(1, ka_count))  14.5 us
    ppermute x8, starting transfers between devices, halved_sum(): results.append(lax.ppermute(pieces[place], ('ta', 'ka'), pairs))  13.6 us
    ppermute x8, waiting for transfers between devices, halved_sum(): results.append(lax.ppermute(pieces[place], ('ta', 'ka'), pairs))  9.71 us
    unnamed x16, local copies, waits for them, and re-layouts  8.18 us
    ppermute x3, waiting for transfers between devices, halved_sum(): results.append(lax.ppermute(pieces[place], 'ta', flip(across, ta_count)))  5 us
  transfers between devices with their start and end apart: 36, of which 16 were waited for; matrix products, arithmetic and copies ran while one was open for 1% of the time, Pallas kernels for 8%

profile of v3, /device:TPU:0, one launch (start us, length us, event | category | flops | bytes accessed | tf_op | source)
XLA Modules:
  0.0 140.6 jit_solution(3944246502871889685)
XLA Ops:
  0.6 0.9 copy-done.3
  1.5 0.9 copy-done.4
  2.4 0.9 copy-done.5
  3.5 3.0 %collective-permute-start = (f32[3,2,2,8,512]{4,3,2,1,0:T(8,128)S(1)}, f32[3,2,2,8,512]{4,3,2,1,0:T(8,128)S(1)}, u32[]{:S(2)}, u32[]{:S(2)}) collective-permute-start(f32[3,2,2,8,512]{4,3,2,1,0:T(8,128)S(1)} %get-tuple-element.36), channel_id=1, source_target_pairs={{0,1},{1,0},{2,3},{3,2},{4,5},{5,4},{6,7},{7,6},{8,9},{9,8},{10,11... | collective-permute-start | bytes 589832 | tf_op jit(solution)/shard_map/ppermute | solution.py:622
  7.3 1.6 %copy-done = bf16[2,4,4,2,32,512]{5,4,3,2,1,0:T(8,128)(2,1)S(1)} copy-done((bf16[2,4,4,2,32,512]{5,4,3,2,1,0:T(8,128)(2,1)S(1)}, bf16[2,4,4,2,32,512]{5,4,3,2,1,0:T(8,128)(2,1)}, u32[]{:S(2)}) %copy-start) | copy-done | bytes 2097176
  8.9 1.6 %copy-done.1 = bf16[2,4,4,2,32,512]{5,4,3,2,1,0:T(8,128)(2,1)S(1)} copy-done((bf16[2,4,4,2,32,512]{5,4,3,2,1,0:T(8,128)(2,1)S(1)}, bf16[2,4,4,2,32,512]{5,4,3,2,1,0:T(8,128)(2,1)}, u32[]{:S(2)}) %copy-start.1) | copy-done | bytes 2097176
  10.4 1.0 copy-done.2
  12.7 1.6 %stage.1 = (bf16[2,4,4,2,32,512]{5,4,3,2,1,0:T(8,128)(2,1)S(1)}, bf16[2,4,4,2,32,512]{5,4,3,2,1,0:T(8,128)(2,1)S(1)}, f32[2,512]{1,0:T(2,128)S(1)}, f32[32,128]{...) custom-call(s32[16]{0:T(128)S(1)} %copy-done.7, f32[2,4,4]{2,1,0:T(4,128)S(1)} %copy-done.6, ...), custom_call_target="tpu_custom_call" | custom-call | flops 8388608 | bytes 8388608 | tf_op jit(solution)/shard_map/stage/pallas_call | solution.py:623
  15.1 3.0 %collide.6 = (f32[8,2,2,8,512]{4,3,2,1,0:T(8,128)S(1)}, f32[8,2,2,8,512]{4,3,2,1,0:T(8,128)S(1)}) custom-call(f32[2,2,2,8,512]{4,3,2,1,0:T(8,128)S(1)} %get-tuple-element.40.sigma_ref, bf16[2,4,4,2,32,512]{5,4,3,2,1,0:T(8,128)(2,1)S(1)} %get-tuple-element.41.lesser_ref, bf16[2,4,4,2,32,512]{5,4,3,2,1,0:T(8,128)(2,1)S(1)} %get-tuple-element.42.advanced_ref), custom_call_target="tpu_custom_call" | custom-call | flops 16777216 | bytes 4194304 | tf_op jit(solution)/shard_map/collide/pallas_call | solution.py:657
  18.2 5.8 %collective-permute-done.6.sigma_ref = f32[2,2,2,8,512]{4,3,2,1,0:T(8,128)S(1)} collective-permute-done((f32[2,2,2,8,512]{4,3,2,1,0:T(8,128)S(1)}, f32[2,2,2,8,512]{4,3,2,1,0:T(8,128)S(1)}, u32[]{:S(2)}, u32[]{:S(2)}) %collective-permute-start.6) | collective-permute-done | bytes 131104 | tf_op jit(solution)/shard_map/ppermute | solution.py:672
  24.0 3.0 %collide.7 = (f32[8,2,2,8,512]{4,3,2,1,0:T(8,128)S(1)}, f32[8,2,2,8,512]{4,3,2,1,0:T(8,128)S(1)}) custom-call(f32[2,2,2,8,512]{4,3,2,1,0:T(8,128)S(1)} %collective-permute-done.6.sigma_ref, bf16[2,4,4,2,32,512]{5,4,3,2,1,0:T(8,128)(2,1)S(1)} %get-tuple-element.41.lesser_ref, bf16[2,4,4,2,32,512]{5,4,3,2,1,0:T(8,128)(2,1)S(1)} %get-tuple-element.42.advanced_ref), custom_call_target="tpu_custom_call" | custom-call | flops 16777216 | bytes 4194304 | tf_op jit(solution)/shard_map/collide/pallas_call | solution.py:657
  27.2 1.6 %collective-permute-start.3 = (f32[4,2,2,8,512]{4,3,2,1,0:T(8,128)S(1)}, f32[4,2,2,8,512]{4,3,2,1,0:T(8,128)S(1)}, u32[]{:S(2)}, u32[]{:S(2)}) collective-permute-start(f32[4,2,2,8,512]{4,3,2,1,0:T(8,128)S(1)} %get-tuple-element.75), channel_id=1, source_target_pairs={{0,4},{2,6},{4,0},{6,2},{8,12},{10,14},{12,8},{14,10},{16,20},{18,... | collective-permute-start | bytes 786440 | tf_op jit(solution)/shard_map/ppermute | solution.py:572
  29.4 1.3 collective-permute-start.8
  30.7 5.8 %collective-permute-done.3 = f32[4,2,2,8,512]{4,3,2,1,0:T(8,128)S(1)} collective-permute-done((f32[4,2,2,8,512]{4,3,2,1,0:T(8,128)S(1)}, f32[4,2,2,8,512]{4,3,2,1,0:T(8,128)S(1)}, u32[]{:S(2)}, u32[]{:S(2)}) %collective-permute-start.3) | collective-permute-done | bytes 262176 | tf_op jit(solution)/shard_map/ppermute | solution.py:572
  36.5 2.6 %collective-permute-start.4 = (f32[2,2,2,8,512]{4,3,2,1,0:T(8,128)S(1)}, f32[2,2,2,8,512]{4,3,2,1,0:T(8,128)S(1)}, u32[]{:S(2)}, u32[]{:S(2)}) collective-permute-start(f32[2,2,2,8,512]{4,3,2,1,0:T(8,128)S(1)} %get-tuple-element.93), channel_id=1, source_target_pairs={{0,16},{2,18},{4,20},{6,22},{8,24},{10,26},{12,28},{14,30},{16,0},... | collective-permute-start | bytes 393224 | tf_op jit(solution)/shard_map/ppermute | solution.py:572
  39.2 5.7 %collective-permute-done.4 = f32[2,2,2,8,512]{4,3,2,1,0:T(8,128)S(1)} collective-permute-done((f32[2,2,2,8,512]{4,3,2,1,0:T(8,128)S(1)}, f32[2,2,2,8,512]{4,3,2,1,0:T(8,128)S(1)}, u32[]{:S(2)}, u32[]{:S(2)}) %collective-permute-start.4) | collective-permute-done | bytes 131104 | tf_op jit(solution)/shard_map/ppermute | solution.py:572
  46.2 2.3 %collective-permute-start.10 = (f32[2,2,8,512]{3,2,1,0:T(8,128)S(1)}, f32[2,2,8,512]{3,2,1,0:T(8,128)S(1)}, u32[]{:S(2)}, u32[]{:S(2)}) collective-permute-start(f32[2,2,8,512]{3,2,1,0:T(8,128)S(1)} %get-tuple-element.90), channel_id=1, source_target_pairs={{0,9},{1,8},{2,11},{3,10},{4,13},{5,12},{6,15},{7,14},{8,1},{9,0},... | collective-permute-start | bytes 196616 | tf_op jit(solution)/shard_map/ppermute | solution.py:582
  48.5 2.0 %collective-permute-start.11 = (f32[2,2,8,512]{3,2,1,0:T(8,128)S(1)}, f32[2,2,8,512]{3,2,1,0:T(8,128)S(1)}, u32[]{:S(2)}, u32[]{:S(2)}) collective-permute-start(f32[2,2,8,512]{3,2,1,0:T(8,128)S(1)} %get-tuple-element.89), channel_id=1, source_target_pairs={{0,17},{1,16},{2,19},{3,18},{4,21},{5,20},{6,23},{7,22},{8,25},{9,... | collective-permute-start | bytes 196616 | tf_op jit(solution)/shard_map/ppermute | solution.py:582
  50.5 1.9 %collective-permute-start.12 = (f32[2,2,8,512]{3,2,1,0:T(8,128)S(1)}, f32[2,2,8,512]{3,2,1,0:T(8,128)S(1)}, u32[]{:S(2)}, u32[]{:S(2)}) collective-permute-start(f32[2,2,8,512]{3,2,1,0:T(8,128)S(1)} %get-tuple-element.88), channel_id=1, source_target_pairs={{0,25},{1,24},{2,27},{3,26},{4,29},{5,28},{6,31},{7,30},{8,17},{9,... | collective-permute-start | bytes 196616 | tf_op jit(solution)/shard_map/ppermute | solution.py:582
  52.5 4.0 %collective-permute-done.11.refs_4_ = f32[2,2,8,512]{3,2,1,0:T(8,128)S(1)} collective-permute-done((f32[2,2,8,512]{3,2,1,0:T(8,128)S(1)}, f32[2,2,8,512]{3,2,1,0:T(8,128)S(1)}, u32[]{:S(2)}, u32[]{:S(2)}) %collective-permute-start.11) | collective-permute-done | bytes 65568 | tf_op jit(solution)/shard_map/ppermute | solution.py:582
  56.5 1.1 collective-permute-done.12.refs_5_
  58.3 3.0 %collide.8 = (f32[8,2,2,8,512]{4,3,2,1,0:T(8,128)S(1)}, f32[8,2,2,8,512]{4,3,2,1,0:T(8,128)S(1)}) custom-call(f32[2,2,2,8,512]{4,3,2,1,0:T(8,128)S(1)} %get-tuple-element.49.sigma_ref, bf16[2,4,4,2,32,512]{5,4,3,2,1,0:T(8,128)(2,1)S(1)} %get-tuple-element.41.lesser_ref, bf16[2,4,4,2,32,512]{5,4,3,2,1,0:T(8,128)(2,1)S(1)} %get-tuple-element.42.advanced_ref), custom_call_target="tpu_custom_call" | custom-call | flops 16777216 | bytes 4194304 | tf_op jit(solution)/shard_map/collide/pallas_call | solution.py:657
  61.3 1.5 %collective-permute-start.18 = (f32[2,2,2,8,512]{4,3,2,1,0:T(8,128)S(1)}, f32[2,2,2,8,512]{4,3,2,1,0:T(8,128)S(1)}, u32[]{:S(2)}, u32[]{:S(2)}) collective-permute-start(f32[2,2,2,8,512]{4,3,2,1,0:T(8,128)S(1)} %get-tuple-element.52), channel_id=1, source_target_pairs={{0,1},{1,0},{2,3},{3,2},{4,5},{5,4},{6,7},{7,6},{8,9},{9,8},{10,11... | collective-permute-start | bytes 393224 | tf_op jit(solution)/shard_map/ppermute | solution.py:672
  62.9 4.3 %collective-permute-done.18.sigma_ref = f32[2,2,2,8,512]{4,3,2,1,0:T(8,128)S(1)} collective-permute-done((f32[2,2,2,8,512]{4,3,2,1,0:T(8,128)S(1)}, f32[2,2,2,8,512]{4,3,2,1,0:T(8,128)S(1)}, u32[]{:S(2)}, u32[]{:S(2)}) %collective-permute-start.18) | collective-permute-done | bytes 131104 | tf_op jit(solution)/shard_map/ppermute | solution.py:672
  67.2 3.0 %collide.9 = (f32[8,2,2,8,512]{4,3,2,1,0:T(8,128)S(1)}, f32[8,2,2,8,512]{4,3,2,1,0:T(8,128)S(1)}) custom-call(f32[2,2,2,8,512]{4,3,2,1,0:T(8,128)S(1)} %collective-permute-done.18.sigma_ref, bf16[2,4,4,2,32,512]{5,4,3,2,1,0:T(8,128)(2,1)S(1)} %get-tuple-element.41.lesser_ref, bf16[2,4,4,2,32,512]{5,4,3,2,1,0:T(8,128)(2,1)S(1)} %get-tuple-element.42.advanced_ref), custom_call_target="tpu_custom_call" | custom-call | flops 16777216 | bytes 4194304 | tf_op jit(solution)/shard_map/collide/pallas_call | solution.py:657
  70.4 1.6 %collective-permute-start.15 = (f32[4,2,2,8,512]{4,3,2,1,0:T(8,128)S(1)}, f32[4,2,2,8,512]{4,3,2,1,0:T(8,128)S(1)}, u32[]{:S(2)}, u32[]{:S(2)}) collective-permute-start(f32[4,2,2,8,512]{4,3,2,1,0:T(8,128)S(1)} %get-tuple-element.71), channel_id=1, source_target_pairs={{0,4},{2,6},{4,0},{6,2},{8,12},{10,14},{12,8},{14,10},{16,20},{18,... | collective-permute-start | bytes 786440 | tf_op jit(solution)/shard_map/ppermute | solution.py:572
  72.3 1.6 %collective-permute-start.20 = (f32[4,2,2,8,512]{4,3,2,1,0:T(8,128)S(1)}, f32[4,2,2,8,512]{4,3,2,1,0:T(8,128)S(1)}, u32[]{:S(2)}, u32[]{:S(2)}) collective-permute-start(f32[4,2,2,8,512]{4,3,2,1,0:T(8,128)S(1)} %get-tuple-element.69), channel_id=1, source_target_pairs={{0,4},{2,6},{4,0},{6,2},{8,12},{10,14},{12,8},{14,10},{16,20},{18,... | collective-permute-start | bytes 786440 | tf_op jit(solution)/shard_map/ppermute | solution.py:572
  73.9 5.8 %collective-permute-done.15 = f32[4,2,2,8,512]{4,3,2,1,0:T(8,128)S(1)} collective-permute-done((f32[4,2,2,8,512]{4,3,2,1,0:T(8,128)S(1)}, f32[4,2,2,8,512]{4,3,2,1,0:T(8,128)S(1)}, u32[]{:S(2)}, u32[]{:S(2)}) %collective-permute-start.15) | collective-permute-done | bytes 262176 | tf_op jit(solution)/shard_map/ppermute | solution.py:572
  79.7 2.2 %collective-permute-start.16 = (f32[2,2,2,8,512]{4,3,2,1,0:T(8,128)S(1)}, f32[2,2,2,8,512]{4,3,2,1,0:T(8,128)S(1)}, u32[]{:S(2)}, u32[]{:S(2)}) collective-permute-start(f32[2,2,2,8,512]{4,3,2,1,0:T(8,128)S(1)} %get-tuple-element.87), channel_id=1, source_target_pairs={{0,16},{2,18},{4,20},{6,22},{8,24},{10,26},{12,28},{14,30},{16,0},... | collective-permute-start | bytes 393224 | tf_op jit(solution)/shard_map/ppermute | solution.py:572
  82.6 5.4 %collective-permute-done.16 = f32[2,2,2,8,512]{4,3,2,1,0:T(8,128)S(1)} collective-permute-done((f32[2,2,2,8,512]{4,3,2,1,0:T(8,128)S(1)}, f32[2,2,2,8,512]{4,3,2,1,0:T(8,128)S(1)}, u32[]{:S(2)}, u32[]{:S(2)}) %collective-permute-start.16) | collective-permute-done | bytes 131104 | tf_op jit(solution)/shard_map/ppermute | solution.py:572
  88.2 1.5 %collective-permute-start.21 = (f32[2,2,8,512]{3,2,1,0:T(8,128)S(1)}, f32[2,2,8,512]{3,2,1,0:T(8,128)S(1)}, u32[]{:S(2)}, u32[]{:S(2)}) collective-permute-start(f32[2,2,8,512]{3,2,1,0:T(8,128)S(1)} %get-tuple-element.85), channel_id=1, source_target_pairs={{0,1},{1,0},{2,3},{3,2},{4,5},{5,4},{6,7},{7,6},{8,9},{9,8},{10,11... | collective-permute-start | bytes 196616 | tf_op jit(solution)/shard_map/ppermute | solution.py:582
  89.7 2.0 %collective-permute-start.22 = (f32[2,2,8,512]{3,2,1,0:T(8,128)S(1)}, f32[2,2,8,512]{3,2,1,0:T(8,128)S(1)}, u32[]{:S(2)}, u32[]{:S(2)}) collective-permute-start(f32[2,2,8,512]{3,2,1,0:T(8,128)S(1)} %get-tuple-element.84), channel_id=1, source_target_pairs={{0,9},{1,8},{2,11},{3,10},{4,13},{5,12},{6,15},{7,14},{8,1},{9,0},... | collective-permute-start | bytes 196616 | tf_op jit(solution)/shard_map/ppermute | solution.py:582
  92.5 2.5 %collective-permute-start.24 = (f32[2,2,8,512]{3,2,1,0:T(8,128)S(1)}, f32[2,2,8,512]{3,2,1,0:T(8,128)S(1)}, u32[]{:S(2)}, u32[]{:S(2)}) collective-permute-start(f32[2,2,8,512]{3,2,1,0:T(8,128)S(1)} %get-tuple-element.82), channel_id=1, source_target_pairs={{0,25},{1,24},{2,27},{3,26},{4,29},{5,28},{6,31},{7,30},{8,17},{9,... | collective-permute-start | bytes 196616 | tf_op jit(solution)/shard_map/ppermute | solution.py:582
  95.0 4.6 %collective-permute-done.23.refs_4_ = f32[2,2,8,512]{3,2,1,0:T(8,128)S(1)} collective-permute-done((f32[2,2,8,512]{3,2,1,0:T(8,128)S(1)}, f32[2,2,8,512]{3,2,1,0:T(8,128)S(1)}, u32[]{:S(2)}, u32[]{:S(2)}) %collective-permute-start.23) | collective-permute-done | bytes 65568 | tf_op jit(solution)/shard_map/ppermute | solution.py:582
  100.3 3.0 %collide.10 = (f32[8,2,2,8,512]{4,3,2,1,0:T(8,128)S(1)}, f32[8,2,2,8,512]{4,3,2,1,0:T(8,128)S(1)}) custom-call(f32[2,2,2,8,512]{4,3,2,1,0:T(8,128)S(1)} %get-tuple-element.58.sigma_ref, bf16[2,4,4,2,32,512]{5,4,3,2,1,0:T(8,128)(2,1)S(1)} %get-tuple-element.41.lesser_ref, bf16[2,4,4,2,32,512]{5,4,3,2,1,0:T(8,128)(2,1)S(1)} %get-tuple-element.42.advanced_ref), custom_call_target="tpu_custom_call" | custom-call | flops 16777216 | bytes 4194304 | tf_op jit(solution)/shard_map/collide/pallas_call | solution.py:657
  103.4 1.5 %collective-permute-start.30 = (f32[2,2,2,8,512]{4,3,2,1,0:T(8,128)S(1)}, f32[2,2,2,8,512]{4,3,2,1,0:T(8,128)S(1)}, u32[]{:S(2)}, u32[]{:S(2)}) collective-permute-start(f32[2,2,2,8,512]{4,3,2,1,0:T(8,128)S(1)} %get-tuple-element.61), channel_id=1, source_target_pairs={{0,1},{1,0},{2,3},{3,2},{4,5},{5,4},{6,7},{7,6},{8,9},{9,8},{10,11... | collective-permute-start | bytes 393224 | tf_op jit(solution)/shard_map/ppermute | solution.py:672
  104.9 4.4 %collective-permute-done.30.sigma_ref = f32[2,2,2,8,512]{4,3,2,1,0:T(8,128)S(1)} collective-permute-done((f32[2,2,2,8,512]{4,3,2,1,0:T(8,128)S(1)}, f32[2,2,2,8,512]{4,3,2,1,0:T(8,128)S(1)}, u32[]{:S(2)}, u32[]{:S(2)}) %collective-permute-start.30) | collective-permute-done | bytes 131104 | tf_op jit(solution)/shard_map/ppermute | solution.py:672
  109.3 3.0 %collide.11 = (f32[8,2,2,8,512]{4,3,2,1,0:T(8,128)S(1)}, f32[8,2,2,8,512]{4,3,2,1,0:T(8,128)S(1)}) custom-call(f32[2,2,2,8,512]{4,3,2,1,0:T(8,128)S(1)} %collective-permute-done.30.sigma_ref, bf16[2,4,4,2,32,512]{5,4,3,2,1,0:T(8,128)(2,1)S(1)} %get-tuple-element.41.lesser_ref, bf16[2,4,4,2,32,512]{5,4,3,2,1,0:T(8,128)(2,1)S(1)} %get-tuple-element.42.advanced_ref), custom_call_target="tpu_custom_call" | custom-call | flops 16777216 | bytes 4194304 | tf_op jit(solution)/shard_map/collide/pallas_call | solution.py:657
  112.4 1.6 %collective-permute-start.27 = (f32[4,2,2,8,512]{4,3,2,1,0:T(8,128)S(1)}, f32[4,2,2,8,512]{4,3,2,1,0:T(8,128)S(1)}, u32[]{:S(2)}, u32[]{:S(2)}) collective-permute-start(f32[4,2,2,8,512]{4,3,2,1,0:T(8,128)S(1)} %get-tuple-element.67), channel_id=1, source_target_pairs={{0,4},{2,6},{4,0},{6,2},{8,12},{10,14},{12,8},{14,10},{16,20},{18,... | collective-permute-start | bytes 786440 | tf_op jit(solution)/shard_map/ppermute | solution.py:572
  114.3 1.6 %collective-permute-start.32 = (f32[4,2,2,8,512]{4,3,2,1,0:T(8,128)S(1)}, f32[4,2,2,8,512]{4,3,2,1,0:T(8,128)S(1)}, u32[]{:S(2)}, u32[]{:S(2)}) collective-permute-start(f32[4,2,2,8,512]{4,3,2,1,0:T(8,128)S(1)} %get-tuple-element.65), channel_id=1, source_target_pairs={{0,4},{2,6},{4,0},{6,2},{8,12},{10,14},{12,8},{14,10},{16,20},{18,... | collective-permute-start | bytes 786440 | tf_op jit(solution)/shard_map/ppermute | solution.py:572
  115.9 5.8 %collective-permute-done.27 = f32[4,2,2,8,512]{4,3,2,1,0:T(8,128)S(1)} collective-permute-done((f32[4,2,2,8,512]{4,3,2,1,0:T(8,128)S(1)}, f32[4,2,2,8,512]{4,3,2,1,0:T(8,128)S(1)}, u32[]{:S(2)}, u32[]{:S(2)}) %collective-permute-start.27) | collective-permute-done | bytes 262176 | tf_op jit(solution)/shard_map/ppermute | solution.py:572
  121.7 2.3 %collective-permute-start.28 = (f32[2,2,2,8,512]{4,3,2,1,0:T(8,128)S(1)}, f32[2,2,2,8,512]{4,3,2,1,0:T(8,128)S(1)}, u32[]{:S(2)}, u32[]{:S(2)}) collective-permute-start(f32[2,2,2,8,512]{4,3,2,1,0:T(8,128)S(1)} %get-tuple-element.81), channel_id=1, source_target_pairs={{0,16},{2,18},{4,20},{6,22},{8,24},{10,26},{12,28},{14,30},{16,0},... | collective-permute-start | bytes 393224 | tf_op jit(solution)/shard_map/ppermute | solution.py:572
  124.5 5.6 %collective-permute-done.28 = f32[2,2,2,8,512]{4,3,2,1,0:T(8,128)S(1)} collective-permute-done((f32[2,2,2,8,512]{4,3,2,1,0:T(8,128)S(1)}, f32[2,2,2,8,512]{4,3,2,1,0:T(8,128)S(1)}, u32[]{:S(2)}, u32[]{:S(2)}) %collective-permute-start.28) | collective-permute-done | bytes 131104 | tf_op jit(solution)/shard_map/ppermute | solution.py:572
  130.2 2.1 %collective-permute-start.33 = (f32[2,2,8,512]{3,2,1,0:T(8,128)S(1)}, f32[2,2,8,512]{3,2,1,0:T(8,128)S(1)}, u32[]{:S(2)}, u32[]{:S(2)}) collective-permute-start(f32[2,2,8,512]{3,2,1,0:T(8,128)S(1)} %get-tuple-element.78), channel_id=1, source_target_pairs={{0,8},{2,10},{4,12},{6,14},{8,0},{10,2},{12,4},{14,6},{16,24},{18,... | collective-permute-start | bytes 196616 | tf_op jit(solution)/shard_map/ppermute | solution.py:586
  132.3 1.1 collective-permute-start.34
  133.3 1.4 collective-permute-start.35
  134.8 1.0 collective-permute-done.33.refs_3_
  135.8 4.0 %collective-permute-done.34.refs_4_ = f32[2,2,8,512]{3,2,1,0:T(8,128)S(1)} collective-permute-done((f32[2,2,8,512]{3,2,1,0:T(8,128)S(1)}, f32[2,2,8,512]{3,2,1,0:T(8,128)S(1)}, u32[]{:S(2)}, u32[]{:S(2)}) %collective-permute-start.34) | collective-permute-done | bytes 65568 | tf_op jit(solution)/shard_map/ppermute | solution.py:586
  (77 shorter events, 10.2 us)
Async XLA Ops:
  0.6 0.9 copy-start.3
  1.5 0.9 copy-start.4
  2.4 0.9 copy-start.5
  3.5 10.9 %collective-permute-start = (f32[3,2,2,8,512]{4,3,2,1,0:T(8,128)S(1)}, f32[3,2,2,8,512]{4,3,2,1,0:T(8,128)S(1)}, u32[]{:S(2)}, u32[]{:S(2)}) collective-permute-start(f32[3,2,2,8,512]{4,3,2,1,0:T(8,128)S(1)} %get-tuple-element.36), channel_id=1, source_target_pairs={{0,1},{1,0},{2,3},{3,2},{4,5},{5,4},{6,7},{7,6},{8,9},{9,8},{10,11... | collective-permute-start | bytes 589832 | tf_op jit(solution)/shard_map/ppermute | solution.py:622
  7.3 1.6 %copy-start = (bf16[2,4,4,2,32,512]{5,4,3,2,1,0:T(8,128)(2,1)S(1)}, bf16[2,4,4,2,32,512]{5,4,3,2,1,0:T(8,128)(2,1)}, u32[]{:S(2)}) copy-start(bf16[2,4,4,2,32,512]{5,4,3,2,1,0:T(8,128)(2,1)} %lesser_ref.2) | copy-start | bytes 6291460
  8.9 1.6 %copy-start.1 = (bf16[2,4,4,2,32,512]{5,4,3,2,1,0:T(8,128)(2,1)S(1)}, bf16[2,4,4,2,32,512]{5,4,3,2,1,0:T(8,128)(2,1)}, u32[]{:S(2)}) copy-start(bf16[2,4,4,2,32,512]{5,4,3,2,1,0:T(8,128)(2,1)} %advanced_ref.1) | copy-start | bytes 6291460
  10.4 1.0 copy-start.2
  11.4 0.7 copy-start.6
  12.1 0.7 copy-start.7
  18.1 9.1 %collective-permute-start.2 = (f32[8,2,2,8,512]{4,3,2,1,0:T(8,128)S(1)}, f32[8,2,2,8,512]{4,3,2,1,0:T(8,128)S(1)}, u32[]{:S(2)}, u32[]{:S(2)}) collective-permute-start(f32[8,2,2,8,512]{4,3,2,1,0:T(8,128)S(1)} %get-tuple-element.44), channel_id=1, source_target_pairs={{0,2},{2,0},{4,6},{6,4},{8,10},{10,8},{12,14},{14,12},{16,18},{18,... | collective-permute-start | bytes 1572872 | tf_op jit(solution)/shard_map/ppermute | solution.py:568
  18.1 5.9 %collective-permute-start.6 = (f32[2,2,2,8,512]{4,3,2,1,0:T(8,128)S(1)}, f32[2,2,2,8,512]{4,3,2,1,0:T(8,128)S(1)}, u32[]{:S(2)}, u32[]{:S(2)}) collective-permute-start(f32[2,2,2,8,512]{4,3,2,1,0:T(8,128)S(1)} %get-tuple-element.45), channel_id=1, source_target_pairs={{0,1},{1,0},{2,3},{3,2},{4,5},{5,4},{6,7},{7,6},{8,9},{9,8},{10,11... | collective-permute-start | bytes 393224 | tf_op jit(solution)/shard_map/ppermute | solution.py:672
  27.0 2.3 %collective-permute-start.7 = (f32[8,2,2,8,512]{4,3,2,1,0:T(8,128)S(1)}, f32[8,2,2,8,512]{4,3,2,1,0:T(8,128)S(1)}, u32[]{:S(2)}, u32[]{:S(2)}) collective-permute-start(f32[8,2,2,8,512]{4,3,2,1,0:T(8,128)S(1)} %get-tuple-element.47), channel_id=1, source_target_pairs={{0,2},{2,0},{4,6},{6,4},{8,10},{10,8},{12,14},{14,12},{16,18},{18,... | collective-permute-start | bytes 1572872 | tf_op jit(solution)/shard_map/ppermute | solution.py:568
  27.2 9.2 %collective-permute-start.3 = (f32[4,2,2,8,512]{4,3,2,1,0:T(8,128)S(1)}, f32[4,2,2,8,512]{4,3,2,1,0:T(8,128)S(1)}, u32[]{:S(2)}, u32[]{:S(2)}) collective-permute-start(f32[4,2,2,8,512]{4,3,2,1,0:T(8,128)S(1)} %get-tuple-element.75), channel_id=1, source_target_pairs={{0,4},{2,6},{4,0},{6,2},{8,12},{10,14},{12,8},{14,10},{16,20},{18,... | collective-permute-start | bytes 786440 | tf_op jit(solution)/shard_map/ppermute | solution.py:572
  28.8 21.7 %collective-permute-start.1 = (f32[2,2,8,512]{3,2,1,0:T(8,128)S(1)}, f32[2,2,8,512]{3,2,1,0:T(8,128)S(1)}, u32[]{:S(2)}, u32[]{:S(2)}) collective-permute-start(f32[2,2,8,512]{3,2,1,0:T(8,128)S(1)} %slice_bitcast_fusion.9.near_here_ref.green_here_ref.green_near_ref), channel_id=1, source_target_pairs={{0,1},{1,0},{2,3},{3,2},{4,5},{5,4},{6,7},{7,6},{8,9},{9,8},{10,11... | collective-permute-start | bytes 196616 | tf_op jit(solution)/shard_map/ppermute | solution.py:672
  29.4 16.2 %collective-permute-start.8 = (f32[4,2,2,8,512]{4,3,2,1,0:T(8,128)S(1)}, f32[4,2,2,8,512]{4,3,2,1,0:T(8,128)S(1)}, u32[]{:S(2)}, u32[]{:S(2)}) collective-permute-start(f32[4,2,2,8,512]{4,3,2,1,0:T(8,128)S(1)} %get-tuple-element.73), channel_id=1, source_target_pairs={{0,4},{2,6},{4,0},{6,2},{8,12},{10,14},{12,8},{14,10},{16,20},{18,... | collective-permute-start | bytes 786440 | tf_op jit(solution)/shard_map/ppermute | solution.py:572
  36.5 8.3 %collective-permute-start.4 = (f32[2,2,2,8,512]{4,3,2,1,0:T(8,128)S(1)}, f32[2,2,2,8,512]{4,3,2,1,0:T(8,128)S(1)}, u32[]{:S(2)}, u32[]{:S(2)}) collective-permute-start(f32[2,2,2,8,512]{4,3,2,1,0:T(8,128)S(1)} %get-tuple-element.93), channel_id=1, source_target_pairs={{0,16},{2,18},{4,20},{6,22},{8,24},{10,26},{12,28},{14,30},{16,0},... | collective-permute-start | bytes 393224 | tf_op jit(solution)/shard_map/ppermute | solution.py:572
  44.8 7.6 %collective-permute-start.5 = (f32[1,2,2,8,512]{4,3,2,1,0:T(8,128)S(1)}, f32[1,2,2,8,512]{4,3,2,1,0:T(8,128)S(1)}, u32[]{:S(2)}, u32[]{:S(2)}) collective-permute-start(f32[1,2,2,8,512]{4,3,2,1,0:T(8,128)S(1)} %get-tuple-element.98), channel_id=1, source_target_pairs={{0,8},{2,10},{4,12},{6,14},{8,0},{10,2},{12,4},{14,6},{16,24},{18,... | collective-permute-start | bytes 196616 | tf_op jit(solution)/shard_map/ppermute | solution.py:572
  45.6 6.8 %collective-permute-start.9 = (f32[2,2,8,512]{3,2,1,0:T(8,128)S(1)}, f32[2,2,8,512]{3,2,1,0:T(8,128)S(1)}, u32[]{:S(2)}, u32[]{:S(2)}) collective-permute-start(f32[2,2,8,512]{3,2,1,0:T(8,128)S(1)} %get-tuple-element.91), channel_id=1, source_target_pairs={{0,1},{1,0},{2,3},{3,2},{4,5},{5,4},{6,7},{7,6},{8,9},{9,8},{10,11... | collective-permute-start | bytes 196616 | tf_op jit(solution)/shard_map/ppermute | solution.py:582
  46.2 6.2 %collective-permute-start.10 = (f32[2,2,8,512]{3,2,1,0:T(8,128)S(1)}, f32[2,2,8,512]{3,2,1,0:T(8,128)S(1)}, u32[]{:S(2)}, u32[]{:S(2)}) collective-permute-start(f32[2,2,8,512]{3,2,1,0:T(8,128)S(1)} %get-tuple-element.90), channel_id=1, source_target_pairs={{0,9},{1,8},{2,11},{3,10},{4,13},{5,12},{6,15},{7,14},{8,1},{9,0},... | collective-permute-start | bytes 196616 | tf_op jit(solution)/shard_map/ppermute | solution.py:582
  48.5 8.0 %collective-permute-start.11 = (f32[2,2,8,512]{3,2,1,0:T(8,128)S(1)}, f32[2,2,8,512]{3,2,1,0:T(8,128)S(1)}, u32[]{:S(2)}, u32[]{:S(2)}) collective-permute-start(f32[2,2,8,512]{3,2,1,0:T(8,128)S(1)} %get-tuple-element.89), channel_id=1, source_target_pairs={{0,17},{1,16},{2,19},{3,18},{4,21},{5,20},{6,23},{7,22},{8,25},{9,... | collective-permute-start | bytes 196616 | tf_op jit(solution)/shard_map/ppermute | solution.py:582
  50.5 7.1 %collective-permute-start.12 = (f32[2,2,8,512]{3,2,1,0:T(8,128)S(1)}, f32[2,2,8,512]{3,2,1,0:T(8,128)S(1)}, u32[]{:S(2)}, u32[]{:S(2)}) collective-permute-start(f32[2,2,8,512]{3,2,1,0:T(8,128)S(1)} %get-tuple-element.88), channel_id=1, source_target_pairs={{0,25},{1,24},{2,27},{3,26},{4,29},{5,28},{6,31},{7,30},{8,17},{9,... | collective-permute-start | bytes 196616 | tf_op jit(solution)/shard_map/ppermute | solution.py:582
  61.3 9.1 %collective-permute-start.14 = (f32[8,2,2,8,512]{4,3,2,1,0:T(8,128)S(1)}, f32[8,2,2,8,512]{4,3,2,1,0:T(8,128)S(1)}, u32[]{:S(2)}, u32[]{:S(2)}) collective-permute-start(f32[8,2,2,8,512]{4,3,2,1,0:T(8,128)S(1)} %get-tuple-element.51), channel_id=1, source_target_pairs={{0,2},{2,0},{4,6},{6,4},{8,10},{10,8},{12,14},{14,12},{16,18},{18,... | collective-permute-start | bytes 1572872 | tf_op jit(solution)/shard_map/ppermute | solution.py:568
  61.3 5.9 %collective-permute-start.18 = (f32[2,2,2,8,512]{4,3,2,1,0:T(8,128)S(1)}, f32[2,2,2,8,512]{4,3,2,1,0:T(8,128)S(1)}, u32[]{:S(2)}, u32[]{:S(2)}) collective-permute-start(f32[2,2,2,8,512]{4,3,2,1,0:T(8,128)S(1)} %get-tuple-element.52), channel_id=1, source_target_pairs={{0,1},{1,0},{2,3},{3,2},{4,5},{5,4},{6,7},{7,6},{8,9},{9,8},{10,11... | collective-permute-start | bytes 393224 | tf_op jit(solution)/shard_map/ppermute | solution.py:672
  70.2 2.0 %collective-permute-start.19 = (f32[8,2,2,8,512]{4,3,2,1,0:T(8,128)S(1)}, f32[8,2,2,8,512]{4,3,2,1,0:T(8,128)S(1)}, u32[]{:S(2)}, u32[]{:S(2)}) collective-permute-start(f32[8,2,2,8,512]{4,3,2,1,0:T(8,128)S(1)} %get-tuple-element.54), channel_id=1, source_target_pairs={{0,2},{2,0},{4,6},{6,4},{8,10},{10,8},{12,14},{14,12},{16,18},{18,... | collective-permute-start | bytes 1572872 | tf_op jit(solution)/shard_map/ppermute | solution.py:568
  70.4 9.2 %collective-permute-start.15 = (f32[4,2,2,8,512]{4,3,2,1,0:T(8,128)S(1)}, f32[4,2,2,8,512]{4,3,2,1,0:T(8,128)S(1)}, u32[]{:S(2)}, u32[]{:S(2)}) collective-permute-start(f32[4,2,2,8,512]{4,3,2,1,0:T(8,128)S(1)} %get-tuple-element.71), channel_id=1, source_target_pairs={{0,4},{2,6},{4,0},{6,2},{8,12},{10,14},{12,8},{14,10},{16,20},{18,... | collective-permute-start | bytes 786440 | tf_op jit(solution)/shard_map/ppermute | solution.py:572
  72.3 15.8 %collective-permute-start.20 = (f32[4,2,2,8,512]{4,3,2,1,0:T(8,128)S(1)}, f32[4,2,2,8,512]{4,3,2,1,0:T(8,128)S(1)}, u32[]{:S(2)}, u32[]{:S(2)}) collective-permute-start(f32[4,2,2,8,512]{4,3,2,1,0:T(8,128)S(1)} %get-tuple-element.69), channel_id=1, source_target_pairs={{0,4},{2,6},{4,0},{6,2},{8,12},{10,14},{12,8},{14,10},{16,20},{18,... | collective-permute-start | bytes 786440 | tf_op jit(solution)/shard_map/ppermute | solution.py:572
  79.7 8.3 %collective-permute-start.16 = (f32[2,2,2,8,512]{4,3,2,1,0:T(8,128)S(1)}, f32[2,2,2,8,512]{4,3,2,1,0:T(8,128)S(1)}, u32[]{:S(2)}, u32[]{:S(2)}) collective-permute-start(f32[2,2,2,8,512]{4,3,2,1,0:T(8,128)S(1)} %get-tuple-element.87), channel_id=1, source_target_pairs={{0,16},{2,18},{4,20},{6,22},{8,24},{10,26},{12,28},{14,30},{16,0},... | collective-permute-start | bytes 393224 | tf_op jit(solution)/shard_map/ppermute | solution.py:572
  81.9 10.6 %collective-permute-start.13 = (f32[2,2,2,8,512]{4,3,2,1,0:T(8,128)S(1)}, f32[2,2,2,8,512]{4,3,2,1,0:T(8,128)S(1)}, u32[]{:S(2)}, u32[]{:S(2)}) collective-permute-start(f32[2,2,2,8,512]{4,3,2,1,0:T(8,128)S(1)} %get-tuple-element.48), channel_id=1, source_target_pairs={{0,1},{1,0},{2,3},{3,2},{4,5},{5,4},{6,7},{7,6},{8,9},{9,8},{10,11... | collective-permute-start | bytes 393224 | tf_op jit(solution)/shard_map/ppermute | solution.py:672
  88.0 7.0 %collective-permute-start.17 = (f32[1,2,2,8,512]{4,3,2,1,0:T(8,128)S(1)}, f32[1,2,2,8,512]{4,3,2,1,0:T(8,128)S(1)}, u32[]{:S(2)}, u32[]{:S(2)}) collective-permute-start(f32[1,2,2,8,512]{4,3,2,1,0:T(8,128)S(1)} %get-tuple-element.96), channel_id=1, source_target_pairs={{0,8},{2,10},{4,12},{6,14},{8,0},{10,2},{12,4},{14,6},{16,24},{18,... | collective-permute-start | bytes 196616 | tf_op jit(solution)/shard_map/ppermute | solution.py:572
  88.2 6.8 %collective-permute-start.21 = (f32[2,2,8,512]{3,2,1,0:T(8,128)S(1)}, f32[2,2,8,512]{3,2,1,0:T(8,128)S(1)}, u32[]{:S(2)}, u32[]{:S(2)}) collective-permute-start(f32[2,2,8,512]{3,2,1,0:T(8,128)S(1)} %get-tuple-element.85), channel_id=1, source_target_pairs={{0,1},{1,0},{2,3},{3,2},{4,5},{5,4},{6,7},{7,6},{8,9},{9,8},{10,11... | collective-permute-start | bytes 196616 | tf_op jit(solution)/shard_map/ppermute | solution.py:582
  89.7 5.3 %collective-permute-start.22 = (f32[2,2,8,512]{3,2,1,0:T(8,128)S(1)}, f32[2,2,8,512]{3,2,1,0:T(8,128)S(1)}, u32[]{:S(2)}, u32[]{:S(2)}) collective-permute-start(f32[2,2,8,512]{3,2,1,0:T(8,128)S(1)} %get-tuple-element.84), channel_id=1, source_target_pairs={{0,9},{1,8},{2,11},{3,10},{4,13},{5,12},{6,15},{7,14},{8,1},{9,0},... | collective-permute-start | bytes 196616 | tf_op jit(solution)/shard_map/ppermute | solution.py:582
  91.7 7.9 %collective-permute-start.23 = (f32[2,2,8,512]{3,2,1,0:T(8,128)S(1)}, f32[2,2,8,512]{3,2,1,0:T(8,128)S(1)}, u32[]{:S(2)}, u32[]{:S(2)}) collective-permute-start(f32[2,2,8,512]{3,2,1,0:T(8,128)S(1)} %get-tuple-element.83), channel_id=1, source_target_pairs={{0,17},{1,16},{2,19},{3,18},{4,21},{5,20},{6,23},{7,22},{8,25},{9,... | collective-permute-start | bytes 196616 | tf_op jit(solution)/shard_map/ppermute | solution.py:582
  92.5 7.1 %collective-permute-start.24 = (f32[2,2,8,512]{3,2,1,0:T(8,128)S(1)}, f32[2,2,8,512]{3,2,1,0:T(8,128)S(1)}, u32[]{:S(2)}, u32[]{:S(2)}) collective-permute-start(f32[2,2,8,512]{3,2,1,0:T(8,128)S(1)} %get-tuple-element.82), channel_id=1, source_target_pairs={{0,25},{1,24},{2,27},{3,26},{4,29},{5,28},{6,31},{7,30},{8,17},{9,... | collective-permute-start | bytes 196616 | tf_op jit(solution)/shard_map/ppermute | solution.py:582
  103.3 9.1 %collective-permute-start.26 = (f32[8,2,2,8,512]{4,3,2,1,0:T(8,128)S(1)}, f32[8,2,2,8,512]{4,3,2,1,0:T(8,128)S(1)}, u32[]{:S(2)}, u32[]{:S(2)}) collective-permute-start(f32[8,2,2,8,512]{4,3,2,1,0:T(8,128)S(1)} %get-tuple-element.60), channel_id=1, source_target_pairs={{0,2},{2,0},{4,6},{6,4},{8,10},{10,8},{12,14},{14,12},{16,18},{18,... | collective-permute-start | bytes 1572872 | tf_op jit(solution)/shard_map/ppermute | solution.py:568
  103.4 5.9 %collective-permute-start.30 = (f32[2,2,2,8,512]{4,3,2,1,0:T(8,128)S(1)}, f32[2,2,2,8,512]{4,3,2,1,0:T(8,128)S(1)}, u32[]{:S(2)}, u32[]{:S(2)}) collective-permute-start(f32[2,2,2,8,512]{4,3,2,1,0:T(8,128)S(1)} %get-tuple-element.61), channel_id=1, source_target_pairs={{0,1},{1,0},{2,3},{3,2},{4,5},{5,4},{6,7},{7,6},{8,9},{9,8},{10,11... | collective-permute-start | bytes 393224 | tf_op jit(solution)/shard_map/ppermute | solution.py:672
  112.3 2.0 %collective-permute-start.31 = (f32[8,2,2,8,512]{4,3,2,1,0:T(8,128)S(1)}, f32[8,2,2,8,512]{4,3,2,1,0:T(8,128)S(1)}, u32[]{:S(2)}, u32[]{:S(2)}) collective-permute-start(f32[8,2,2,8,512]{4,3,2,1,0:T(8,128)S(1)} %get-tuple-element.63), channel_id=1, source_target_pairs={{0,2},{2,0},{4,6},{6,4},{8,10},{10,8},{12,14},{14,12},{16,18},{18,... | collective-permute-start | bytes 1572872 | tf_op jit(solution)/shard_map/ppermute | solution.py:568
  112.4 9.2 %collective-permute-start.27 = (f32[4,2,2,8,512]{4,3,2,1,0:T(8,128)S(1)}, f32[4,2,2,8,512]{4,3,2,1,0:T(8,128)S(1)}, u32[]{:S(2)}, u32[]{:S(2)}) collective-permute-start(f32[4,2,2,8,512]{4,3,2,1,0:T(8,128)S(1)} %get-tuple-element.67), channel_id=1, source_target_pairs={{0,4},{2,6},{4,0},{6,2},{8,12},{10,14},{12,8},{14,10},{16,20},{18,... | collective-permute-start | bytes 786440 | tf_op jit(solution)/shard_map/ppermute | solution.py:572
  114.3 15.8 %collective-permute-start.32 = (f32[4,2,2,8,512]{4,3,2,1,0:T(8,128)S(1)}, f32[4,2,2,8,512]{4,3,2,1,0:T(8,128)S(1)}, u32[]{:S(2)}, u32[]{:S(2)}) collective-permute-start(f32[4,2,2,8,512]{4,3,2,1,0:T(8,128)S(1)} %get-tuple-element.65), channel_id=1, source_target_pairs={{0,4},{2,6},{4,0},{6,2},{8,12},{10,14},{12,8},{14,10},{16,20},{18,... | collective-permute-start | bytes 786440 | tf_op jit(solution)/shard_map/ppermute | solution.py:572
  121.7 8.3 %collective-permute-start.28 = (f32[2,2,2,8,512]{4,3,2,1,0:T(8,128)S(1)}, f32[2,2,2,8,512]{4,3,2,1,0:T(8,128)S(1)}, u32[]{:S(2)}, u32[]{:S(2)}) collective-permute-start(f32[2,2,2,8,512]{4,3,2,1,0:T(8,128)S(1)} %get-tuple-element.81), channel_id=1, source_target_pairs={{0,16},{2,18},{4,20},{6,22},{8,24},{10,26},{12,28},{14,30},{16,0},... | collective-permute-start | bytes 393224 | tf_op jit(solution)/shard_map/ppermute | solution.py:572
  124.0 10.7 %collective-permute-start.25 = (f32[2,2,2,8,512]{4,3,2,1,0:T(8,128)S(1)}, f32[2,2,2,8,512]{4,3,2,1,0:T(8,128)S(1)}, u32[]{:S(2)}, u32[]{:S(2)}) collective-permute-start(f32[2,2,2,8,512]{4,3,2,1,0:T(8,128)S(1)} %slice.305), channel_id=1, source_target_pairs={{0,1},{1,0},{2,3},{3,2},{4,5},{5,4},{6,7},{7,6},{8,9},{9,8},{10,11... | collective-permute-start | bytes 393224 | tf_op jit(solution)/shard_map/ppermute | solution.py:672
  130.1 4.7 %collective-permute-start.29 = (f32[1,2,2,8,512]{4,3,2,1,0:T(8,128)S(1)}, f32[1,2,2,8,512]{4,3,2,1,0:T(8,128)S(1)}, u32[]{:S(2)}, u32[]{:S(2)}) collective-permute-start(f32[1,2,2,8,512]{4,3,2,1,0:T(8,128)S(1)} %get-tuple-element.94), channel_id=1, source_target_pairs={{0,8},{2,10},{4,12},{6,14},{8,0},{10,2},{12,4},{14,6},{16,24},{18,... | collective-permute-start | bytes 196616 | tf_op jit(solution)/shard_map/ppermute | solution.py:572
  130.2 5.6 %collective-permute-start.33 = (f32[2,2,8,512]{3,2,1,0:T(8,128)S(1)}, f32[2,2,8,512]{3,2,1,0:T(8,128)S(1)}, u32[]{:S(2)}, u32[]{:S(2)}) collective-permute-start(f32[2,2,8,512]{3,2,1,0:T(8,128)S(1)} %get-tuple-element.78), channel_id=1, source_target_pairs={{0,8},{2,10},{4,12},{6,14},{8,0},{10,2},{12,4},{14,6},{16,24},{18,... | collective-permute-start | bytes 196616 | tf_op jit(solution)/shard_map/ppermute | solution.py:586
  132.3 7.5 %collective-permute-start.34 = (f32[2,2,8,512]{3,2,1,0:T(8,128)S(1)}, f32[2,2,8,512]{3,2,1,0:T(8,128)S(1)}, u32[]{:S(2)}, u32[]{:S(2)}) collective-permute-start(f32[2,2,8,512]{3,2,1,0:T(8,128)S(1)} %get-tuple-element.77), channel_id=1, source_target_pairs={{0,16},{2,18},{4,20},{6,22},{8,24},{10,26},{12,28},{14,30},{16,0},... | collective-permute-start | bytes 196616 | tf_op jit(solution)/shard_map/ppermute | solution.py:586
  133.3 6.4 %collective-permute-start.35 = (f32[2,2,8,512]{3,2,1,0:T(8,128)S(1)}, f32[2,2,8,512]{3,2,1,0:T(8,128)S(1)}, u32[]{:S(2)}, u32[]{:S(2)}) collective-permute-start(f32[2,2,8,512]{3,2,1,0:T(8,128)S(1)} %get-tuple-element.76), channel_id=1, source_target_pairs={{0,24},{2,26},{4,28},{6,30},{8,16},{10,18},{12,20},{14,22},{16,8},... | collective-permute-start | bytes 196616 | tf_op jit(solution)/shard_map/ppermute | solution.py:586

commit v4 on v3

--- a/solution.py
+++ b/solution.py
@@ -297,22 +297,14 @@
                         ]
 
 
-def stage_kernel(
-    blocks_ref, onsite_ref, lesser_ref, advanced_ref, energies_ref, tables_ref, held_ref, masked_ref,
-    energy_ref, onsite_out_ref, table_ref, twiddle_ref
-):
-    ta, ka = lax.axis_index("ta"), lax.axis_index("ka")
-    table_rows = table_ref.shape[1]
-    table_ref[...] = tables_ref[:, :table_rows]
-    turns = tables_ref[:, table_rows:].astype(jnp.float32)
-    twiddle_ref[...] = turns[0] + turns[1]
-    k_local = energy_ref.shape[1]
-    planes, orbitals, _, local_rows, all_times, _ = lesser_ref.shape
+def couple_kernel(onsite_ref, energies_ref, energy_ref, onsite_out_ref):
+    ka = lax.axis_index("ka")
+    orbitals, k_local = onsite_ref.shape[1], energy_ref.shape[1]
+    halves = orbitals // 2
     for side, begin in enumerate((ka * k_local, (1 - ka) * k_local)):
         energy_ref[side : side + 1, :] = energies_ref[
             :, pl.ds(pl.multiple_of(begin, LANES), k_local)
         ]
-    halves = orbitals // 2
     for row in range(orbitals):
         for column in range(orbitals):
             for plane in range(2):
@@ -321,6 +313,17 @@
                 ]
                 place = (plane * orbitals + row) * orbitals + column
                 onsite_out_ref[place : place + 1, :] = jnp.full((1, LANES), value)
+
+
+def stage_kernel(
+    blocks_ref, lesser_ref, advanced_ref, tables_ref, held_ref, masked_ref, table_ref, twiddle_ref
+):
+    ta = lax.axis_index("ta")
+    table_rows = table_ref.shape[1]
+    table_ref[...] = tables_ref[:, :table_rows]
+    turns = tables_ref[:, table_rows:].astype(jnp.float32)
+    twiddle_ref[...] = turns[0] + turns[1]
+    planes, orbitals, _, local_rows, all_times, k_local = lesser_ref.shape
     position = lax.broadcasted_iota(jnp.int32, (all_times, LANES), 0)
     column_times = jnp.zeros((all_times, LANES), jnp.int32)
     for block in range(all_times // local_rows):
@@ -492,13 +495,14 @@
 
 
 def collide_kernel(
-    order, sigma_ref, lesser_ref, advanced_ref, keep_ref, send_ref
+    order, sigma_ref, lesser_ref, advanced_ref, keep_ref, send_ref, summed_ref
 ):
     halves, k_local = sigma_ref.shape[2], sigma_ref.shape[4]
     orbitals, local_rows, times = lesser_ref.shape[1], lesser_ref.shape[3], lesser_ref.shape[4]
     rows = SUBLANES
     time_steps = times // rows
     me = lax.axis_index("ta")
+    summed_ref[...] = sigma_ref[:, 0] + sigma_ref[:, 1]
 
     def gather(total, value):
         return value if total is None else total + value
@@ -520,7 +524,8 @@
                             )
                             for plane in range(2)
                         ]
-                        sigmas.append(triple + [triple[0] + triple[1]])
+                        both = summed_ref[field, half, row : row + 1, lanes]
+                        sigmas.append(triple + [jnp.broadcast_to(both, (rows, LANES))])
                     for outer in range(orbitals):
                         slabs = [
                             slab_ref[plane, inner, outer, stored, here, lanes].astype(jnp.float32)
@@ -620,22 +625,20 @@
         name="pack",
     )(screen_lesser, screen_retarded, green_row)
     arrived_fields = lax.ppermute(far_fields, "ka", flip(1, ka_count))
-    lesser_slab, advanced_slab, energy, onsite, table, twiddle = pl.pallas_call(
+    lesser_slab, advanced_slab, table, twiddle = pl.pallas_call(
         stage_kernel,
         out_shape=(
             jax.ShapeDtypeStruct(lesser_slab.shape, lesser_slab.dtype),
             jax.ShapeDtypeStruct(advanced_slab.shape, advanced_slab.dtype),
-            float_like(2, k_local),
-            float_like(2 * orbitals * orbitals, LANES),
             jax.ShapeDtypeStruct((2, 2 * LANES, 2 * LANES), tables_in.dtype),
             float_like(tiles, 2 * LANES),
         ),
-        in_specs=[scalar] * 2 + [whole()] * 4,
-        out_specs=(whole(),) * 6,
+        in_specs=[scalar] + [whole()] * 3,
+        out_specs=(whole(),) * 4,
         compiler_params=small,
         cost_estimate=hint,
         name="stage",
-    )(block_table, onsite, lesser_slab, advanced_slab, energies, tables_in)
+    )(block_table, lesser_slab, advanced_slab, tables_in)
     green_near, green_far, green_there = near_fields[2], far_fields[2], arrived_fields[2]
 
     screens, sigma_near, sigma_send = pl.pallas_call(
@@ -659,6 +662,7 @@
             out_shape=(float_like(ta_count // 2, *chunk),) * 2,
             in_specs=[whole()] * 3,
             out_specs=(whole(),) * 2,
+            scratch_shapes=[pltpu.VMEM((2,) + chunk[1:], jnp.float32)],
             compiler_params=small,
             cost_estimate=pl.CostEstimate(
                 flops=16 * halves * orbitals * orbitals * local_rows * all_times * k_local,
@@ -687,6 +691,16 @@
         is_first = corrector == 0
         near_sums, far_sums = collisions(sigma_near, sigma_send, ka_count)
         if is_first:
+            energy, onsite = pl.pallas_call(
+                couple_kernel,
+                out_shape=(
+                    float_like(2, k_local), float_like(2 * orbitals * orbitals, LANES)
+                ),
+                in_specs=[scalar, whole()],
+                out_specs=(whole(),) * 2,
+                compiler_params=small,
+                name="couple",
+            )(onsite, energies)
             far_there = exchanged(green_near)
         else:
             swapped = exchanged(estimate)

time: 141 us -> 133 us (0.943)
  waiting for transfers between devices: 63.7 us -> 58.9 us
  starting transfers between devices: 43.6 us -> 41 us
    ppermute x12, starting transfers between devices: 17.2 us -> 13.5 us  [halved_sum(): got = lax.ppermute(outgoing, 'ta', flip(1 << bit, ta_count))]
    ppermute x12, waiting for transfers between devices: 34 us -> 30.5 us  [halved_sum(): got = lax.ppermute(outgoing, 'ta', flip(1 << bit, ta_count))]
  transfers between devices with their start and end apart: 36 -> 36, of which waited for: 16 -> 19; matrix products, arithmetic and copies ran while one was open for 1% -> 1% of each run, Pallas kernels for 8% -> 8%
where the time goes in v4:
time: 133 us
  waiting for transfers between devices  58.9 us (44%)
  starting transfers between devices  41 us (31%)
  Pallas kernels  23 us (17%)
  local copies, waits for them, and re-layouts  7.56 us (6%)
  between operations  1.65 us (1%)
    ppermute x12, waiting for transfers between devices, halved_sum(): got = lax.ppermute(outgoing, 'ta', flip(1 << bit, ta_count))  30.5 us
    pallas_call x6, Pallas kernels, collide(): pl.pallas_call(functools.partial(collide_kernel, order), out_shape=(float...  17.9 us
    ppermute x6, waiting for transfers between devices, exchanged(): return lax.ppermute(value, 'ka', flip(1, ka_count))  15 us
    ppermute x8, starting transfers between devices, halved_sum(): results.append(lax.ppermute(pieces[place], ('ta', 'ka'), pairs))  14.1 us
    ppermute x12, starting transfers between devices, halved_sum(): got = lax.ppermute(outgoing, 'ta', flip(1 << bit, ta_count))  13.5 us
    ppermute x8, waiting for transfers between devices, halved_sum(): results.append(lax.ppermute(pieces[place], ('ta', 'ka'), pairs))  8.95 us
    unnamed x16, local copies, waits for them, and re-layouts  7.5 us
    ppermute x6, starting transfers between devices, exchanged(): return lax.ppermute(value, 'ka', flip(1, ka_count))  5.5 us
  transfers between devices with their start and end apart: 36, of which 19 were waited for; matrix products, arithmetic and copies ran while one was open for 1% of the time, Pallas kernels for 8%

profile of v4, /device:TPU:0, one launch (start us, length us, event | category | flops | bytes accessed | tf_op | source)
XLA Modules:
  0.0 133.0 jit_solution(14839206222143299817)
XLA Ops:
  0.6 0.9 copy-done.3
  1.5 0.9 copy-done.4
  2.4 0.9 copy-done.5
  3.5 3.0 %collective-permute-start = (f32[3,2,2,8,512]{4,3,2,1,0:T(8,128)S(1)}, f32[3,2,2,8,512]{4,3,2,1,0:T(8,128)S(1)}, u32[]{:S(2)}, u32[]{:S(2)}) collective-permute-start(f32[3,2,2,8,512]{4,3,2,1,0:T(8,128)S(1)} %get-tuple-element.36), channel_id=1, source_target_pairs={{0,1},{1,0},{2,3},{3,2},{4,5},{5,4},{6,7},{7,6},{8,9},{9,8},{10,11... | collective-permute-start | bytes 589832 | tf_op jit(solution)/shard_map/ppermute | solution.py:627
  6.5 1.6 %copy-done = bf16[2,4,4,2,32,512]{5,4,3,2,1,0:T(8,128)(2,1)S(1)} copy-done((bf16[2,4,4,2,32,512]{5,4,3,2,1,0:T(8,128)(2,1)S(1)}, bf16[2,4,4,2,32,512]{5,4,3,2,1,0:T(8,128)(2,1)}, u32[]{:S(2)}) %copy-start) | copy-done | bytes 2097176
  8.1 1.6 %copy-done.1 = bf16[2,4,4,2,32,512]{5,4,3,2,1,0:T(8,128)(2,1)S(1)} copy-done((bf16[2,4,4,2,32,512]{5,4,3,2,1,0:T(8,128)(2,1)S(1)}, bf16[2,4,4,2,32,512]{5,4,3,2,1,0:T(8,128)(2,1)}, u32[]{:S(2)}) %copy-start.1) | copy-done | bytes 2097176
  9.7 1.0 copy-done.2
  11.3 1.5 %stage.1 = (bf16[2,4,4,2,32,512]{5,4,3,2,1,0:T(8,128)(2,1)S(1)}, bf16[2,4,4,2,32,512]{5,4,3,2,1,0:T(8,128)(2,1)S(1)}, bf16[2,256,256]{2,1,0:T(8,128)(2,1)S(1)}, f32[8,256]{1,0:T(8,128)S(1)}) custom-call(s32[16]{0:T(128)S(1)} %copy-done.7, bf16[2,4,4,2,32,512]{5,4,3,2,1,0:T(8,128)(2,1)S(1)} %copy-done, bf16[2,4,4,2,32,512]{5,4,3,2,1,0:T(8,128)(2,1)S(1)} %copy-done.1, ...), custom_call_target="tpu_custom_call" | custom-call | flops 8388608 | bytes 8388608 | tf_op jit(solution)/shard_map/stage/pallas_call | solution.py:628
  13.5 3.0 %collide.6 = (f32[8,2,2,8,512]{4,3,2,1,0:T(8,128)S(1)}, f32[8,2,2,8,512]{4,3,2,1,0:T(8,128)S(1)}) custom-call(f32[2,2,2,8,512]{4,3,2,1,0:T(8,128)S(1)} %get-tuple-element.40.sigma_ref, bf16[2,4,4,2,32,512]{5,4,3,2,1,0:T(8,128)(2,1)S(1)} %get-tuple-element.41.lesser_ref, bf16[2,4,4,2,32,512]{5,4,3,2,1,0:T(8,128)(2,1)S(1)} %get-tuple-element.42.advanced_ref), custom_call_target="tpu_custom_call" | custom-call | flops 16777216 | bytes 4194304 | tf_op jit(solution)/shard_map/collide/pallas_call | solution.py:660
  16.9 5.5 %collective-permute-done.6.sigma_ref = f32[2,2,2,8,512]{4,3,2,1,0:T(8,128)S(1)} collective-permute-done((f32[2,2,2,8,512]{4,3,2,1,0:T(8,128)S(1)}, f32[2,2,2,8,512]{4,3,2,1,0:T(8,128)S(1)}, u32[]{:S(2)}, u32[]{:S(2)}) %collective-permute-start.6) | collective-permute-done | bytes 131104 | tf_op jit(solution)/shard_map/ppermute | solution.py:676
  22.5 3.0 %collide.7 = (f32[8,2,2,8,512]{4,3,2,1,0:T(8,128)S(1)}, f32[8,2,2,8,512]{4,3,2,1,0:T(8,128)S(1)}) custom-call(f32[2,2,2,8,512]{4,3,2,1,0:T(8,128)S(1)} %collective-permute-done.6.sigma_ref, bf16[2,4,4,2,32,512]{5,4,3,2,1,0:T(8,128)(2,1)S(1)} %get-tuple-element.41.lesser_ref, bf16[2,4,4,2,32,512]{5,4,3,2,1,0:T(8,128)(2,1)S(1)} %get-tuple-element.42.advanced_ref), custom_call_target="tpu_custom_call" | custom-call | flops 16777216 | bytes 4194304 | tf_op jit(solution)/shard_map/collide/pallas_call | solution.py:660
  26.0 1.8 %collective-permute-start.3 = (f32[4,2,2,8,512]{4,3,2,1,0:T(8,128)S(1)}, f32[4,2,2,8,512]{4,3,2,1,0:T(8,128)S(1)}, u32[]{:S(2)}, u32[]{:S(2)}) collective-permute-start(f32[4,2,2,8,512]{4,3,2,1,0:T(8,128)S(1)} %get-tuple-element.75), channel_id=1, source_target_pairs={{0,4},{2,6},{4,0},{6,2},{8,12},{10,14},{12,8},{14,10},{16,20},{18,... | collective-permute-start | bytes 786440 | tf_op jit(solution)/shard_map/ppermute | solution.py:577
  29.1 6.1 %collective-permute-done.3 = f32[4,2,2,8,512]{4,3,2,1,0:T(8,128)S(1)} collective-permute-done((f32[4,2,2,8,512]{4,3,2,1,0:T(8,128)S(1)}, f32[4,2,2,8,512]{4,3,2,1,0:T(8,128)S(1)}, u32[]{:S(2)}, u32[]{:S(2)}) %collective-permute-start.3) | collective-permute-done | bytes 262176 | tf_op jit(solution)/shard_map/ppermute | solution.py:577
  35.3 2.9 %collective-permute-start.4 = (f32[2,2,2,8,512]{4,3,2,1,0:T(8,128)S(1)}, f32[2,2,2,8,512]{4,3,2,1,0:T(8,128)S(1)}, u32[]{:S(2)}, u32[]{:S(2)}) collective-permute-start(f32[2,2,2,8,512]{4,3,2,1,0:T(8,128)S(1)} %get-tuple-element.93), channel_id=1, source_target_pairs={{0,16},{2,18},{4,20},{6,22},{8,24},{10,26},{12,28},{14,30},{16,0},... | collective-permute-start | bytes 393224 | tf_op jit(solution)/shard_map/ppermute | solution.py:577
  39.0 4.2 %collective-permute-done.4 = f32[2,2,2,8,512]{4,3,2,1,0:T(8,128)S(1)} collective-permute-done((f32[2,2,2,8,512]{4,3,2,1,0:T(8,128)S(1)}, f32[2,2,2,8,512]{4,3,2,1,0:T(8,128)S(1)}, u32[]{:S(2)}, u32[]{:S(2)}) %collective-permute-start.4) | collective-permute-done | bytes 131104 | tf_op jit(solution)/shard_map/ppermute | solution.py:577
  44.0 2.3 %collective-permute-start.10 = (f32[2,2,8,512]{3,2,1,0:T(8,128)S(1)}, f32[2,2,8,512]{3,2,1,0:T(8,128)S(1)}, u32[]{:S(2)}, u32[]{:S(2)}) collective-permute-start(f32[2,2,8,512]{3,2,1,0:T(8,128)S(1)} %get-tuple-element.90), channel_id=1, source_target_pairs={{0,9},{1,8},{2,11},{3,10},{4,13},{5,12},{6,15},{7,14},{8,1},{9,0},... | collective-permute-start | bytes 196616 | tf_op jit(solution)/shard_map/ppermute | solution.py:587
  46.3 2.1 %collective-permute-start.11 = (f32[2,2,8,512]{3,2,1,0:T(8,128)S(1)}, f32[2,2,8,512]{3,2,1,0:T(8,128)S(1)}, u32[]{:S(2)}, u32[]{:S(2)}) collective-permute-start(f32[2,2,8,512]{3,2,1,0:T(8,128)S(1)} %get-tuple-element.89), channel_id=1, source_target_pairs={{0,17},{1,16},{2,19},{3,18},{4,21},{5,20},{6,23},{7,22},{8,25},{9,... | collective-permute-start | bytes 196616 | tf_op jit(solution)/shard_map/ppermute | solution.py:587
  48.5 1.8 %collective-permute-start.12 = (f32[2,2,8,512]{3,2,1,0:T(8,128)S(1)}, f32[2,2,8,512]{3,2,1,0:T(8,128)S(1)}, u32[]{:S(2)}, u32[]{:S(2)}) collective-permute-start(f32[2,2,8,512]{3,2,1,0:T(8,128)S(1)} %get-tuple-element.88), channel_id=1, source_target_pairs={{0,25},{1,24},{2,27},{3,26},{4,29},{5,28},{6,31},{7,30},{8,17},{9,... | collective-permute-start | bytes 196616 | tf_op jit(solution)/shard_map/ppermute | solution.py:587
  50.3 1.0 collective-permute-start.9
  51.3 3.0 %collective-permute-done.11.refs_4_ = f32[2,2,8,512]{3,2,1,0:T(8,128)S(1)} collective-permute-done((f32[2,2,8,512]{3,2,1,0:T(8,128)S(1)}, f32[2,2,8,512]{3,2,1,0:T(8,128)S(1)}, u32[]{:S(2)}, u32[]{:S(2)}) %collective-permute-start.11) | collective-permute-done | bytes 65568 | tf_op jit(solution)/shard_map/ppermute | solution.py:587
  54.3 1.2 collective-permute-done.12.refs_5_
  56.2 3.0 %collide.8 = (f32[8,2,2,8,512]{4,3,2,1,0:T(8,128)S(1)}, f32[8,2,2,8,512]{4,3,2,1,0:T(8,128)S(1)}) custom-call(f32[2,2,2,8,512]{4,3,2,1,0:T(8,128)S(1)} %get-tuple-element.49.sigma_ref, bf16[2,4,4,2,32,512]{5,4,3,2,1,0:T(8,128)(2,1)S(1)} %get-tuple-element.41.lesser_ref, bf16[2,4,4,2,32,512]{5,4,3,2,1,0:T(8,128)(2,1)S(1)} %get-tuple-element.42.advanced_ref), custom_call_target="tpu_custom_call" | custom-call | flops 16777216 | bytes 4194304 | tf_op jit(solution)/shard_map/collide/pallas_call | solution.py:660
  59.3 1.4 %collective-permute-start.18 = (f32[2,2,2,8,512]{4,3,2,1,0:T(8,128)S(1)}, f32[2,2,2,8,512]{4,3,2,1,0:T(8,128)S(1)}, u32[]{:S(2)}, u32[]{:S(2)}) collective-permute-start(f32[2,2,2,8,512]{4,3,2,1,0:T(8,128)S(1)} %get-tuple-element.52), channel_id=1, source_target_pairs={{0,1},{1,0},{2,3},{3,2},{4,5},{5,4},{6,7},{7,6},{8,9},{9,8},{10,11... | collective-permute-start | bytes 393224 | tf_op jit(solution)/shard_map/ppermute | solution.py:676
  60.7 4.5 %collective-permute-done.18.sigma_ref = f32[2,2,2,8,512]{4,3,2,1,0:T(8,128)S(1)} collective-permute-done((f32[2,2,2,8,512]{4,3,2,1,0:T(8,128)S(1)}, f32[2,2,2,8,512]{4,3,2,1,0:T(8,128)S(1)}, u32[]{:S(2)}, u32[]{:S(2)}) %collective-permute-start.18) | collective-permute-done | bytes 131104 | tf_op jit(solution)/shard_map/ppermute | solution.py:676
  65.2 3.0 %collide.9 = (f32[8,2,2,8,512]{4,3,2,1,0:T(8,128)S(1)}, f32[8,2,2,8,512]{4,3,2,1,0:T(8,128)S(1)}) custom-call(f32[2,2,2,8,512]{4,3,2,1,0:T(8,128)S(1)} %collective-permute-done.18.sigma_ref, bf16[2,4,4,2,32,512]{5,4,3,2,1,0:T(8,128)(2,1)S(1)} %get-tuple-element.41.lesser_ref, bf16[2,4,4,2,32,512]{5,4,3,2,1,0:T(8,128)(2,1)S(1)} %get-tuple-element.42.advanced_ref), custom_call_target="tpu_custom_call" | custom-call | flops 16777216 | bytes 4194304 | tf_op jit(solution)/shard_map/collide/pallas_call | solution.py:660
  68.3 1.4 %collective-permute-start.13 = (f32[2,2,2,8,512]{4,3,2,1,0:T(8,128)S(1)}, f32[2,2,2,8,512]{4,3,2,1,0:T(8,128)S(1)}, u32[]{:S(2)}, u32[]{:S(2)}) collective-permute-start(f32[2,2,2,8,512]{4,3,2,1,0:T(8,128)S(1)} %get-tuple-element.48), channel_id=1, source_target_pairs={{0,1},{1,0},{2,3},{3,2},{4,5},{5,4},{6,7},{7,6},{8,9},{9,8},{10,11... | collective-permute-start | bytes 393224 | tf_op jit(solution)/shard_map/ppermute | solution.py:676
  69.8 1.6 %collective-permute-start.15 = (f32[4,2,2,8,512]{4,3,2,1,0:T(8,128)S(1)}, f32[4,2,2,8,512]{4,3,2,1,0:T(8,128)S(1)}, u32[]{:S(2)}, u32[]{:S(2)}) collective-permute-start(f32[4,2,2,8,512]{4,3,2,1,0:T(8,128)S(1)} %get-tuple-element.71), channel_id=1, source_target_pairs={{0,4},{2,6},{4,0},{6,2},{8,12},{10,14},{12,8},{14,10},{16,20},{18,... | collective-permute-start | bytes 786440 | tf_op jit(solution)/shard_map/ppermute | solution.py:577
  72.0 7.0 %collective-permute-done.15 = f32[4,2,2,8,512]{4,3,2,1,0:T(8,128)S(1)} collective-permute-done((f32[4,2,2,8,512]{4,3,2,1,0:T(8,128)S(1)}, f32[4,2,2,8,512]{4,3,2,1,0:T(8,128)S(1)}, u32[]{:S(2)}, u32[]{:S(2)}) %collective-permute-start.15) | collective-permute-done | bytes 262176 | tf_op jit(solution)/shard_map/ppermute | solution.py:577
  79.1 1.4 %collective-permute-start.16 = (f32[2,2,2,8,512]{4,3,2,1,0:T(8,128)S(1)}, f32[2,2,2,8,512]{4,3,2,1,0:T(8,128)S(1)}, u32[]{:S(2)}, u32[]{:S(2)}) collective-permute-start(f32[2,2,2,8,512]{4,3,2,1,0:T(8,128)S(1)} %get-tuple-element.87), channel_id=1, source_target_pairs={{0,16},{2,18},{4,20},{6,22},{8,24},{10,26},{12,28},{14,30},{16,0},... | collective-permute-start | bytes 393224 | tf_op jit(solution)/shard_map/ppermute | solution.py:577
  80.4 3.4 %collective-permute-done.20 = f32[4,2,2,8,512]{4,3,2,1,0:T(8,128)S(1)} collective-permute-done((f32[4,2,2,8,512]{4,3,2,1,0:T(8,128)S(1)}, f32[4,2,2,8,512]{4,3,2,1,0:T(8,128)S(1)}, u32[]{:S(2)}, u32[]{:S(2)}) %collective-permute-start.20) | collective-permute-done | bytes 262176 | tf_op jit(solution)/shard_map/ppermute | solution.py:577
  84.6 1.6 %collective-permute-start.22 = (f32[2,2,8,512]{3,2,1,0:T(8,128)S(1)}, f32[2,2,8,512]{3,2,1,0:T(8,128)S(1)}, u32[]{:S(2)}, u32[]{:S(2)}) collective-permute-start(f32[2,2,8,512]{3,2,1,0:T(8,128)S(1)} %get-tuple-element.84), channel_id=1, source_target_pairs={{0,9},{1,8},{2,11},{3,10},{4,13},{5,12},{6,15},{7,14},{8,1},{9,0},... | collective-permute-start | bytes 196616 | tf_op jit(solution)/shard_map/ppermute | solution.py:587
  86.2 2.2 %collective-permute-start.23 = (f32[2,2,8,512]{3,2,1,0:T(8,128)S(1)}, f32[2,2,8,512]{3,2,1,0:T(8,128)S(1)}, u32[]{:S(2)}, u32[]{:S(2)}) collective-permute-start(f32[2,2,8,512]{3,2,1,0:T(8,128)S(1)} %get-tuple-element.83), channel_id=1, source_target_pairs={{0,17},{1,16},{2,19},{3,18},{4,21},{5,20},{6,23},{7,22},{8,25},{9,... | collective-permute-start | bytes 196616 | tf_op jit(solution)/shard_map/ppermute | solution.py:587
  88.4 2.2 %collective-permute-start.24 = (f32[2,2,8,512]{3,2,1,0:T(8,128)S(1)}, f32[2,2,8,512]{3,2,1,0:T(8,128)S(1)}, u32[]{:S(2)}, u32[]{:S(2)}) collective-permute-start(f32[2,2,8,512]{3,2,1,0:T(8,128)S(1)} %get-tuple-element.82), channel_id=1, source_target_pairs={{0,25},{1,24},{2,27},{3,26},{4,29},{5,28},{6,31},{7,30},{8,17},{9,... | collective-permute-start | bytes 196616 | tf_op jit(solution)/shard_map/ppermute | solution.py:587
  90.8 3.0 %collective-permute-done.23.refs_4_ = f32[2,2,8,512]{3,2,1,0:T(8,128)S(1)} collective-permute-done((f32[2,2,8,512]{3,2,1,0:T(8,128)S(1)}, f32[2,2,8,512]{3,2,1,0:T(8,128)S(1)}, u32[]{:S(2)}, u32[]{:S(2)}) %collective-permute-start.23) | collective-permute-done | bytes 65568 | tf_op jit(solution)/shard_map/ppermute | solution.py:587
  93.9 1.6 %collective-permute-done.24.refs_5_ = f32[2,2,8,512]{3,2,1,0:T(8,128)S(1)} collective-permute-done((f32[2,2,8,512]{3,2,1,0:T(8,128)S(1)}, f32[2,2,8,512]{3,2,1,0:T(8,128)S(1)}, u32[]{:S(2)}, u32[]{:S(2)}) %collective-permute-start.24) | collective-permute-done | bytes 65568 | tf_op jit(solution)/shard_map/ppermute | solution.py:587
  96.2 3.0 %collide.10 = (f32[8,2,2,8,512]{4,3,2,1,0:T(8,128)S(1)}, f32[8,2,2,8,512]{4,3,2,1,0:T(8,128)S(1)}) custom-call(f32[2,2,2,8,512]{4,3,2,1,0:T(8,128)S(1)} %get-tuple-element.58.sigma_ref, bf16[2,4,4,2,32,512]{5,4,3,2,1,0:T(8,128)(2,1)S(1)} %get-tuple-element.41.lesser_ref, bf16[2,4,4,2,32,512]{5,4,3,2,1,0:T(8,128)(2,1)S(1)} %get-tuple-element.42.advanced_ref), custom_call_target="tpu_custom_call" | custom-call | flops 16777216 | bytes 4194304 | tf_op jit(solution)/shard_map/collide/pallas_call | solution.py:660
  99.2 1.0 collective-permute-start.30
  100.2 4.9 %collective-permute-done.30.sigma_ref = f32[2,2,2,8,512]{4,3,2,1,0:T(8,128)S(1)} collective-permute-done((f32[2,2,2,8,512]{4,3,2,1,0:T(8,128)S(1)}, f32[2,2,2,8,512]{4,3,2,1,0:T(8,128)S(1)}, u32[]{:S(2)}, u32[]{:S(2)}) %collective-permute-start.30) | collective-permute-done | bytes 131104 | tf_op jit(solution)/shard_map/ppermute | solution.py:676
  105.1 3.0 %collide.11 = (f32[8,2,2,8,512]{4,3,2,1,0:T(8,128)S(1)}, f32[8,2,2,8,512]{4,3,2,1,0:T(8,128)S(1)}) custom-call(f32[2,2,2,8,512]{4,3,2,1,0:T(8,128)S(1)} %collective-permute-done.30.sigma_ref, bf16[2,4,4,2,32,512]{5,4,3,2,1,0:T(8,128)(2,1)S(1)} %get-tuple-element.41.lesser_ref, bf16[2,4,4,2,32,512]{5,4,3,2,1,0:T(8,128)(2,1)S(1)} %get-tuple-element.42.advanced_ref), custom_call_target="tpu_custom_call" | custom-call | flops 16777216 | bytes 4194304 | tf_op jit(solution)/shard_map/collide/pallas_call | solution.py:660
  108.3 1.6 %collective-permute-start.27 = (f32[4,2,2,8,512]{4,3,2,1,0:T(8,128)S(1)}, f32[4,2,2,8,512]{4,3,2,1,0:T(8,128)S(1)}, u32[]{:S(2)}, u32[]{:S(2)}) collective-permute-start(f32[4,2,2,8,512]{4,3,2,1,0:T(8,128)S(1)} %get-tuple-element.67), channel_id=1, source_target_pairs={{0,4},{2,6},{4,0},{6,2},{8,12},{10,14},{12,8},{14,10},{16,20},{18,... | collective-permute-start | bytes 786440 | tf_op jit(solution)/shard_map/ppermute | solution.py:577
  110.2 1.6 %collective-permute-start.32 = (f32[4,2,2,8,512]{4,3,2,1,0:T(8,128)S(1)}, f32[4,2,2,8,512]{4,3,2,1,0:T(8,128)S(1)}, u32[]{:S(2)}, u32[]{:S(2)}) collective-permute-start(f32[4,2,2,8,512]{4,3,2,1,0:T(8,128)S(1)} %get-tuple-element.65), channel_id=1, source_target_pairs={{0,4},{2,6},{4,0},{6,2},{8,12},{10,14},{12,8},{14,10},{16,20},{18,... | collective-permute-start | bytes 786440 | tf_op jit(solution)/shard_map/ppermute | solution.py:577
  111.8 1.0 collective-permute-start.25
  112.8 4.8 %collective-permute-done.27 = f32[4,2,2,8,512]{4,3,2,1,0:T(8,128)S(1)} collective-permute-done((f32[4,2,2,8,512]{4,3,2,1,0:T(8,128)S(1)}, f32[4,2,2,8,512]{4,3,2,1,0:T(8,128)S(1)}, u32[]{:S(2)}, u32[]{:S(2)}) %collective-permute-start.27) | collective-permute-done | bytes 262176 | tf_op jit(solution)/shard_map/ppermute | solution.py:577
  118.3 4.4 %collective-permute-done.32 = f32[4,2,2,8,512]{4,3,2,1,0:T(8,128)S(1)} collective-permute-done((f32[4,2,2,8,512]{4,3,2,1,0:T(8,128)S(1)}, f32[4,2,2,8,512]{4,3,2,1,0:T(8,128)S(1)}, u32[]{:S(2)}, u32[]{:S(2)}) %collective-permute-start.32) | collective-permute-done | bytes 262176 | tf_op jit(solution)/shard_map/ppermute | solution.py:577
  122.9 2.3 %collective-permute-start.34 = (f32[2,2,8,512]{3,2,1,0:T(8,128)S(1)}, f32[2,2,8,512]{3,2,1,0:T(8,128)S(1)}, u32[]{:S(2)}, u32[]{:S(2)}) collective-permute-start(f32[2,2,8,512]{3,2,1,0:T(8,128)S(1)} %get-tuple-element.77), channel_id=1, source_target_pairs={{0,16},{2,18},{4,20},{6,22},{8,24},{10,26},{12,28},{14,30},{16,0},... | collective-permute-start | bytes 196616 | tf_op jit(solution)/shard_map/ppermute | solution.py:591
  125.3 1.9 %collective-permute-start.35 = (f32[2,2,8,512]{3,2,1,0:T(8,128)S(1)}, f32[2,2,8,512]{3,2,1,0:T(8,128)S(1)}, u32[]{:S(2)}, u32[]{:S(2)}) collective-permute-start(f32[2,2,8,512]{3,2,1,0:T(8,128)S(1)} %get-tuple-element.76), channel_id=1, source_target_pairs={{0,24},{2,26},{4,28},{6,30},{8,16},{10,18},{12,20},{14,22},{16,8},... | collective-permute-start | bytes 196616 | tf_op jit(solution)/shard_map/ppermute | solution.py:591
  127.6 2.7 %collective-permute-done.34.refs_4_ = f32[2,2,8,512]{3,2,1,0:T(8,128)S(1)} collective-permute-done((f32[2,2,8,512]{3,2,1,0:T(8,128)S(1)}, f32[2,2,8,512]{3,2,1,0:T(8,128)S(1)}, u32[]{:S(2)}, u32[]{:S(2)}) %collective-permute-start.34) | collective-permute-done | bytes 65568 | tf_op jit(solution)/shard_map/ppermute | solution.py:591
  130.2 1.3 %collective-permute-done.35.refs_5_ = f32[2,2,8,512]{3,2,1,0:T(8,128)S(1)} collective-permute-done((f32[2,2,8,512]{3,2,1,0:T(8,128)S(1)}, f32[2,2,8,512]{3,2,1,0:T(8,128)S(1)}, u32[]{:S(2)}, u32[]{:S(2)}) %collective-permute-start.35) | collective-permute-done | bytes 65568 | tf_op jit(solution)/shard_map/ppermute | solution.py:591
  (78 shorter events, 11.1 us)
Async XLA Ops:
  0.6 0.9 copy-start.3
  1.5 0.9 copy-start.4
  2.4 0.9 copy-start.5
  3.5 9.4 %collective-permute-start = (f32[3,2,2,8,512]{4,3,2,1,0:T(8,128)S(1)}, f32[3,2,2,8,512]{4,3,2,1,0:T(8,128)S(1)}, u32[]{:S(2)}, u32[]{:S(2)}) collective-permute-start(f32[3,2,2,8,512]{4,3,2,1,0:T(8,128)S(1)} %get-tuple-element.36), channel_id=1, source_target_pairs={{0,1},{1,0},{2,3},{3,2},{4,5},{5,4},{6,7},{7,6},{8,9},{9,8},{10,11... | collective-permute-start | bytes 589832 | tf_op jit(solution)/shard_map/ppermute | solution.py:627
  6.5 1.6 %copy-start = (bf16[2,4,4,2,32,512]{5,4,3,2,1,0:T(8,128)(2,1)S(1)}, bf16[2,4,4,2,32,512]{5,4,3,2,1,0:T(8,128)(2,1)}, u32[]{:S(2)}) copy-start(bf16[2,4,4,2,32,512]{5,4,3,2,1,0:T(8,128)(2,1)} %lesser_ref.3) | copy-start | bytes 6291460
  8.1 1.6 %copy-start.1 = (bf16[2,4,4,2,32,512]{5,4,3,2,1,0:T(8,128)(2,1)S(1)}, bf16[2,4,4,2,32,512]{5,4,3,2,1,0:T(8,128)(2,1)}, u32[]{:S(2)}) copy-start(bf16[2,4,4,2,32,512]{5,4,3,2,1,0:T(8,128)(2,1)} %advanced_ref.1) | copy-start | bytes 6291460
  9.7 1.0 copy-start.2
  10.6 0.7 copy-start.7
  16.5 9.4 %collective-permute-start.2 = (f32[8,2,2,8,512]{4,3,2,1,0:T(8,128)S(1)}, f32[8,2,2,8,512]{4,3,2,1,0:T(8,128)S(1)}, u32[]{:S(2)}, u32[]{:S(2)}) collective-permute-start(f32[8,2,2,8,512]{4,3,2,1,0:T(8,128)S(1)} %get-tuple-element.44), channel_id=1, source_target_pairs={{0,2},{2,0},{4,6},{6,4},{8,10},{10,8},{12,14},{14,12},{16,18},{18,... | collective-permute-start | bytes 1572872 | tf_op jit(solution)/shard_map/ppermute | solution.py:573
  16.6 5.9 %collective-permute-start.6 = (f32[2,2,2,8,512]{4,3,2,1,0:T(8,128)S(1)}, f32[2,2,2,8,512]{4,3,2,1,0:T(8,128)S(1)}, u32[]{:S(2)}, u32[]{:S(2)}) collective-permute-start(f32[2,2,2,8,512]{4,3,2,1,0:T(8,128)S(1)} %get-tuple-element.45), channel_id=1, source_target_pairs={{0,1},{1,0},{2,3},{3,2},{4,5},{5,4},{6,7},{7,6},{8,9},{9,8},{10,11... | collective-permute-start | bytes 393224 | tf_op jit(solution)/shard_map/ppermute | solution.py:676
  25.5 12.8 %copy-start.6 = (f32[2,4,4]{2,1,0:T(4,128)S(1)}, f32[2,4,4]{2,1,0:T(4,128)}, u32[]{:S(2)}) copy-start(f32[2,4,4]{2,1,0:T(4,128)} %onsite_ref.1) | copy-start | bytes 388
  25.5 3.0 %collective-permute-start.7 = (f32[8,2,2,8,512]{4,3,2,1,0:T(8,128)S(1)}, f32[8,2,2,8,512]{4,3,2,1,0:T(8,128)S(1)}, u32[]{:S(2)}, u32[]{:S(2)}) collective-permute-start(f32[8,2,2,8,512]{4,3,2,1,0:T(8,128)S(1)} %get-tuple-element.47), channel_id=1, source_target_pairs={{0,2},{2,0},{4,6},{6,4},{8,10},{10,8},{12,14},{14,12},{16,18},{18,... | collective-permute-start | bytes 1572872 | tf_op jit(solution)/shard_map/ppermute | solution.py:573
  25.6 24.7 %collective-permute-start.1 = (f32[2,2,8,512]{3,2,1,0:T(8,128)S(1)}, f32[2,2,8,512]{3,2,1,0:T(8,128)S(1)}, u32[]{:S(2)}, u32[]{:S(2)}) collective-permute-start(f32[2,2,8,512]{3,2,1,0:T(8,128)S(1)} %slice_bitcast_fusion.9.near_here_ref.green_here_ref.green_near_ref), channel_id=1, source_target_pairs={{0,1},{1,0},{2,3},{3,2},{4,5},{5,4},{6,7},{7,6},{8,9},{9,8},{10,11... | collective-permute-start | bytes 196616 | tf_op jit(solution)/shard_map/ppermute | solution.py:676
  26.0 9.2 %collective-permute-start.3 = (f32[4,2,2,8,512]{4,3,2,1,0:T(8,128)S(1)}, f32[4,2,2,8,512]{4,3,2,1,0:T(8,128)S(1)}, u32[]{:S(2)}, u32[]{:S(2)}) collective-permute-start(f32[4,2,2,8,512]{4,3,2,1,0:T(8,128)S(1)} %get-tuple-element.75), channel_id=1, source_target_pairs={{0,4},{2,6},{4,0},{6,2},{8,12},{10,14},{12,8},{14,10},{16,20},{18,... | collective-permute-start | bytes 786440 | tf_op jit(solution)/shard_map/ppermute | solution.py:577
  28.6 15.3 %collective-permute-start.8 = (f32[4,2,2,8,512]{4,3,2,1,0:T(8,128)S(1)}, f32[4,2,2,8,512]{4,3,2,1,0:T(8,128)S(1)}, u32[]{:S(2)}, u32[]{:S(2)}) collective-permute-start(f32[4,2,2,8,512]{4,3,2,1,0:T(8,128)S(1)} %get-tuple-element.73), channel_id=1, source_target_pairs={{0,4},{2,6},{4,0},{6,2},{8,12},{10,14},{12,8},{14,10},{16,20},{18,... | collective-permute-start | bytes 786440 | tf_op jit(solution)/shard_map/ppermute | solution.py:577
  35.3 7.8 %collective-permute-start.4 = (f32[2,2,2,8,512]{4,3,2,1,0:T(8,128)S(1)}, f32[2,2,2,8,512]{4,3,2,1,0:T(8,128)S(1)}, u32[]{:S(2)}, u32[]{:S(2)}) collective-permute-start(f32[2,2,2,8,512]{4,3,2,1,0:T(8,128)S(1)} %get-tuple-element.93), channel_id=1, source_target_pairs={{0,16},{2,18},{4,20},{6,22},{8,24},{10,26},{12,28},{14,30},{16,0},... | collective-permute-start | bytes 393224 | tf_op jit(solution)/shard_map/ppermute | solution.py:577
  43.2 8.1 %collective-permute-start.5 = (f32[1,2,2,8,512]{4,3,2,1,0:T(8,128)S(1)}, f32[1,2,2,8,512]{4,3,2,1,0:T(8,128)S(1)}, u32[]{:S(2)}, u32[]{:S(2)}) collective-permute-start(f32[1,2,2,8,512]{4,3,2,1,0:T(8,128)S(1)} %get-tuple-element.98), channel_id=1, source_target_pairs={{0,8},{2,10},{4,12},{6,14},{8,0},{10,2},{12,4},{14,6},{16,24},{18,... | collective-permute-start | bytes 196616 | tf_op jit(solution)/shard_map/ppermute | solution.py:577
  44.0 7.3 %collective-permute-start.10 = (f32[2,2,8,512]{3,2,1,0:T(8,128)S(1)}, f32[2,2,8,512]{3,2,1,0:T(8,128)S(1)}, u32[]{:S(2)}, u32[]{:S(2)}) collective-permute-start(f32[2,2,8,512]{3,2,1,0:T(8,128)S(1)} %get-tuple-element.90), channel_id=1, source_target_pairs={{0,9},{1,8},{2,11},{3,10},{4,13},{5,12},{6,15},{7,14},{8,1},{9,0},... | collective-permute-start | bytes 196616 | tf_op jit(solution)/shard_map/ppermute | solution.py:587
  46.3 7.9 %collective-permute-start.11 = (f32[2,2,8,512]{3,2,1,0:T(8,128)S(1)}, f32[2,2,8,512]{3,2,1,0:T(8,128)S(1)}, u32[]{:S(2)}, u32[]{:S(2)}) collective-permute-start(f32[2,2,8,512]{3,2,1,0:T(8,128)S(1)} %get-tuple-element.89), channel_id=1, source_target_pairs={{0,17},{1,16},{2,19},{3,18},{4,21},{5,20},{6,23},{7,22},{8,25},{9,... | collective-permute-start | bytes 196616 | tf_op jit(solution)/shard_map/ppermute | solution.py:587
  48.5 7.1 %collective-permute-start.12 = (f32[2,2,8,512]{3,2,1,0:T(8,128)S(1)}, f32[2,2,8,512]{3,2,1,0:T(8,128)S(1)}, u32[]{:S(2)}, u32[]{:S(2)}) collective-permute-start(f32[2,2,8,512]{3,2,1,0:T(8,128)S(1)} %get-tuple-element.88), channel_id=1, source_target_pairs={{0,25},{1,24},{2,27},{3,26},{4,29},{5,28},{6,31},{7,30},{8,17},{9,... | collective-permute-start | bytes 196616 | tf_op jit(solution)/shard_map/ppermute | solution.py:587
  50.3 5.3 %collective-permute-start.9 = (f32[2,2,8,512]{3,2,1,0:T(8,128)S(1)}, f32[2,2,8,512]{3,2,1,0:T(8,128)S(1)}, u32[]{:S(2)}, u32[]{:S(2)}) collective-permute-start(f32[2,2,8,512]{3,2,1,0:T(8,128)S(1)} %get-tuple-element.91), channel_id=1, source_target_pairs={{0,1},{1,0},{2,3},{3,2},{4,5},{5,4},{6,7},{7,6},{8,9},{9,8},{10,11... | collective-permute-start | bytes 196616 | tf_op jit(solution)/shard_map/ppermute | solution.py:587
  59.2 10.5 %collective-permute-start.14 = (f32[8,2,2,8,512]{4,3,2,1,0:T(8,128)S(1)}, f32[8,2,2,8,512]{4,3,2,1,0:T(8,128)S(1)}, u32[]{:S(2)}, u32[]{:S(2)}) collective-permute-start(f32[8,2,2,8,512]{4,3,2,1,0:T(8,128)S(1)} %get-tuple-element.51), channel_id=1, source_target_pairs={{0,2},{2,0},{4,6},{6,4},{8,10},{10,8},{12,14},{14,12},{16,18},{18,... | collective-permute-start | bytes 1572872 | tf_op jit(solution)/shard_map/ppermute | solution.py:573
  59.3 5.9 %collective-permute-start.18 = (f32[2,2,2,8,512]{4,3,2,1,0:T(8,128)S(1)}, f32[2,2,2,8,512]{4,3,2,1,0:T(8,128)S(1)}, u32[]{:S(2)}, u32[]{:S(2)}) collective-permute-start(f32[2,2,2,8,512]{4,3,2,1,0:T(8,128)S(1)} %get-tuple-element.52), channel_id=1, source_target_pairs={{0,1},{1,0},{2,3},{3,2},{4,5},{5,4},{6,7},{7,6},{8,9},{9,8},{10,11... | collective-permute-start | bytes 393224 | tf_op jit(solution)/shard_map/ppermute | solution.py:676
  68.2 3.2 %collective-permute-start.19 = (f32[8,2,2,8,512]{4,3,2,1,0:T(8,128)S(1)}, f32[8,2,2,8,512]{4,3,2,1,0:T(8,128)S(1)}, u32[]{:S(2)}, u32[]{:S(2)}) collective-permute-start(f32[8,2,2,8,512]{4,3,2,1,0:T(8,128)S(1)} %get-tuple-element.54), channel_id=1, source_target_pairs={{0,2},{2,0},{4,6},{6,4},{8,10},{10,8},{12,14},{14,12},{16,18},{18,... | collective-permute-start | bytes 1572872 | tf_op jit(solution)/shard_map/ppermute | solution.py:573
  68.3 22.4 %collective-permute-start.13 = (f32[2,2,2,8,512]{4,3,2,1,0:T(8,128)S(1)}, f32[2,2,2,8,512]{4,3,2,1,0:T(8,128)S(1)}, u32[]{:S(2)}, u32[]{:S(2)}) collective-permute-start(f32[2,2,2,8,512]{4,3,2,1,0:T(8,128)S(1)} %get-tuple-element.48), channel_id=1, source_target_pairs={{0,1},{1,0},{2,3},{3,2},{4,5},{5,4},{6,7},{7,6},{8,9},{9,8},{10,11... | collective-permute-start | bytes 393224 | tf_op jit(solution)/shard_map/ppermute | solution.py:676
  69.8 9.2 %collective-permute-start.15 = (f32[4,2,2,8,512]{4,3,2,1,0:T(8,128)S(1)}, f32[4,2,2,8,512]{4,3,2,1,0:T(8,128)S(1)}, u32[]{:S(2)}, u32[]{:S(2)}) collective-permute-start(f32[4,2,2,8,512]{4,3,2,1,0:T(8,128)S(1)} %get-tuple-element.71), channel_id=1, source_target_pairs={{0,4},{2,6},{4,0},{6,2},{8,12},{10,14},{12,8},{14,10},{16,20},{18,... | collective-permute-start | bytes 786440 | tf_op jit(solution)/shard_map/ppermute | solution.py:577
  71.4 12.4 %collective-permute-start.20 = (f32[4,2,2,8,512]{4,3,2,1,0:T(8,128)S(1)}, f32[4,2,2,8,512]{4,3,2,1,0:T(8,128)S(1)}, u32[]{:S(2)}, u32[]{:S(2)}) collective-permute-start(f32[4,2,2,8,512]{4,3,2,1,0:T(8,128)S(1)} %get-tuple-element.69), channel_id=1, source_target_pairs={{0,4},{2,6},{4,0},{6,2},{8,12},{10,14},{12,8},{14,10},{16,20},{18,... | collective-permute-start | bytes 786440 | tf_op jit(solution)/shard_map/ppermute | solution.py:577
  79.1 9.4 %collective-permute-start.16 = (f32[2,2,2,8,512]{4,3,2,1,0:T(8,128)S(1)}, f32[2,2,2,8,512]{4,3,2,1,0:T(8,128)S(1)}, u32[]{:S(2)}, u32[]{:S(2)}) collective-permute-start(f32[2,2,2,8,512]{4,3,2,1,0:T(8,128)S(1)} %get-tuple-element.87), channel_id=1, source_target_pairs={{0,16},{2,18},{4,20},{6,22},{8,24},{10,26},{12,28},{14,30},{16,0},... | collective-permute-start | bytes 393224 | tf_op jit(solution)/shard_map/ppermute | solution.py:577
  83.9 7.0 %collective-permute-start.21 = (f32[2,2,8,512]{3,2,1,0:T(8,128)S(1)}, f32[2,2,8,512]{3,2,1,0:T(8,128)S(1)}, u32[]{:S(2)}, u32[]{:S(2)}) collective-permute-start(f32[2,2,8,512]{3,2,1,0:T(8,128)S(1)} %get-tuple-element.85), channel_id=1, source_target_pairs={{0,1},{1,0},{2,3},{3,2},{4,5},{5,4},{6,7},{7,6},{8,9},{9,8},{10,11... | collective-permute-start | bytes 196616 | tf_op jit(solution)/shard_map/ppermute | solution.py:587
  84.6 6.2 %collective-permute-start.22 = (f32[2,2,8,512]{3,2,1,0:T(8,128)S(1)}, f32[2,2,8,512]{3,2,1,0:T(8,128)S(1)}, u32[]{:S(2)}, u32[]{:S(2)}) collective-permute-start(f32[2,2,8,512]{3,2,1,0:T(8,128)S(1)} %get-tuple-element.84), channel_id=1, source_target_pairs={{0,9},{1,8},{2,11},{3,10},{4,13},{5,12},{6,15},{7,14},{8,1},{9,0},... | collective-permute-start | bytes 196616 | tf_op jit(solution)/shard_map/ppermute | solution.py:587
  86.2 7.7 %collective-permute-start.23 = (f32[2,2,8,512]{3,2,1,0:T(8,128)S(1)}, f32[2,2,8,512]{3,2,1,0:T(8,128)S(1)}, u32[]{:S(2)}, u32[]{:S(2)}) collective-permute-start(f32[2,2,8,512]{3,2,1,0:T(8,128)S(1)} %get-tuple-element.83), channel_id=1, source_target_pairs={{0,17},{1,16},{2,19},{3,18},{4,21},{5,20},{6,23},{7,22},{8,25},{9,... | collective-permute-start | bytes 196616 | tf_op jit(solution)/shard_map/ppermute | solution.py:587
  88.4 7.1 %collective-permute-start.24 = (f32[2,2,8,512]{3,2,1,0:T(8,128)S(1)}, f32[2,2,8,512]{3,2,1,0:T(8,128)S(1)}, u32[]{:S(2)}, u32[]{:S(2)}) collective-permute-start(f32[2,2,8,512]{3,2,1,0:T(8,128)S(1)} %get-tuple-element.82), channel_id=1, source_target_pairs={{0,25},{1,24},{2,27},{3,26},{4,29},{5,28},{6,31},{7,30},{8,17},{9,... | collective-permute-start | bytes 196616 | tf_op jit(solution)/shard_map/ppermute | solution.py:587
  90.7 4.8 %collective-permute-start.17 = (f32[1,2,2,8,512]{4,3,2,1,0:T(8,128)S(1)}, f32[1,2,2,8,512]{4,3,2,1,0:T(8,128)S(1)}, u32[]{:S(2)}, u32[]{:S(2)}) collective-permute-start(f32[1,2,2,8,512]{4,3,2,1,0:T(8,128)S(1)} %get-tuple-element.96), channel_id=1, source_target_pairs={{0,8},{2,10},{4,12},{6,14},{8,0},{10,2},{12,4},{14,6},{16,24},{18,... | collective-permute-start | bytes 196616 | tf_op jit(solution)/shard_map/ppermute | solution.py:577
  99.2 9.1 %collective-permute-start.26 = (f32[8,2,2,8,512]{4,3,2,1,0:T(8,128)S(1)}, f32[8,2,2,8,512]{4,3,2,1,0:T(8,128)S(1)}, u32[]{:S(2)}, u32[]{:S(2)}) collective-permute-start(f32[8,2,2,8,512]{4,3,2,1,0:T(8,128)S(1)} %get-tuple-element.60), channel_id=1, source_target_pairs={{0,2},{2,0},{4,6},{6,4},{8,10},{10,8},{12,14},{14,12},{16,18},{18,... | collective-permute-start | bytes 1572872 | tf_op jit(solution)/shard_map/ppermute | solution.py:573
  99.2 5.9 %collective-permute-start.30 = (f32[2,2,2,8,512]{4,3,2,1,0:T(8,128)S(1)}, f32[2,2,2,8,512]{4,3,2,1,0:T(8,128)S(1)}, u32[]{:S(2)}, u32[]{:S(2)}) collective-permute-start(f32[2,2,2,8,512]{4,3,2,1,0:T(8,128)S(1)} %get-tuple-element.61), channel_id=1, source_target_pairs={{0,1},{1,0},{2,3},{3,2},{4,5},{5,4},{6,7},{7,6},{8,9},{9,8},{10,11... | collective-permute-start | bytes 393224 | tf_op jit(solution)/shard_map/ppermute | solution.py:676
  108.1 2.0 %collective-permute-start.31 = (f32[8,2,2,8,512]{4,3,2,1,0:T(8,128)S(1)}, f32[8,2,2,8,512]{4,3,2,1,0:T(8,128)S(1)}, u32[]{:S(2)}, u32[]{:S(2)}) collective-permute-start(f32[8,2,2,8,512]{4,3,2,1,0:T(8,128)S(1)} %get-tuple-element.63), channel_id=1, source_target_pairs={{0,2},{2,0},{4,6},{6,4},{8,10},{10,8},{12,14},{14,12},{16,18},{18,... | collective-permute-start | bytes 1572872 | tf_op jit(solution)/shard_map/ppermute | solution.py:573
  108.3 9.2 %collective-permute-start.27 = (f32[4,2,2,8,512]{4,3,2,1,0:T(8,128)S(1)}, f32[4,2,2,8,512]{4,3,2,1,0:T(8,128)S(1)}, u32[]{:S(2)}, u32[]{:S(2)}) collective-permute-start(f32[4,2,2,8,512]{4,3,2,1,0:T(8,128)S(1)} %get-tuple-element.67), channel_id=1, source_target_pairs={{0,4},{2,6},{4,0},{6,2},{8,12},{10,14},{12,8},{14,10},{16,20},{18,... | collective-permute-start | bytes 786440 | tf_op jit(solution)/shard_map/ppermute | solution.py:577
  110.2 12.5 %collective-permute-start.32 = (f32[4,2,2,8,512]{4,3,2,1,0:T(8,128)S(1)}, f32[4,2,2,8,512]{4,3,2,1,0:T(8,128)S(1)}, u32[]{:S(2)}, u32[]{:S(2)}) collective-permute-start(f32[4,2,2,8,512]{4,3,2,1,0:T(8,128)S(1)} %get-tuple-element.65), channel_id=1, source_target_pairs={{0,4},{2,6},{4,0},{6,2},{8,12},{10,14},{12,8},{14,10},{16,20},{18,... | collective-permute-start | bytes 786440 | tf_op jit(solution)/shard_map/ppermute | solution.py:577
  111.8 15.5 %collective-permute-start.25 = (f32[2,2,2,8,512]{4,3,2,1,0:T(8,128)S(1)}, f32[2,2,2,8,512]{4,3,2,1,0:T(8,128)S(1)}, u32[]{:S(2)}, u32[]{:S(2)}) collective-permute-start(f32[2,2,2,8,512]{4,3,2,1,0:T(8,128)S(1)} %slice.305), channel_id=1, source_target_pairs={{0,1},{1,0},{2,3},{3,2},{4,5},{5,4},{6,7},{7,6},{8,9},{9,8},{10,11... | collective-permute-start | bytes 393224 | tf_op jit(solution)/shard_map/ppermute | solution.py:676
  117.6 9.6 %collective-permute-start.28 = (f32[2,2,2,8,512]{4,3,2,1,0:T(8,128)S(1)}, f32[2,2,2,8,512]{4,3,2,1,0:T(8,128)S(1)}, u32[]{:S(2)}, u32[]{:S(2)}) collective-permute-start(f32[2,2,2,8,512]{4,3,2,1,0:T(8,128)S(1)} %get-tuple-element.81), channel_id=1, source_target_pairs={{0,16},{2,18},{4,20},{6,22},{8,24},{10,26},{12,28},{14,30},{16,0},... | collective-permute-start | bytes 393224 | tf_op jit(solution)/shard_map/ppermute | solution.py:577
  122.7 4.9 %collective-permute-start.33 = (f32[2,2,8,512]{3,2,1,0:T(8,128)S(1)}, f32[2,2,8,512]{3,2,1,0:T(8,128)S(1)}, u32[]{:S(2)}, u32[]{:S(2)}) collective-permute-start(f32[2,2,8,512]{3,2,1,0:T(8,128)S(1)} %get-tuple-element.78), channel_id=1, source_target_pairs={{0,8},{2,10},{4,12},{6,14},{8,0},{10,2},{12,4},{14,6},{16,24},{18,... | collective-permute-start | bytes 196616 | tf_op jit(solution)/shard_map/ppermute | solution.py:591
  122.9 7.3 %collective-permute-start.34 = (f32[2,2,8,512]{3,2,1,0:T(8,128)S(1)}, f32[2,2,8,512]{3,2,1,0:T(8,128)S(1)}, u32[]{:S(2)}, u32[]{:S(2)}) collective-permute-start(f32[2,2,8,512]{3,2,1,0:T(8,128)S(1)} %get-tuple-element.77), channel_id=1, source_target_pairs={{0,16},{2,18},{4,20},{6,22},{8,24},{10,26},{12,28},{14,30},{16,0},... | collective-permute-start | bytes 196616 | tf_op jit(solution)/shard_map/ppermute | solution.py:591
  125.3 6.3 %collective-permute-start.35 = (f32[2,2,8,512]{3,2,1,0:T(8,128)S(1)}, f32[2,2,8,512]{3,2,1,0:T(8,128)S(1)}, u32[]{:S(2)}, u32[]{:S(2)}) collective-permute-start(f32[2,2,8,512]{3,2,1,0:T(8,128)S(1)} %get-tuple-element.76), channel_id=1, source_target_pairs={{0,24},{2,26},{4,28},{6,30},{8,16},{10,18},{12,20},{14,22},{16,8},... | collective-permute-start | bytes 196616 | tf_op jit(solution)/shard_map/ppermute | solution.py:591
  127.2 4.9 %collective-permute-start.29 = (f32[1,2,2,8,512]{4,3,2,1,0:T(8,128)S(1)}, f32[1,2,2,8,512]{4,3,2,1,0:T(8,128)S(1)}, u32[]{:S(2)}, u32[]{:S(2)}) collective-permute-start(f32[1,2,2,8,512]{4,3,2,1,0:T(8,128)S(1)} %get-tuple-element.94), channel_id=1, source_target_pairs={{0,8},{2,10},{4,12},{6,14},{8,0},{10,2},{12,4},{14,6},{16,24},{18,... | collective-permute-start | bytes 196616 | tf_op jit(solution)/shard_map/ppermute | solution.py:577
